TPU v7x, 16 devices: a whole 2x2x2 slice. The times are simulated.
16 devices in a mesh: rep: 4 (over z, y), data: 4 (over x, core).
Axes of the slice: x: 2, y: 2, z: 2, core: 2. Of those that a mesh axis runs over, the one named last changes fastest.
Arguments:
- x_now: bfloat16 [32, 256, 1024], P(('rep', 'data'))
- x_next: bfloat16 [32, 256, 1024], P(('rep', 'data'))
- labels: int32 [32], P(('rep', 'data'))
- w_up: float32 [6, 1024, 4096], replicated
- w_down: float32 [6, 4096, 1024], replicated
- w_head: float32 [1024, 1000], replicated
- mom_up: float32 [6, 1024, 4096], replicated
- mom_down: float32 [6, 4096, 1024], replicated
- mom_head: float32 [1024, 1000], replicated
- learn_rate: float32 [], replicated
- momentum: float32 [], replicated
Outputs:
- output 1: float32 [32, 1000], P(('rep', 'data'))
- output 2: float32 [6, 1024, 4096], replicated
- output 3: float32 [6, 4096, 1024], replicated
- output 4: float32 [1024, 1000], replicated
- output 5: float32 [6, 1024, 4096], replicated
- output 6: float32 [6, 4096, 1024], replicated
- output 7: float32 [1024, 1000], replicated
All inputs are finite; a program needn't handle non-finite values.
Results may differ from a plain program's by a relative error of at most 0.0111779.
Values are sent between devices in bfloat16 or wider.
A program may use at most 3.25 GiB of HBM per device.

v0:
```python
import jax
import jax.numpy as jnp
from jax import lax
from jax.sharding import PartitionSpec as P

LN_EPS = 1e-6
BATCH_AXES = ('rep', 'data')


def layer_norm(residual):
    centered = residual - jnp.mean(residual, axis=-1, keepdims=True)
    inv_std = lax.rsqrt(jnp.mean(centered * centered, axis=-1, keepdims=True) + LN_EPS)
    return centered * inv_std, inv_std


def norm_back(normed, inv_std, grad_out):
    return inv_std * (grad_out - jnp.mean(grad_out, axis=-1, keepdims=True)
                      - normed * jnp.mean(grad_out * normed, axis=-1, keepdims=True))


def gelu_parts(pre_act):
    gauss_cdf = 0.5 * (1.0 + lax.erf(pre_act * 0.7071067811865476))
    density = jnp.exp(-0.5 * pre_act * pre_act) * 0.3989422804014327
    return pre_act * gauss_cdf, gauss_cdf + pre_act * density


def block_forward(residual, up_bf, down_bf):
    normed, inv_std = layer_norm(residual)
    act_in = normed.astype(jnp.bfloat16)
    pre_act = jnp.dot(act_in, up_bf, preferred_element_type=jnp.float32)
    hidden, gelu_slope = gelu_parts(pre_act)
    hid_bf = hidden.astype(jnp.bfloat16)
    result = residual + jnp.dot(hid_bf, down_bf, preferred_element_type=jnp.float32)
    return result, (normed, inv_std, act_in, gelu_slope, hid_bf)


def pool_logits(residual, images, head_bf):
    pooled = jnp.mean(residual.reshape(images, -1, residual.shape[-1]), axis=1).astype(jnp.bfloat16)
    return pooled, jnp.dot(pooled, head_bf, preferred_element_type=jnp.float32)


def solution(mesh):
    num_dev = mesh.shape['rep'] * mesh.shape['data']

    def local_step(x_now, x_next, labels, w_up, w_down, w_head, mom_up, mom_down, mom_head, learn_rate, momentum):
        images, seq_len, model_dim = x_now.shape
        layers = w_up.shape[0]
        classes = w_head.shape[1]
        global_batch = images * num_dev
        up_list = [w_up[layer_idx].astype(jnp.bfloat16) for layer_idx in range(layers)]
        down_list = [w_down[layer_idx].astype(jnp.bfloat16) for layer_idx in range(layers)]
        head_bf = w_head.astype(jnp.bfloat16)
        residual = x_now.reshape(images * seq_len, model_dim).astype(jnp.float32)
        saved_acts = []
        for layer_idx in range(layers):
            residual, layer_acts = block_forward(residual, up_list[layer_idx], down_list[layer_idx])
            saved_acts.append(layer_acts)
        pooled, logits = pool_logits(residual, images, head_bf)
        soft_probs = jax.nn.softmax(logits, axis=-1)
        onehot = (labels[:, None] == jnp.arange(classes, dtype=jnp.int32)[None, :]).astype(jnp.float32)
        d_logits = ((soft_probs - onehot) / global_batch).astype(jnp.bfloat16)
        grad_head = jnp.einsum('bd,bc->dc', pooled, d_logits, preferred_element_type=jnp.float32)
        red_head = lax.psum(grad_head.astype(jnp.bfloat16), BATCH_AXES)
        d_pooled = jnp.einsum('bc,dc->bd', d_logits, head_bf, preferred_element_type=jnp.float32)
        d_resid = jnp.broadcast_to((d_pooled / seq_len)[:, None, :], (images, seq_len, model_dim)).reshape(images * seq_len, model_dim)
        red_up = [None] * layers
        red_down = [None] * layers
        for layer_idx in reversed(range(layers)):
            normed, inv_std, act_in, gelu_slope, hid_bf = saved_acts[layer_idx]
            d_out = d_resid.astype(jnp.bfloat16)
            grad_down = jnp.einsum('tf,td->fd', hid_bf, d_out, preferred_element_type=jnp.float32)
            red_down[layer_idx] = lax.psum(grad_down.astype(jnp.bfloat16), BATCH_AXES)
            d_hidden = jnp.einsum('td,fd->tf', d_out, down_list[layer_idx], preferred_element_type=jnp.float32)
            d_pre = (d_hidden * gelu_slope).astype(jnp.bfloat16)
            grad_up = jnp.einsum('td,tf->df', act_in, d_pre, preferred_element_type=jnp.float32)
            red_up[layer_idx] = lax.psum(grad_up.astype(jnp.bfloat16), BATCH_AXES)
            if layer_idx > 0:
                d_normed = jnp.einsum('tf,df->td', d_pre, up_list[layer_idx], preferred_element_type=jnp.float32)
                d_resid = d_resid + norm_back(normed, inv_std, d_normed)
        new_mom_up = momentum * mom_up + jnp.stack(red_up).astype(jnp.float32)
        new_mom_down = momentum * mom_down + jnp.stack(red_down).astype(jnp.float32)
        new_mom_head = momentum * mom_head + red_head.astype(jnp.float32)
        new_up = w_up - learn_rate * new_mom_up
        new_down = w_down - learn_rate * new_mom_down
        new_head = w_head - learn_rate * new_mom_head
        residual = x_next.reshape(images * seq_len, model_dim).astype(jnp.float32)
        for layer_idx in range(layers):
            residual, _ = block_forward(residual, new_up[layer_idx].astype(jnp.bfloat16),
                                        new_down[layer_idx].astype(jnp.bfloat16))
        _, logits_next = pool_logits(residual, images, new_head.astype(jnp.bfloat16))
        return logits_next, new_up, new_down, new_head, new_mom_up, new_mom_down, new_mom_head

    batch_spec = P(BATCH_AXES)
    whole_spec = P()
    return jax.shard_map(local_step, mesh=mesh,
                         in_specs=(batch_spec, batch_spec, batch_spec) + (whole_spec,) * 8,
                         out_specs=(batch_spec,) + (whole_spec,) * 6,
                         check_vma=False)
```

profile of v0, /device:TPU:0, one launch (start us, length us, event | category | flops | bytes accessed | tf_op | source)
XLA Modules:
  0.0 2522.9 jit_solution(3778887762509599369)
XLA Ops:
  7.2 48.1 %convert.33 = bf16[6,1024,4096]{2,1,0:T(8,128)(2,1)} convert(f32[6,1024,4096]{2,1,0:T(8,128)} %param.14) | non-fusion elementwise | flops 25165824 | bytes 150994944 | tf_op jit(solution)/shard_map/convert.24
  57.4 48.0 %convert.34 = bf16[6,4096,1024]{2,1,0:T(8,128)(2,1)} convert(f32[6,4096,1024]{2,1,0:T(8,128)} %param.15) | non-fusion elementwise | flops 25165824 | bytes 150994944 | tf_op jit(solution)/shard_map/convert.23
  105.4 9.4 multiply_convert_fusion.11
  114.9 8.5 fusion.196
  123.8 10.0 multiply_convert_fusion.10
  133.8 8.5 fusion.197
  142.8 9.9 multiply_convert_fusion.9
  152.6 8.5 fusion.198
  161.5 9.6 multiply_convert_fusion.8
  171.2 8.5 fusion.199
  180.1 9.5 multiply_convert_fusion.7
  189.6 8.5 fusion.200
  198.5 9.6 multiply_convert_fusion.6
  208.2 10.1 bitcast_reduce_fusion.1
  220.0 11.5 fusion.5
  246.5 10.4 fusion.11
  272.3 10.2 fusion.17
  297.9 10.3 fusion.23
  323.4 10.3 fusion.29
  348.2 9.4 convert_bitcast_fusion.1
  395.7 15.3 convert_bitcast_fusion.11
  414.3 1581.8 %all-reduce.3.cloned.1.call-done = (bf16[1024,1000]{0,1:T(8,128)(2,1)}, bf16[1,4096,1024]{2,1,0:T(8,128)(2,1)}, bf16[1,4096,1024]{2,1,0:T(8,128)(2,1)}, bf16[1,4...) async-done(((bf16[1024,1000]{0,1:T(8,128)(2,1)}, ...) | async-done | bytes 102711312 | tf_op jit(solution)/shard_map/psum | solution.py:63
  1996.2 7.9 constant_dynamic-update-slice_fusion.5
  2027.4 7.9 constant_dynamic-update-slice_fusion.2
  2088.9 156.6 %fusion.194 = (bf16[6,1024,4096]{2,1,0:T(8,128)(2,1)}, f32[6,1024,4096]{2,1,0:T(8,128)}, f32[6,1024,4096]{2,1,0:T(8,128)}) fusion(f32[6,1024,4096]{2,1,0:T(8,128)} %param.14, f32[]{:T(128)S(6)} %copy.43, bf16[6,1024,4096]{2,1,0:T(8,128)(2,1)} %constant_dynamic-update-slice_fusion, f32[6,1024,4096]{2,1,0:T(8,128)} %param.17, f32[]{:T(128)S(6)} %copy.44), kind=kLoop, calls=%fused_computation.328 | loop fusion | flops 150994944 | bytes 503316480 | tf_op jit(solution)/shard_map/convert.13
  2245.5 159.2 %fusion.195 = (bf16[6,4096,1024]{2,1,0:T(8,128)(2,1)}, f32[6,4096,1024]{2,1,0:T(8,128)}, f32[6,4096,1024]{2,1,0:T(8,128)}) fusion(f32[6,4096,1024]{2,1,0:T(8,128)} %param.15, f32[]{:T(128)S(6)} %copy.43, bf16[6,4096,1024]{2,1,0:T(8,128)(2,1)} %constant_dynamic-update-slice_fusion.6, f32[6,4096,1024]{2,1,0:T(8,128)} %param.18, f32[]{:T(128)S(6)} %copy.44), kind=kLoop, calls=%fused_computation.329 | loop fusion | flops 150994944 | bytes 503316480 | tf_op jit(solution)/shard_map/convert.12
  2404.7 15.0 fusion.203
  2421.1 16.2 fusion.204
  2437.7 16.1 fusion.205
  2455.7 16.3 fusion.206
  2472.3 16.1 fusion.207
  2490.3 16.3 bitcast_reduce_fusion
  (178 shorter events, 212.6 us)
Async XLA Ops:
  7.2 48.1 %copy-start.1 = (bf16[2,256,1024]{2,1,0:T(8,128)(2,1)S(1)}, bf16[2,256,1024]{2,1,0:T(8,128)(2,1)}, u32[]{:S(2)}) copy-start(bf16[2,256,1024]{2,1,0:T(8,128)(2,1)} %param.11) | copy-start | bytes 3145732
  7.2 1989.0 %all-reduce.3.cloned.1.call-start = ((), (), s32[]{:S(2)}) async-start(), calls=%async_computation | async-start | bytes 205422592 | tf_op jit(solution)/shard_map/psum | solution.py:63
  114.9 8.5 copy-start.34
  123.4 10.4 copy-start.8
  123.5 10.3 copy-start.16
  123.8 10.0 copy-start.20
  133.8 8.6 copy-start.36
  142.4 10.3 copy-start.6
  142.4 10.2 copy-start.18
  142.8 9.9 copy-start.22
  152.6 8.5 copy-start.38
  171.2 8.5 copy-start.40
  189.6 8.5 copy-start.42
  208.2 10.2 copy-start.32
  208.2 10.2 copy-start
  208.2 11.2 copy-start.30
  297.8 10.3 copy-start.7
  297.8 10.3 copy-start.19
  297.9 10.3 copy-start.23
  323.3 10.3 copy-start.9
  323.4 10.3 copy-start.17
  323.4 10.3 copy-start.21
  348.2 9.5 copy-start.41
  371.5 7.0 copy-start.27
  371.5 7.0 copy-start.29
  371.5 7.0 copy-start.31
  371.5 9.1 copy-start.25
  371.6 9.1 copy-start.24
  371.6 9.1 copy-start.33
  380.7 7.8 copy-start.35
  2245.5 159.2 %copy-start.5 = (bf16[2,256,1024]{2,1,0:T(8,128)(2,1)S(1)}, bf16[2,256,1024]{2,1,0:T(8,128)(2,1)}, u32[]{:S(2)}) copy-start(bf16[2,256,1024]{2,1,0:T(8,128)(2,1)} %param.12) | copy-start | bytes 3145732
  2490.3 16.4 copy-start.11
  (12 other events, 43.0 us)
Sparse Core Ops, SparseCore 0:
  411.1 1584.9 all-reduce.2
where the time goes:
time: 2530 us; the launch traced here: 2520 us
  waiting for transfers between devices  1580 us (62%)
  other arithmetic  433 us (17%)
  matrix products  397 us (16%)
  local copies, waits for them, and re-layouts  94.4 us (4%)
    psum x1, waiting for transfers between devices, local_step(): red_head = lax.psum(grad_head.astype(jnp.bfloat16), BATCH_AXES)  1580 us
    another operation x4, other arithmetic  412 us
    dot_general x12, matrix products, block_forward(): jnp.dot(hid_bf, down_bf, preferred_element_type=jnp.float32)  149 us
    unnamed x98, local copies, waits for them, and re-layouts  78.7 us
    dot_general x6, matrix products, block_forward(): pre_act = jnp.dot(act_in, up_bf, preferred_element_type=jnp.float32)  58.1 us
    dot_general x5, matrix products, local_step(): jnp.einsum('td,fd->tf', d_out, down_list[layer_idx], preferred_element_ty...  52.6 us
    dot_general x6, matrix products, local_step(): jnp.einsum('td,tf->df', act_in, d_pre, preferred_element_type=jnp.float32)  51.3 us
  transfers between devices with their start and end apart: 1, of which 1 were waited for; matrix products, arithmetic and copies ran while one was open for 0% of the time, Pallas kernels for 0%

commit v1 on v0

v1 whole, which is shorter than its diff:
```python
import functools

import jax
import jax.numpy as jnp
from jax import lax
from jax.experimental import pallas as pl
from jax.experimental.pallas import tpu as pltpu
from jax.sharding import PartitionSpec as P


LN_EPS = 1e-6
BATCH_AXES = ('rep', 'data')
BLOCKS = 16
BW = 256
LINKS = (2, 4, 8)
ADMIT = ((5, 1), (5, 0), (4, 1), (4, 0)) + tuple((l, k) for l in range(4) for k in (0, 1))
GATHER_SC = frozenset(m for i, m in enumerate(ADMIT) if i % 2 == 0)

ORDER = tuple((t[0], int(t[1]), int(t[2])) for t in (
    'g51', 'S50', 'a51', 'g50', 'N50', 'g41', 'a50', 'S40', 'a41', 'g40',
    'N40', 'b51', 'a40', 'S30', 'b50', 'N30', 'S20', 'c51', 'b41', 'N20',
    'c50', 'b40', 'g11', 'S10', 'd51', 'c41', 'g10', 'N10', 'd50', 'c40',
    'g01', 'S00', 'a01', 'a10', 'd40', 'a11', 'd41', 'e50', 'g00', 'g20',
    'g21', 'g30', 'U51', 'e40', 'b01', 'b10', 'b11', 'U41', 'H00', 'g31',
    'a00', 'c01', 'a20', 'f50', 'f40', 'c11', 'c10', 'a21', 'h40', 'b20',
    'b00', 'd11', 'U40', 'd01', 'd10', 'c00', 'b21', 'h50', 'U50', 'e01',
    'e11', 'c20', 'a30', 'a31', 'f11', 'c21', 'd00', 'd20', 'f01', 'b31',
    'd21', 'b30', 'K00', 'h11', 'c31', 'h01', 'K01', 'd31', 'e21', 'c30',
    'K10', 'd30', 'e31', 'K11', 'f21', 'K20', 'f31', 'h21', 'h31', 'K21',
    'K30', 'K31', 'F40', 'F41', 'F50', 'F51',
))


def layer_norm(residual):
    centered = residual - jnp.mean(residual, axis=-1, keepdims=True)
    inv_std = lax.rsqrt(jnp.mean(centered * centered, axis=-1, keepdims=True) + LN_EPS)
    return centered * inv_std, inv_std


def norm_back(normed, inv_std, grad_out):
    return inv_std * (grad_out - jnp.mean(grad_out, axis=-1, keepdims=True)
                      - normed * jnp.mean(grad_out * normed, axis=-1, keepdims=True))


def gelu(pre_act):
    return pre_act * (0.5 * (1.0 + lax.erf(pre_act * 0.7071067811865476)))


def gelu_parts(pre_act):
    gauss_cdf = 0.5 * (1.0 + lax.erf(pre_act * 0.7071067811865476))
    density = jnp.exp(-0.5 * pre_act * pre_act) * 0.3989422804014327
    return pre_act * gauss_cdf, gauss_cdf + pre_act * density


def pool_logits(residual, images, head_bf):
    pooled = jnp.mean(residual.reshape(images, -1, residual.shape[-1]), axis=1).astype(jnp.bfloat16)
    return pooled, jnp.dot(pooled, head_bf, preferred_element_type=jnp.float32)


def order_of(m):
    i = ADMIT.index(m) % 3
    return tuple(LINKS[(i + s) % 3] for s in range(3))


def flip(a, b):
    out = 0
    for s in range(4):
        x = lax.rem(lax.div(a, 1 << s), 2)
        y = lax.rem(lax.div(b, 1 << s), 2)
        out = out + (x + y - 2 * x * y) * (1 << s)
    return out


def block_at(pos, order, me):
    vals = (1,) + order
    mask = 0
    for s in range(4):
        mask = mask + lax.rem(lax.div(pos, 1 << (3 - s)), 2) * vals[s]
    return flip(mask, me)


def dot_tn(a, b):
    return lax.dot_general(a, b, (((0,), (0,)), ((), ())), preferred_element_type=jnp.float32)


def grad_down_send(me_ref, z_ref, v_ref, o_ref):
    o_ref[...] = dot_tn(z_ref[...], v_ref[...]).astype(jnp.bfloat16)


def grad_up_send(me_ref, a_ref, s_ref, o_ref, at_ref):
    @pl.when(pl.program_id(0) == 0)
    def _():
        at_ref[...] = a_ref[...].astype(jnp.float32).T.astype(jnp.bfloat16)

    o_ref[...] = jnp.dot(at_ref[...], s_ref[...], preferred_element_type=jnp.float32).astype(jnp.bfloat16)


def grad_down_keep(me_ref, z_ref, v_ref, r_ref, os_ref, ok_ref):
    g = dot_tn(z_ref[...], v_ref[...]).astype(jnp.bfloat16)
    out = (g.astype(jnp.float32) + r_ref[...].astype(jnp.float32)).astype(jnp.bfloat16)

    @pl.when(pl.program_id(0) < 4)
    def _():
        os_ref[...] = out

    @pl.when(pl.program_id(0) >= 4)
    def _():
        ok_ref[...] = out


def grad_up_keep(me_ref, a_ref, s_ref, r_ref, os_ref, ok_ref, at_ref):
    @pl.when(pl.program_id(0) == 0)
    def _():
        at_ref[...] = a_ref[...].astype(jnp.float32).T.astype(jnp.bfloat16)

    g = jnp.dot(at_ref[...], s_ref[...], preferred_element_type=jnp.float32).astype(jnp.bfloat16)
    out = (g.astype(jnp.float32) + r_ref[...].astype(jnp.float32)).astype(jnp.bfloat16)

    @pl.when(pl.program_id(0) < 4)
    def _():
        os_ref[...] = out

    @pl.when(pl.program_id(0) >= 4)
    def _():
        ok_ref[...] = out


def grad_send(m, me, left, right):
    order = order_of(m)
    rows, dim = left.shape[0], 1024
    if m[1] == 1:
        return pl.pallas_call(
            grad_down_send,
            grid_spec=pltpu.PrefetchScalarGridSpec(
                num_scalar_prefetch=1, grid=(8,),
                in_specs=[pl.BlockSpec((rows, BW), lambda i, me: (0, block_at(i + 8, order, me[0]))),
                          pl.BlockSpec((rows, dim), lambda i, me: (0, 0))],
                out_specs=pl.BlockSpec((BW, dim), lambda i, me: (i, 0))),
            out_shape=jax.ShapeDtypeStruct((8 * BW, dim), jnp.bfloat16),
            cost_estimate=pl.CostEstimate(flops=2 * rows * dim * 8 * BW, bytes_accessed=7 << 20, transcendentals=0),
            name='gds')(me, left, right)
    return pl.pallas_call(
        grad_up_send,
        grid_spec=pltpu.PrefetchScalarGridSpec(
            num_scalar_prefetch=1, grid=(8,),
            in_specs=[pl.BlockSpec((rows, dim), lambda i, me: (0, 0)),
                      pl.BlockSpec((rows, BW), lambda i, me: (0, block_at(i + 8, order, me[0])))],
            out_specs=pl.BlockSpec((dim, BW), lambda i, me: (0, i)),
            scratch_shapes=[pltpu.VMEM((dim, rows), jnp.bfloat16)]),
        out_shape=jax.ShapeDtypeStruct((dim, 8 * BW), jnp.bfloat16),
        cost_estimate=pl.CostEstimate(flops=2 * rows * dim * 8 * BW, bytes_accessed=7 << 20, transcendentals=0),
        name='gus')(me, left, right)


def grad_keep(m, me, left, right, got):
    order = order_of(m)
    rows, dim = left.shape[0], 1024
    spot = lambda i: lax.rem(i + 4, 8)
    low = lambda i: jnp.minimum(i, 3)
    high = lambda i: jnp.maximum(i - 4, 0)
    if m[1] == 1:
        return pl.pallas_call(
            grad_down_keep,
            grid_spec=pltpu.PrefetchScalarGridSpec(
                num_scalar_prefetch=1, grid=(8,),
                in_specs=[pl.BlockSpec((rows, BW), lambda i, me: (0, block_at(spot(i), order, me[0]))),
                          pl.BlockSpec((rows, dim), lambda i, me: (0, 0)),
                          pl.BlockSpec((BW, dim), lambda i, me: (spot(i), 0))],
                out_specs=[pl.BlockSpec((BW, dim), lambda i, me: (low(i), 0)),
                           pl.BlockSpec((BW, dim), lambda i, me: (high(i), 0))]),
            out_shape=[jax.ShapeDtypeStruct((4 * BW, dim), jnp.bfloat16)] * 2,
            cost_estimate=pl.CostEstimate(flops=2 * rows * dim * 8 * BW, bytes_accessed=11 << 20, transcendentals=0),
            name='gdk')(me, left, right, got)
    return pl.pallas_call(
        grad_up_keep,
        grid_spec=pltpu.PrefetchScalarGridSpec(
            num_scalar_prefetch=1, grid=(8,),
            in_specs=[pl.BlockSpec((rows, dim), lambda i, me: (0, 0)),
                      pl.BlockSpec((rows, BW), lambda i, me: (0, block_at(spot(i), order, me[0]))),
                      pl.BlockSpec((dim, BW), lambda i, me: (0, spot(i)))],
            out_specs=[pl.BlockSpec((dim, BW), lambda i, me: (0, low(i))),
                       pl.BlockSpec((dim, BW), lambda i, me: (0, high(i)))],
            scratch_shapes=[pltpu.VMEM((dim, rows), jnp.bfloat16)]),
        out_shape=[jax.ShapeDtypeStruct((dim, 4 * BW), jnp.bfloat16)] * 2,
        cost_estimate=pl.CostEstimate(flops=2 * rows * dim * 8 * BW, bytes_accessed=11 << 20, transcendentals=0),
        name='guk')(me, left, right, got)


def update_body(kind, pieces, *refs):
    _, rates_ref = refs[:2]
    refs = refs[2:]
    acts = ()
    if kind == 'up':
        acts, refs = refs[:1], refs[1:]
    elif kind == 'down':
        acts, refs = refs[:2], refs[2:]
    grads, refs = refs[:pieces], refs[pieces:]
    w_ref, m_ref = refs[:2]
    nw_ref, nm_ref = refs[-2 - {'up': 2, 'down': 1, 'plain': 1}[kind]:][:2]
    outs = refs[-{'up': 2, 'down': 1, 'plain': 1}[kind]:]
    step = pl.program_id(0)

    if kind == 'up':
        @pl.when(step == 0)
        def _():
            outs[1][...] = layer_norm(acts[0][...])[0].astype(jnp.bfloat16)
    if kind == 'down':
        @pl.when(step == 0)
        def _():
            outs[0][...] = acts[0][...]

    def apply(grad_ref):
        grad = grad_ref[...]
        shape = w_ref.shape[1:]
        new_m = rates_ref[1] * m_ref[...].reshape(shape) + grad.reshape(shape).astype(jnp.float32)
        new_w = w_ref[...].reshape(shape) - rates_ref[0] * new_m
        nm_ref[...] = new_m.reshape(nm_ref.shape)
        nw_ref[...] = new_w.reshape(nw_ref.shape)
        new_bf = new_w.astype(jnp.bfloat16)
        if kind == 'up':
            outs[0][...] = gelu(jnp.dot(outs[1][...], new_bf, preferred_element_type=jnp.float32)).astype(jnp.bfloat16)
        elif kind == 'down':
            outs[0][...] += jnp.dot(acts[1][...], new_bf, preferred_element_type=jnp.float32)
        else:
            outs[0][...] = new_bf

    if pieces == 1:
        apply(grads[0])
    else:
        for p in range(pieces):
            pl.when(lax.div(step, 4) == p)(functools.partial(apply, grads[p]))


def update(m, kind, me, rates, acts, grads, w, mom, into):
    l, k = m
    order = order_of(m)
    sc = len(grads) == 1
    dim, hid, rows = 1024, 4096, 512
    natural = (lambda i, me: i) if sc else (lambda i, me: block_at(i, order, me[0]))
    part = lambda p, i: jnp.clip(i - 4 * p, 0, 3)
    if k == 0:
        w_spec = pl.BlockSpec((1, dim, BW), lambda i, me: (l, 0, natural(i, me)))
        bf_spec, bf_shape = pl.BlockSpec((dim, BW), lambda i, me: (0, natural(i, me))), (dim, hid)
        if sc:
            g_specs = [pl.BlockSpec((1, dim, BW), lambda i, me: (i, 0, 0))]
        else:
            g_specs = [pl.BlockSpec((dim, BW), lambda i, me, p=p: (0, part(p, i))) for p in range(4)]
    else:
        w_spec = pl.BlockSpec((1, BW, dim), lambda i, me: (l, natural(i, me), 0))
        bf_spec, bf_shape = pl.BlockSpec((BW, dim), lambda i, me: (natural(i, me), 0)), (hid, dim)
        if sc:
            g_specs = [pl.BlockSpec((1, BW, dim), lambda i, me: (i, 0, 0))]
        else:
            g_specs = [pl.BlockSpec((BW, dim), lambda i, me, p=p: (part(p, i), 0)) for p in range(4)]
    whole = pl.BlockSpec((rows, dim), lambda i, me: (0, 0))
    z_spec = pl.BlockSpec((rows, BW), lambda i, me: (0, natural(i, me)))
    scratch = []
    if kind == 'up':
        act_specs = [whole]
        last, last_shape = z_spec, jax.ShapeDtypeStruct((rows, hid), jnp.bfloat16)
        scratch = [pltpu.VMEM((rows, dim), jnp.bfloat16)]
    elif kind == 'down':
        act_specs = [whole, z_spec]
        last, last_shape = whole, jax.ShapeDtypeStruct((rows, dim), jnp.float32)
    else:
        act_specs = []
        last, last_shape = bf_spec, jax.ShapeDtypeStruct(bf_shape, jnp.bfloat16)
    any_spec = pl.BlockSpec(memory_space=pl.ANY)
    in_specs = [pl.BlockSpec(memory_space=pltpu.SMEM)] + act_specs + g_specs + [w_spec, w_spec]
    args = [me, rates, *acts, *grads, w, mom]
    aliases = {}
    if into is not None:
        aliases = {len(args): 0, len(args) + 1: 1}
        in_specs += [any_spec, any_spec]
        args += list(into)
    full = jax.ShapeDtypeStruct(w.shape, jnp.float32)
    return pl.pallas_call(
        functools.partial(update_body, kind, len(grads)),
        grid_spec=pltpu.PrefetchScalarGridSpec(
            num_scalar_prefetch=1, grid=(BLOCKS,), in_specs=in_specs,
            out_specs=[w_spec, w_spec, last], scratch_shapes=scratch),
        out_shape=[full, full, last_shape],
        input_output_aliases=aliases,
        compiler_params=pltpu.CompilerParams(vmem_limit_bytes=48 << 20),
        cost_estimate=pl.CostEstimate(flops=10_000_000_000, bytes_accessed=80 << 20, transcendentals=0))(*args)


def solution(mesh):
    num_dev = mesh.shape['rep'] * mesh.shape['data']
    pairs = {bit: [(i, i ^ bit) for i in range(num_dev)] for bit in (1, 2, 4, 8)}

    def local_step(x_now, x_next, labels, w_up, w_down, w_head, mom_up, mom_down, mom_head, learn_rate, momentum):
        images, seq_len, model_dim = x_now.shape
        layers = w_up.shape[0]
        classes = w_head.shape[1]
        rows = images * seq_len
        global_batch = images * num_dev
        weights = (w_up, w_down)
        moms = (mom_up, mom_down)
        me = (lax.axis_index('rep') * mesh.shape['data'] + lax.axis_index('data')).astype(jnp.int32).reshape(1)
        rates = jnp.stack([learn_rate, momentum])
        token = [None]

        def hold(*args):
            if token[0] is None:
                return args
            return lax.optimization_barrier((*args, token[0]))[:-1]

        def cp(x, bit):
            return lax.ppermute(x, BATCH_AXES, pairs[bit])

        residual = x_now.reshape(rows, model_dim).astype(jnp.float32)
        saved = []
        for l in range(layers):
            residual, wu, wd = lax.optimization_barrier((residual, w_up, w_down))
            normed, inv_std = layer_norm(residual)
            act_in = normed.astype(jnp.bfloat16)
            pre_act = jnp.dot(act_in, wu[l].astype(jnp.bfloat16), preferred_element_type=jnp.float32)
            hidden, slope = gelu_parts(pre_act)
            hid_bf = hidden.astype(jnp.bfloat16)
            saved.append((normed, inv_std, act_in, slope, hid_bf))
            residual = residual + jnp.dot(hid_bf, wd[l].astype(jnp.bfloat16), preferred_element_type=jnp.float32)
        head_bf = w_head.astype(jnp.bfloat16)
        pooled, logits = pool_logits(residual, images, head_bf)
        soft_probs = jax.nn.softmax(logits, axis=-1)
        onehot = (labels[:, None] == jnp.arange(classes, dtype=jnp.int32)[None, :]).astype(jnp.float32)
        d_logits = ((soft_probs - onehot) / global_batch).astype(jnp.bfloat16)
        grad_head = jnp.einsum('bd,bc->dc', pooled, d_logits, preferred_element_type=jnp.float32)
        red_head = lax.psum(grad_head.astype(jnp.bfloat16), BATCH_AXES)
        d_pooled = jnp.einsum('bc,dc->bd', d_logits, head_bf, preferred_element_type=jnp.float32)
        d_resid = jnp.broadcast_to((d_pooled / seq_len)[:, None, :], (images, seq_len, model_dim)).reshape(rows, model_dim)

        d_res = {layers - 1: d_resid}
        v_bf = {layers - 1: d_resid.astype(jnp.bfloat16)}
        s_bf = {}
        box = {}
        new = [None, None]
        res_next = {(0, 0): x_next.reshape(rows, model_dim).astype(jnp.float32)}
        z_next = {}
        w_bf = {}

        def cut(x, k, lo, hi):
            n = x.shape[k == 0 and 1 or 0]
            lo, hi = lo * n // 4, hi * n // 4
            return x[:, lo:hi] if k == 0 else x[lo:hi]

        def fadd(a, b):
            return (a.astype(jnp.float32) + b.astype(jnp.float32)).astype(jnp.bfloat16)

        def step(op, l, k):
            m = (l, k)
            if op == 'S':
                normed, inv_std, act_in, slope, hid_bf = saved[l]
                v, sl, w, = hold(v_bf[l], slope, w_down)
                d_hidden = jnp.einsum('td,fd->tf', v, w[l].astype(jnp.bfloat16), preferred_element_type=jnp.float32)
                s_bf[l] = (d_hidden * sl).astype(jnp.bfloat16)
                token[0] = s_bf[l]
                return
            if op == 'N':
                normed, inv_std, act_in, slope, hid_bf = saved[l]
                s, dr, w = hold(s_bf[l], d_res[l], w_up)
                d_normed = jnp.einsum('tf,df->td', s, w[l].astype(jnp.bfloat16), preferred_element_type=jnp.float32)
                d_res[l - 1] = dr + norm_back(normed, inv_std, d_normed)
                v_bf[l - 1] = d_res[l - 1].astype(jnp.bfloat16)
                token[0] = v_bf[l - 1]
                return
            order = order_of(m)
            if op in 'ga':
                left, right = (saved[l][4], v_bf[l]) if k == 1 else (saved[l][2], s_bf[l])
            if op == 'g':
                left, right = hold(left, right)
                out = grad_send(m, me, left, right)
                box['r0', m] = cp(out, 1)
            elif op == 'a':
                left, right, got = hold(left, right, box.pop(('r0', m)))
                out, keep = grad_keep(m, me, left, right, got)
                box['k1', m] = keep
                box['r1', m] = cp(out, order[0])
            elif op in 'bc':
                src, dst = {'b': ('1', '2'), 'c': ('2', '3')}[op]
                keep, got = hold(box.pop(('k' + src, m)), box.pop(('r' + src, m)))
                out = fadd(cut(keep, k, 2, 4), cut(got, k, 2, 4))
                box['k' + dst, m] = fadd(cut(keep, k, 0, 2), cut(got, k, 0, 2))
                box['r' + dst, m] = cp(out, order[1] if op == 'b' else order[2])
                out = box['k' + dst, m]
            elif op == 'd':
                keep, got = hold(box.pop(('k3', m)), box.pop(('r3', m)))
                out = fadd(keep, got)
                if m in GATHER_SC:
                    box['g', m] = (lax.all_gather(out, BATCH_AXES),)
                else:
                    box['p0', m] = out
                    box['q0', m] = cp(out, order[2])
            elif op in 'ef':
                src, dst = {'e': ('0', '1'), 'f': ('1', '2')}[op]
                own, got = hold(box.pop(('p' + src, m)), box.pop(('q' + src, m)))
                out = jnp.concatenate([own, got], axis=1 - k)
                if op == 'e':
                    box['p1', m] = out
                    box['q1', m] = cp(out, order[1])
                else:
                    far = cp(out, order[0])
                    box['g', m] = (out, far, cp(out, 1))
            elif op == 'h':
                own, far, other = box['g', m]
                send, = hold(far)
                box['g', m] = (own, far, other, cp(send, 1))
                return
            elif op in 'KU':
                kind = 'plain' if op == 'U' else ('up' if k == 0 else 'down')
                acts = ()
                if kind == 'up':
                    acts = (res_next[l, 0],)
                elif kind == 'down':
                    acts = (res_next[l, 0], z_next[l])
                held = hold(*acts, *box.pop(('g', m)))
                acts, grads = held[:len(acts)], held[len(acts):]
                nw, nm, out = update(m, kind, me, rates, acts, grads, weights[k], moms[k], new[k])
                new[k] = (nw, nm)
                if kind == 'up':
                    z_next[l] = out
                elif kind == 'down':
                    res_next[l + 1, 0] = out
                else:
                    w_bf[m] = out
            elif op == 'F':
                if k == 0:
                    r, w = hold(res_next[l, 0], w_bf[m])
                    out = gelu(jnp.dot(layer_norm(r)[0].astype(jnp.bfloat16), w,
                                       preferred_element_type=jnp.float32)).astype(jnp.bfloat16)
                    z_next[l] = out
                else:
                    r, z, w = hold(res_next[l, 0], z_next[l], w_bf[m])
                    out = r + jnp.dot(z, w, preferred_element_type=jnp.float32)
                    res_next[l + 1, 0] = out
            elif op == 'H':
                red, mh, wh = hold(red_head, mom_head, w_head)
                nm = momentum * mh + red.astype(jnp.float32)
                nw = wh - learn_rate * nm
                box['head'] = (nw, nm)
                out = nm
            token[0] = out

        for op, l, k in ORDER:
            step(op, l, k)
        new_head, new_mom_head = box['head']
        _, logits_next = pool_logits(res_next[layers, 0], images, new_head.astype(jnp.bfloat16))
        return logits_next, new[0][0], new[1][0], new_head, new[0][1], new[1][1], new_mom_head

    batch_spec = P(BATCH_AXES)
    whole_spec = P()
    return jax.shard_map(local_step, mesh=mesh,
                         in_specs=(batch_spec, batch_spec, batch_spec) + (whole_spec,) * 8,
                         out_specs=(batch_spec,) + (whole_spec,) * 6,
                         check_vma=False)
```

time: 2530 us -> 1670 us (0.66)
  waiting for transfers between devices: 1580 us -> 505 us
  Pallas kernels: 0 us -> 594 us
  other arithmetic: 433 us -> 119 us
  matrix products: 397 us -> 303 us
  starting transfers between devices: 0.04 us -> 61.4 us
  local copies, waits for them, and re-layouts: 94.4 us -> 50.3 us
    psum x1, waiting for transfers between devices: 1580 us -> 17.1 us  [local_step(): red_head = lax.psum(grad_head.astype(jnp.bfloat16), BATCH_AXES)]
    pallas_call x0 -> x36, Pallas kernels: none -> 594 us  [the longest x12 379 us: update(): pl.pallas_call(functools.partial(update_body, kind, len(grads)), grid_spe...]
    ppermute x0 -> x78, waiting for transfers between devices: none -> 487 us  [cp(): return lax.ppermute(x, BATCH_AXES, pairs[bit])]
    another operation x4 -> x1, other arithmetic: 412 us -> 0.08 us  [local_step(): rates = jnp.stack([learn_rate, momentum])]
    dot_general x40 -> x27, matrix products: 391 us -> 298 us  [the longest x6 79.3 us: step(): jnp.einsum('td,fd->tf', v, w[l].astype(jnp.bfloat16), preferred_element_t...]
    convert_element_type x4 -> x49, other arithmetic: 2.51 us -> 90.6 us  [the longest x36 73.7 us: fadd(): return (a.astype(jnp.float32) + b.astype(jnp.float32)).astype(jnp.bfloat16)]
    ppermute x0 -> x78, starting transfers between devices: none -> 61.1 us  [cp(): return lax.ppermute(x, BATCH_AXES, pairs[bit])]
    unnamed x98 -> x232, local copies, waits for them, and re-layouts: 78.7 us -> 38.2 us
  transfers between devices with their start and end apart: 1 -> 85, of which waited for: 1 -> 25; matrix products, arithmetic and copies ran while one was open for 0% -> 15% of each run, Pallas kernels for 0% -> 31%
where the time goes in v1:
time: 1670 us; the launch traced here: 1650 us
  Pallas kernels  594 us (36%)
  waiting for transfers between devices  505 us (30%)
  matrix products  303 us (18%)
  other arithmetic  119 us (7%)
  starting transfers between devices  61.4 us (4%)
  local copies, waits for them, and re-layouts  50.3 us (3%)
  between operations  16.7 us (1%)
    ppermute x78, waiting for transfers between devices, cp(): return lax.ppermute(x, BATCH_AXES, pairs[bit])  487 us
    pallas_call x12, Pallas kernels, update(): pl.pallas_call(functools.partial(update_body, kind, len(grads)), grid_spe...  379 us
    dot_general x6, matrix products, step(): jnp.einsum('td,fd->tf', v, w[l].astype(jnp.bfloat16), preferred_element_t...  79.3 us
    dot_general x6, matrix products, local_step(): jnp.dot(act_in, wu[l].astype(jnp.bfloat16), preferred_element_type=jnp.fl...  77.4 us
    convert_element_type x36, other arithmetic, fadd(): return (a.astype(jnp.float32) + b.astype(jnp.float32)).astype(jnp.bfloat16)  73.7 us
    ppermute x78, starting transfers between devices, cp(): return lax.ppermute(x, BATCH_AXES, pairs[bit])  61.1 us
    dot_general x6, matrix products, local_step(): jnp.dot(hid_bf, wd[l].astype(jnp.bfloat16), preferred_element_type=jnp.fl...  58.9 us
    pallas_call x6, Pallas kernels, grad_keep(): pl.pallas_call(grad_up_keep, grid_spec=pltpu.PrefetchScalarGridSpec(num_s...  57.7 us
  transfers between devices with their start and end apart: 85, of which 25 were waited for; matrix products, arithmetic and copies ran while one was open for 15% of the time, Pallas kernels for 31%

profile of v1, /device:TPU:0, one launch (start us, length us, event | category | flops | bytes accessed | tf_op | source)
XLA Modules:
  0.0 1649.7 jit_solution(3608744726416316518)
XLA Ops:
  184.9 13.2 multiply_convert_fusion.7.s_ref
  247.2 13.2 multiply_convert_fusion.6.s_ref
  284.7 13.6 fusion.149
  302.0 25.9 %collective-permute-done.4 = bf16[1024,1024]{1,0:T(8,128)(2,1)S(1)} collective-permute-done((bf16[1024,1024]{1,0:T(8,128)(2,1)}, bf16[1024,1024]{1,0:T(8,128)(2,1)S(1)}, u32[]{:S(2)}, u32[]{:S(2)}) %collective-permute-start.4) | collective-permute-done | bytes 2097184 | tf_op jit(solution)/shard_map/ppermute | solution.py:310
  371.2 13.5 multiply_convert_fusion.4.s_ref
  430.3 13.1 multiply_convert_fusion.3.s_ref
  447.7 35.2 %collective-permute-done.10 = bf16[512,1024]{1,0:T(8,128)(2,1)S(1)} collective-permute-done((bf16[512,1024]{1,0:T(8,128)(2,1)S(1)}, bf16[512,1024]{1,0:T(8,128)(2,1)S(1)}, u32[]{:S(2)}, u32[]{:S(2)}) %collective-permute-start.10) | collective-permute-done | bytes 1048608 | tf_op jit(solution)/shard_map/ppermute | solution.py:310
  625.3 31.2 %shard_map.162 = (f32[6,4096,1024]{2,1,0:T(8,128)}, f32[6,4096,1024]{2,1,0:T(8,128)}, bf16[4096,1024]{1,0:T(8,128)(2,1)}) custom-call(s32[1]{0:T(128)} %bitcast.me_ref.refs_0_, f32[2]{0:T(128)S(1)} %pad_maximum_fusion.refs_1_, bf16[16,256,1024]{2,1,0:T(8,128)(2,1)} %bitcast.170, f32[6,4096,1024]{2,1,0:T(8,128)} %refs_8_.7, f32[6,4096,1024]{2,1,0:T(8,128)} %refs_9_.7), custom_call_target="tpu_custom_call" | custom-call | flops 10000000000 | bytes 83886080 | tf_op jit(solution)/shard_map/pallas_call | solution.py:277
  678.4 31.4 %shard_map.163 = (f32[6,4096,1024]{2,1,0:T(8,128)}, f32[6,4096,1024]{2,1,0:T(8,128)}, bf16[4096,1024]{1,0:T(8,128)(2,1)}) custom-call(s32[1]{0:T(128)} %bitcast.me_ref.refs_0_, f32[2]{0:T(128)S(1)} %pad_maximum_fusion.refs_1_, bf16[16,256,1024]{2,1,0:T(8,128)(2,1)} %bitcast.173, ...), custom_call_target="tpu_custom_call", output_to_operand_aliasing={{0}: (5, {}), {1}: (6, {})} | custom-call | flops 10000000000 | bytes 83886080 | tf_op jit(solution)/shard_map/pallas_call | solution.py:277
  709.8 17.1 %all-reduce.2.cloned.1.call-done = bf16[1024,1000]{0,1:T(8,128)(2,1)} async-done(((bf16[1024,1000]{0,1:T(8,128)(2,1)}), bf16[1024,1000]{0,1:T(8,128)(2,1)}) %all-reduce.2.cloned.1.call-update) | async-done | bytes 2048016 | tf_op jit(solution)/shard_map/psum | solution.py:329
  777.6 22.7 %collective-permute-done.31 = bf16[512,1024]{1,0:T(8,128)(2,1)S(1)} collective-permute-done((bf16[512,1024]{1,0:T(8,128)(2,1)S(1)}, bf16[512,1024]{1,0:T(8,128)(2,1)S(1)}, u32[]{:S(2)}, u32[]{:S(2)}) %collective-permute-start.31) | collective-permute-done | bytes 1048608 | tf_op jit(solution)/shard_map/ppermute | solution.py:310
  820.5 22.0 %collective-permute-done.28 = bf16[1024,1024]{1,0:T(8,128)(2,1)} collective-permute-done((bf16[1024,1024]{1,0:T(8,128)(2,1)}, bf16[1024,1024]{1,0:T(8,128)(2,1)}, u32[]{:S(2)}, u32[]{:S(2)}) %collective-permute-start.28) | collective-permute-done | bytes 2097184 | tf_op jit(solution)/shard_map/ppermute | solution.py:310
  852.4 27.0 %collective-permute-done.40 = bf16[256,1024]{1,0:T(8,128)(2,1)S(1)} collective-permute-done((bf16[256,1024]{1,0:T(8,128)(2,1)}, bf16[256,1024]{1,0:T(8,128)(2,1)S(1)}, u32[]{:S(2)}, u32[]{:S(2)}) %collective-permute-start.40) | collective-permute-done | bytes 524320 | tf_op jit(solution)/shard_map/ppermute | solution.py:310
  884.0 32.2 %shard_map.164 = (f32[6,1024,4096]{2,1,0:T(8,128)}, f32[6,1024,4096]{2,1,0:T(8,128)}, bf16[1024,4096]{1,0:T(8,128)(2,1)}) custom-call(s32[1]{0:T(128)} %bitcast.me_ref.refs_0_, f32[2]{0:T(128)S(1)} %pad_maximum_fusion.refs_1_, bf16[1024,1024]{1,0:T(8,128)(2,1)} %constant_dynamic-update-slice_fusion.6.refs_2_, ...), custom_call_target="tpu_custom_call" | custom-call | flops 10000000000 | bytes 83886080 | tf_op jit(solution)/shard_map/pallas_call | solution.py:277
  930.9 31.9 %shard_map.165 = (f32[6,1024,4096]{2,1,0:T(8,128)}, f32[6,1024,4096]{2,1,0:T(8,128)}, bf16[1024,4096]{1,0:T(8,128)(2,1)}) custom-call(s32[1]{0:T(128)} %bitcast.me_ref.refs_0_, f32[2]{0:T(128)S(1)} %pad_maximum_fusion.refs_1_, bf16[1024,1024]{1,0:T(8,128)(2,1)S(1)} %constant_dynamic-update-slice_fusion.4.refs_2_, ...), custom_call_target="tpu_custom_call", output_to_operand_aliasing={{0}: (8, {}), {1}: (9, {})} | custom-call | flops 10000000000 | bytes 83886080 | tf_op jit(solution)/shard_map/pallas_call | solution.py:277
  998.5 15.9 collective-permute-done.57
  1018.2 39.8 %collective-permute-done.56 = bf16[512,1024]{1,0:T(8,128)(2,1)S(1)} collective-permute-done((bf16[512,1024]{1,0:T(8,128)(2,1)}, bf16[512,1024]{1,0:T(8,128)(2,1)S(1)}, u32[]{:S(2)}, u32[]{:S(2)}) %collective-permute-start.56) | collective-permute-done | bytes 1048608 | tf_op jit(solution)/shard_map/ppermute | solution.py:310
  1063.3 26.0 %collective-permute-done.55 = bf16[1024,1024]{1,0:T(8,128)(2,1)S(1)} collective-permute-done((bf16[1024,1024]{1,0:T(8,128)(2,1)}, bf16[1024,1024]{1,0:T(8,128)(2,1)S(1)}, u32[]{:S(2)}, u32[]{:S(2)}) %collective-permute-start.55) | collective-permute-done | bytes 2097184 | tf_op jit(solution)/shard_map/ppermute | solution.py:310
  1091.3 14.6 collective-permute-done.54
  1110.0 31.9 %shard_map.166 = (f32[6,1024,4096]{2,1,0:T(8,128)}, f32[6,1024,4096]{2,1,0:T(8,128)}, bf16[512,4096]{1,0:T(8,128)(2,1)}) custom-call(s32[1]{0:T(128)} %bitcast.me_ref.refs_0_, f32[2]{0:T(128)S(1)} %pad_maximum_fusion.refs_1_, f32[512,1024]{1,0:T(8,128)S(1)} %bitcast_convert_fusion.2.refs_2_, ...), custom_call_target="tpu_custom_call", output_to_operand_aliasing={{0}: (6, {}), {1}: (7, {})} | custom-call | flops 10000000000 | bytes 83886080 | tf_op jit(solution)/shard_map/pallas_call | solution.py:277
  1143.6 26.8 %collective-permute-done.58.refs_5_ = bf16[1024,1024]{1,0:T(8,128)(2,1)} collective-permute-done((bf16[1024,1024]{1,0:T(8,128)(2,1)}, bf16[1024,1024]{1,0:T(8,128)(2,1)}, u32[]{:S(2)}, u32[]{:S(2)}) %collective-permute-start.58) | collective-permute-done | bytes 2097184 | tf_op jit(solution)/shard_map/ppermute | solution.py:310
  1176.2 32.4 %shard_map.167 = (f32[6,4096,1024]{2,1,0:T(8,128)}, f32[6,4096,1024]{2,1,0:T(8,128)}, f32[512,1024]{1,0:T(8,128)S(1)}) custom-call(s32[1]{0:T(128)} %bitcast.me_ref.refs_0_, f32[2]{0:T(128)S(1)} %pad_maximum_fusion.refs_1_, f32[512,1024]{1,0:T(8,128)S(1)} %bitcast_convert_fusion.2.refs_2_, ...), custom_call_target="tpu_custom_call", output_to_operand_aliasing={{0}: (10, {}), {1}: (11, {})} | custom-call | flops 10000000000 | bytes 83886080 | tf_op jit(solution)/shard_map/pallas_call | solution.py:277
  1211.0 17.8 %collective-permute-done.62 = bf16[1024,512]{1,0:T(8,128)(2,1)S(1)} collective-permute-done((bf16[1024,512]{1,0:T(8,128)(2,1)S(1)}, bf16[1024,512]{1,0:T(8,128)(2,1)S(1)}, u32[]{:S(2)}, u32[]{:S(2)}) %collective-permute-start.62) | collective-permute-done | bytes 1048608 | tf_op jit(solution)/shard_map/ppermute | solution.py:310
  1231.5 30.6 %shard_map.168 = (f32[6,1024,4096]{2,1,0:T(8,128)}, f32[6,1024,4096]{2,1,0:T(8,128)}, bf16[512,4096]{1,0:T(8,128)(2,1)}) custom-call(s32[1]{0:T(128)} %bitcast.me_ref.refs_0_, f32[2]{0:T(128)S(1)} %pad_maximum_fusion.refs_1_, f32[512,1024]{1,0:T(8,128)S(1)} %copy-done.1, ...), custom_call_target="tpu_custom_call", output_to_operand_aliasing={{0}: (6, {}), {1}: (7, {})} | custom-call | flops 10000000000 | bytes 83886080 | tf_op jit(solution)/shard_map/pallas_call | solution.py:277
  1263.2 73.5 %collective-permute-done.65.refs_5_ = bf16[1024,1024]{1,0:T(8,128)(2,1)S(1)} collective-permute-done((bf16[1024,1024]{1,0:T(8,128)(2,1)}, bf16[1024,1024]{1,0:T(8,128)(2,1)S(1)}, u32[]{:S(2)}, u32[]{:S(2)}) %collective-permute-start.65) | collective-permute-done | bytes 2097184 | tf_op jit(solution)/shard_map/ppermute | solution.py:310
  1356.5 32.0 %shard_map.169 = (f32[6,4096,1024]{2,1,0:T(8,128)}, f32[6,4096,1024]{2,1,0:T(8,128)}, f32[512,1024]{1,0:T(8,128)S(1)}) custom-call(s32[1]{0:T(128)} %bitcast.me_ref.refs_0_, f32[2]{0:T(128)S(1)} %pad_maximum_fusion.refs_1_, f32[512,1024]{1,0:T(8,128)S(1)} %copy-done.1, ...), custom_call_target="tpu_custom_call", output_to_operand_aliasing={{0}: (10, {}), {1}: (11, {})} | custom-call | flops 10000000000 | bytes 83886080 | tf_op jit(solution)/shard_map/pallas_call | solution.py:277
  1393.5 30.5 %shard_map.170 = (f32[6,1024,4096]{2,1,0:T(8,128)}, f32[6,1024,4096]{2,1,0:T(8,128)}, bf16[512,4096]{1,0:T(8,128)(2,1)}) custom-call(s32[1]{0:T(128)} %bitcast.me_ref.refs_0_, f32[2]{0:T(128)S(1)} %pad_maximum_fusion.refs_1_, f32[512,1024]{1,0:T(8,128)S(1)} %copy-done.3, ...), custom_call_target="tpu_custom_call", output_to_operand_aliasing={{0}: (6, {}), {1}: (7, {})} | custom-call | flops 10000000000 | bytes 83886080 | tf_op jit(solution)/shard_map/pallas_call | solution.py:277
  1424.0 35.0 %collective-permute-done.73 = bf16[512,1024]{1,0:T(8,128)(2,1)S(1)} collective-permute-done((bf16[512,1024]{1,0:T(8,128)(2,1)}, bf16[512,1024]{1,0:T(8,128)(2,1)S(1)}, u32[]{:S(2)}, u32[]{:S(2)}) %collective-permute-start.73) | collective-permute-done | bytes 1048608 | tf_op jit(solution)/shard_map/ppermute | solution.py:310
  1463.7 44.9 %collective-permute-done.75.refs_5_ = bf16[1024,1024]{1,0:T(8,128)(2,1)} collective-permute-done((bf16[1024,1024]{1,0:T(8,128)(2,1)}, bf16[1024,1024]{1,0:T(8,128)(2,1)}, u32[]{:S(2)}, u32[]{:S(2)}) %collective-permute-start.75) | collective-permute-done | bytes 2097184 | tf_op jit(solution)/shard_map/ppermute | solution.py:310
  1510.7 32.6 %shard_map.171 = (f32[6,4096,1024]{2,1,0:T(8,128)}, f32[6,4096,1024]{2,1,0:T(8,128)}, f32[512,1024]{1,0:T(8,128)S(1)}) custom-call(s32[1]{0:T(128)} %bitcast.me_ref.refs_0_, f32[2]{0:T(128)S(1)} %pad_maximum_fusion.refs_1_, f32[512,1024]{1,0:T(8,128)S(1)} %copy-done.3, ...), custom_call_target="tpu_custom_call", output_to_operand_aliasing={{0}: (10, {}), {1}: (11, {})} | custom-call | flops 10000000000 | bytes 83886080 | tf_op jit(solution)/shard_map/pallas_call | solution.py:277
  1543.3 30.6 %shard_map.172 = (f32[6,1024,4096]{2,1,0:T(8,128)}, f32[6,1024,4096]{2,1,0:T(8,128)}, bf16[512,4096]{1,0:T(8,128)(2,1)}) custom-call(s32[1]{0:T(128)} %bitcast.me_ref.refs_0_, f32[2]{0:T(128)S(1)} %pad_maximum_fusion.refs_1_, f32[512,1024]{1,0:T(8,128)S(1)} %get-tuple-element.635.refs_2_, ...), custom_call_target="tpu_custom_call", output_to_operand_aliasing={{0}: (6, {}), {1}: (7, {})} | custom-call | flops 10000000000 | bytes 83886080 | tf_op jit(solution)/shard_map/pallas_call | solution.py:277
  1573.8 32.2 %shard_map.173 = (f32[6,4096,1024]{2,1,0:T(8,128)}, f32[6,4096,1024]{2,1,0:T(8,128)}, f32[512,1024]{1,0:T(8,128)S(1)}) custom-call(s32[1]{0:T(128)} %bitcast.me_ref.refs_0_, f32[2]{0:T(128)S(1)} %pad_maximum_fusion.refs_1_, f32[512,1024]{1,0:T(8,128)S(1)} %get-tuple-element.635.refs_2_, ...), custom_call_target="tpu_custom_call", output_to_operand_aliasing={{0}: (10, {}), {1}: (11, {})} | custom-call | flops 10000000000 | bytes 83886080 | tf_op jit(solution)/shard_map/pallas_call | solution.py:277
  (551 shorter events, 742.8 us)
Async XLA Ops:
  7.2 617.7 %all-gather.15.cloned.1.call-start = ((), (), s32[]{:S(2)}) async-start(), calls=%async_computation.2 | async-start | bytes 8912896 | tf_op jit(solution)/shard_map/all_gather | solution.py:390
  281.6 74.7 %collective-permute-start.5 = (bf16[1024,1024]{1,0:T(8,128)(2,1)}, bf16[1024,1024]{1,0:T(8,128)(2,1)}, u32[]{:S(2)}, u32[]{:S(2)}) collective-permute-start(bf16[1024,1024]{1,0:T(8,128)(2,1)} %get-tuple-element.368), channel_id=1, source_target_pairs={{0,4},{1,5},{2,6},{3,7},{4,0},{5,1},{6,2},{7,3},{8,12},{9,13},{10,... | collective-permute-start | bytes 6291464 | tf_op jit(solution)/shard_map/ppermute | solution.py:310
  283.1 104.3 %collective-permute-start.6 = (bf16[1024,1024]{1,0:T(8,128)(2,1)}, bf16[1024,1024]{1,0:T(8,128)(2,1)}, u32[]{:S(2)}, u32[]{:S(2)}) collective-permute-start(bf16[1024,1024]{1,0:T(8,128)(2,1)} %get-tuple-element.375), channel_id=1, source_target_pairs={{0,8},{1,9},{2,10},{3,11},{4,12},{5,13},{6,14},{7,15},{8,0},{9,1},... | collective-permute-start | bytes 6291464 | tf_op jit(solution)/shard_map/ppermute | solution.py:310
  341.7 76.9 %collective-permute-start.8 = (bf16[1024,1024]{1,0:T(8,128)(2,1)}, bf16[1024,1024]{1,0:T(8,128)(2,1)}, u32[]{:S(2)}, u32[]{:S(2)}) collective-permute-start(bf16[1024,1024]{1,0:T(8,128)(2,1)} %get-tuple-element.387), channel_id=1, source_target_pairs={{0,2},{1,3},{2,0},{3,1},{4,6},{5,7},{6,4},{7,5},{8,10},{9,11},{10,... | collective-permute-start | bytes 6291464 | tf_op jit(solution)/shard_map/ppermute | solution.py:310
  445.5 232.9 %all-gather.13.cloned.1.call-start = ((), (), s32[]{:S(2)}) async-start(), calls=%async_computation.1 | async-start | bytes 8912896 | tf_op jit(solution)/shard_map/all_gather | solution.py:390
  572.0 154.9 %all-reduce.2.cloned.1.call-start = ((), (), s32[]{:S(2)}) async-start(), calls=%async_computation | async-start | bytes 4096000 | tf_op jit(solution)/shard_map/psum | solution.py:329
  574.8 535.2 %all-gather.17.cloned.1.call-start = ((), (), s32[]{:S(2)}) async-start(), calls=%async_computation.3 | async-start | bytes 8912896 | tf_op jit(solution)/shard_map/all_gather | solution.py:390
  577.6 87.8 %collective-permute-start.23 = (bf16[1024,1024]{1,0:T(8,128)(2,1)}, bf16[1024,1024]{1,0:T(8,128)(2,1)}, u32[]{:S(2)}, u32[]{:S(2)}) collective-permute-start(bf16[1024,1024]{1,0:T(8,128)(2,1)} %get-tuple-element.439), channel_id=1, source_target_pairs={{0,8},{1,9},{2,10},{3,11},{4,12},{5,13},{6,14},{7,15},{8,0},{9,1},... | collective-permute-start | bytes 6291464 | tf_op jit(solution)/shard_map/ppermute | solution.py:310
  578.3 92.2 %collective-permute-start.22 = (bf16[1024,1024]{1,0:T(8,128)(2,1)}, bf16[1024,1024]{1,0:T(8,128)(2,1)}, u32[]{:S(2)}, u32[]{:S(2)}) collective-permute-start(bf16[1024,1024]{1,0:T(8,128)(2,1)} %get-tuple-element.443), channel_id=1, source_target_pairs={{0,2},{1,3},{2,0},{3,1},{4,6},{5,7},{6,4},{7,5},{8,10},{9,11},{10,... | collective-permute-start | bytes 6291464 | tf_op jit(solution)/shard_map/ppermute | solution.py:310
  579.8 94.0 %collective-permute-start.21 = (bf16[1024,1024]{1,0:T(8,128)(2,1)}, bf16[1024,1024]{1,0:T(8,128)(2,1)}, u32[]{:S(2)}, u32[]{:S(2)}) collective-permute-start(bf16[1024,1024]{1,0:T(8,128)(2,1)} %get-tuple-element.449), channel_id=1, source_target_pairs={{0,4},{1,5},{2,6},{3,7},{4,0},{5,1},{6,2},{7,3},{8,12},{9,13},{10,... | collective-permute-start | bytes 6291464 | tf_op jit(solution)/shard_map/ppermute | solution.py:310
  599.7 136.0 %collective-permute-start.20 = (bf16[1024,2048]{1,0:T(8,128)(2,1)}, bf16[1024,2048]{1,0:T(8,128)(2,1)}, u32[]{:S(2)}, u32[]{:S(2)}) collective-permute-start(bf16[1024,2048]{1,0:T(8,128)(2,1)} %gus.9), channel_id=1, source_target_pairs={{0,1},{1,0},{2,3},{3,2},{4,5},{5,4},{6,7},{7,6},{8,9},{9,8},{10,11... | collective-permute-start | bytes 12582920 | tf_op jit(solution)/shard_map/ppermute | solution.py:310
  624.9 131.5 %collective-permute-start.26 = (bf16[1024,2048]{1,0:T(8,128)(2,1)}, bf16[1024,2048]{1,0:T(8,128)(2,1)}, u32[]{:S(2)}, u32[]{:S(2)}) collective-permute-start(bf16[1024,2048]{1,0:T(8,128)(2,1)} %gus.10), channel_id=1, source_target_pairs={{0,1},{1,0},{2,3},{3,2},{4,5},{5,4},{6,7},{7,6},{8,9},{9,8},{10,11... | collective-permute-start | bytes 12582920 | tf_op jit(solution)/shard_map/ppermute | solution.py:310
  665.3 100.6 %collective-permute-start.33 = (bf16[1024,512]{1,0:T(8,128)(2,1)S(1)}, bf16[1024,512]{1,0:T(8,128)(2,1)}, u32[]{:S(2)}, u32[]{:S(2)}) collective-permute-start(bf16[1024,512]{1,0:T(8,128)(2,1)S(1)} %constant_dynamic-update-slice_fusion), channel_id=1, source_target_pairs={{0,8},{1,9},{2,10},{3,11},{4,12},{5,13},{6,14},{7,15},{8,0},{9,1},... | collective-permute-start | bytes 3145736 | tf_op jit(solution)/shard_map/ppermute | solution.py:310
  670.5 133.8 %collective-permute-start.29 = (bf16[2048,1024]{1,0:T(8,128)(2,1)}, bf16[2048,1024]{1,0:T(8,128)(2,1)}, u32[]{:S(2)}, u32[]{:S(2)}) collective-permute-start(bf16[2048,1024]{1,0:T(8,128)(2,1)} %gds.10), channel_id=1, source_target_pairs={{0,1},{1,0},{2,3},{3,2},{4,5},{5,4},{6,7},{7,6},{8,9},{9,8},{10,11... | collective-permute-start | bytes 12582920 | tf_op jit(solution)/shard_map/ppermute | solution.py:310
  673.8 80.0 %collective-permute-start.27 = (bf16[512,1024]{1,0:T(8,128)(2,1)}, bf16[512,1024]{1,0:T(8,128)(2,1)}, u32[]{:S(2)}, u32[]{:S(2)}) collective-permute-start(bf16[512,1024]{1,0:T(8,128)(2,1)} %get-tuple-element.705), channel_id=1, source_target_pairs={{0,2},{1,3},{2,0},{3,1},{4,6},{5,7},{6,4},{7,5},{8,10},{9,11},{10,... | collective-permute-start | bytes 3145736 | tf_op jit(solution)/shard_map/ppermute | solution.py:310
  776.3 66.2 %collective-permute-start.28 = (bf16[1024,1024]{1,0:T(8,128)(2,1)}, bf16[1024,1024]{1,0:T(8,128)(2,1)}, u32[]{:S(2)}, u32[]{:S(2)}) collective-permute-start(bf16[1024,1024]{1,0:T(8,128)(2,1)} %get-tuple-element.494), channel_id=1, source_target_pairs={{0,8},{1,9},{2,10},{3,11},{4,12},{5,13},{6,14},{7,15},{8,0},{9,1},... | collective-permute-start | bytes 6291464 | tf_op jit(solution)/shard_map/ppermute | solution.py:310
  803.0 78.5 %collective-permute-start.38 = (bf16[1024,1024]{1,0:T(8,128)(2,1)}, bf16[1024,1024]{1,0:T(8,128)(2,1)}, u32[]{:S(2)}, u32[]{:S(2)}) collective-permute-start(bf16[1024,1024]{1,0:T(8,128)(2,1)} %constant_dynamic-update-slice_fusion.6.refs_2_), channel_id=1, source_target_pairs={{0,1},{1,0},{2,3},{3,2},{4,5},{5,4},{6,7},{7,6},{8,9},{9,8},{10,11... | collective-permute-start | bytes 6291464 | tf_op jit(solution)/shard_map/ppermute | solution.py:310
  819.9 101.4 %collective-permute-start.42 = (bf16[1024,1024]{1,0:T(8,128)(2,1)}, bf16[1024,1024]{1,0:T(8,128)(2,1)}, u32[]{:S(2)}, u32[]{:S(2)}) collective-permute-start(bf16[1024,1024]{1,0:T(8,128)(2,1)} %get-tuple-element.506), channel_id=1, source_target_pairs={{0,2},{1,3},{2,0},{3,1},{4,6},{5,7},{6,4},{7,5},{8,10},{9,11},{10,... | collective-permute-start | bytes 6291464 | tf_op jit(solution)/shard_map/ppermute | solution.py:310
  848.1 76.8 %collective-permute-start.46 = (bf16[1024,1024]{1,0:T(8,128)(2,1)S(1)}, bf16[1024,1024]{1,0:T(8,128)(2,1)}, u32[]{:S(2)}, u32[]{:S(2)}) collective-permute-start(bf16[1024,1024]{1,0:T(8,128)(2,1)S(1)} %constant_dynamic-update-slice_fusion.4.refs_2_), channel_id=1, source_target_pairs={{0,4},{1,5},{2,6},{3,7},{4,0},{5,1},{6,2},{7,3},{8,12},{9,13},{10,... | collective-permute-start | bytes 6291464 | tf_op jit(solution)/shard_map/ppermute | solution.py:310
  996.8 233.3 %all-gather.19.cloned.1.call-start = ((), (), s32[]{:S(2)}) async-start(), calls=%async_computation.4 | async-start | bytes 8912896 | tf_op jit(solution)/shard_map/all_gather | solution.py:390
  997.4 394.5 %all-gather.21.cloned.1.call-start = ((), (), s32[]{:S(2)}) async-start(), calls=%async_computation.5 | async-start | bytes 8912896 | tf_op jit(solution)/shard_map/all_gather | solution.py:390
  1015.3 527.9 %all-gather.23.cloned.1.call-start = ((), (), s32[]{:S(2)}) async-start(), calls=%async_computation.6 | async-start | bytes 8912896 | tf_op jit(solution)/shard_map/all_gather | solution.py:390
  1015.4 73.9 %collective-permute-start.55 = (bf16[1024,1024]{1,0:T(8,128)(2,1)}, bf16[1024,1024]{1,0:T(8,128)(2,1)S(1)}, u32[]{:S(2)}, u32[]{:S(2)}) collective-permute-start(bf16[1024,1024]{1,0:T(8,128)(2,1)} %get-tuple-element.549), channel_id=1, source_target_pairs={{0,8},{1,9},{2,10},{3,11},{4,12},{5,13},{6,14},{7,15},{8,0},{9,1},... | collective-permute-start | bytes 6291464 | tf_op jit(solution)/shard_map/ppermute | solution.py:310
  1016.4 90.5 %collective-permute-start.53 = (bf16[1024,1024]{1,0:T(8,128)(2,1)}, bf16[1024,1024]{1,0:T(8,128)(2,1)S(1)}, u32[]{:S(2)}, u32[]{:S(2)}) collective-permute-start(bf16[1024,1024]{1,0:T(8,128)(2,1)} %get-tuple-element.545), channel_id=1, source_target_pairs={{0,4},{1,5},{2,6},{3,7},{4,0},{5,1},{6,2},{7,3},{8,12},{9,13},{10,... | collective-permute-start | bytes 6291464 | tf_op jit(solution)/shard_map/ppermute | solution.py:310
  1062.3 108.1 %collective-permute-start.58 = (bf16[1024,1024]{1,0:T(8,128)(2,1)}, bf16[1024,1024]{1,0:T(8,128)(2,1)}, u32[]{:S(2)}, u32[]{:S(2)}) collective-permute-start(bf16[1024,1024]{1,0:T(8,128)(2,1)} %constant_dynamic-update-slice_fusion.14.refs_4_), channel_id=1, source_target_pairs={{0,8},{1,9},{2,10},{3,11},{4,12},{5,13},{6,14},{7,15},{8,0},{9,1},... | collective-permute-start | bytes 6291464 | tf_op jit(solution)/shard_map/ppermute | solution.py:310
  1063.3 110.2 %collective-permute-start.59 = (bf16[1024,1024]{1,0:T(8,128)(2,1)}, bf16[1024,1024]{1,0:T(8,128)(2,1)}, u32[]{:S(2)}, u32[]{:S(2)}) collective-permute-start(bf16[1024,1024]{1,0:T(8,128)(2,1)} %constant_dynamic-update-slice_fusion.14.refs_4_), channel_id=1, source_target_pairs={{0,1},{1,0},{2,3},{3,2},{4,5},{5,4},{6,7},{7,6},{8,9},{9,8},{10,11... | collective-permute-start | bytes 6291464 | tf_op jit(solution)/shard_map/ppermute | solution.py:310
  1263.1 73.6 %collective-permute-start.65 = (bf16[1024,1024]{1,0:T(8,128)(2,1)}, bf16[1024,1024]{1,0:T(8,128)(2,1)S(1)}, u32[]{:S(2)}, u32[]{:S(2)}) collective-permute-start(bf16[1024,1024]{1,0:T(8,128)(2,1)} %constant_dynamic-update-slice_fusion.12.refs_4_), channel_id=1, source_target_pairs={{0,4},{1,5},{2,6},{3,7},{4,0},{5,1},{6,2},{7,3},{8,12},{9,13},{10,... | collective-permute-start | bytes 6291464 | tf_op jit(solution)/shard_map/ppermute | solution.py:310
  1263.2 91.2 %collective-permute-start.66 = (bf16[1024,1024]{1,0:T(8,128)(2,1)}, bf16[1024,1024]{1,0:T(8,128)(2,1)S(1)}, u32[]{:S(2)}, u32[]{:S(2)}) collective-permute-start(bf16[1024,1024]{1,0:T(8,128)(2,1)} %constant_dynamic-update-slice_fusion.12.refs_4_), channel_id=1, source_target_pairs={{0,1},{1,0},{2,3},{3,2},{4,5},{5,4},{6,7},{7,6},{8,9},{9,8},{10,11... | collective-permute-start | bytes 6291464 | tf_op jit(solution)/shard_map/ppermute | solution.py:310
  1389.9 73.3 %collective-permute-start.71 = (bf16[1024,1024]{1,0:T(8,128)(2,1)S(1)}, bf16[1024,1024]{1,0:T(8,128)(2,1)}, u32[]{:S(2)}, u32[]{:S(2)}) collective-permute-start(bf16[1024,1024]{1,0:T(8,128)(2,1)S(1)} %constant_dynamic-update-slice_fusion.20.refs_4_), channel_id=1, source_target_pairs={{0,2},{1,3},{2,0},{3,1},{4,6},{5,7},{6,4},{7,5},{8,10},{9,11},{10,... | collective-permute-start | bytes 6291464 | tf_op jit(solution)/shard_map/ppermute | solution.py:310
  1390.5 68.5 %collective-permute-start.73 = (bf16[512,1024]{1,0:T(8,128)(2,1)}, bf16[512,1024]{1,0:T(8,128)(2,1)S(1)}, u32[]{:S(2)}, u32[]{:S(2)}) collective-permute-start(bf16[512,1024]{1,0:T(8,128)(2,1)} %constant_dynamic-update-slice_fusion.18), channel_id=1, source_target_pairs={{0,2},{1,3},{2,0},{3,1},{4,6},{5,7},{6,4},{7,5},{8,10},{9,11},{10,... | collective-permute-start | bytes 3145736 | tf_op jit(solution)/shard_map/ppermute | solution.py:310
  1463.7 110.2 %collective-permute-start.76 = (bf16[1024,1024]{1,0:T(8,128)(2,1)}, bf16[1024,1024]{1,0:T(8,128)(2,1)}, u32[]{:S(2)}, u32[]{:S(2)}) collective-permute-start(bf16[1024,1024]{1,0:T(8,128)(2,1)} %constant_dynamic-update-slice_fusion.22.refs_4_), channel_id=1, source_target_pairs={{0,1},{1,0},{2,3},{3,2},{4,5},{5,4},{6,7},{7,6},{8,9},{9,8},{10,11... | collective-permute-start | bytes 6291464 | tf_op jit(solution)/shard_map/ppermute | solution.py:310
  1508.6 65.3 %collective-permute-start.77 = (bf16[1024,1024]{1,0:T(8,128)(2,1)}, bf16[1024,1024]{1,0:T(8,128)(2,1)}, u32[]{:S(2)}, u32[]{:S(2)}) collective-permute-start(bf16[1024,1024]{1,0:T(8,128)(2,1)} %collective-permute-done.75.refs_5_), channel_id=1, source_target_pairs={{0,1},{1,0},{2,3},{3,2},{4,5},{5,4},{6,7},{7,6},{8,9},{9,8},{10,11... | collective-permute-start | bytes 6291464 | tf_op jit(solution)/shard_map/ppermute | solution.py:310
  (163 other events, 3024.1 us)
Sparse Core Ops, SparseCore 0:
  445.7 65.3 all-gather.14
  572.1 74.7 all-gather.12
  651.5 75.3 all-reduce.1
  996.9 74.1 all-gather.16
  1073.3 75.5 all-gather.18
  1151.0 74.6 all-gather.20
  1263.2 73.8 all-gather.22

commit v2 on v0

v2 whole, which is shorter than its diff:
```python
import functools

import jax
import jax.numpy as jnp
from jax import lax
from jax.experimental import pallas as pl
from jax.experimental.pallas import tpu as pltpu
from jax.sharding import PartitionSpec as P


LN_EPS = 1e-6
BATCH_AXES = ('rep', 'data')
NB = 8
HB = 512
NS = 4
LINKS = (1, 2, 4)
ADMIT = ((5, 1), (5, 0), (4, 1), (0, 0), (0, 1), (1, 0), (1, 1), (2, 0), (2, 1), (3, 0), (3, 1), (4, 0),)
GATHER_SC = ((0, 0), (4, 1), (5, 0), (5, 1),)
ORDER = tuple((t[0], int(t[1]), int(t[2])) for t in (
    'B50', 'a51', 'a50', 'B40', 'a41', 'B30', 'b51', 'b50', 'B20', 'c51', 'b41', 'B10',
    'd51', 'c50', 'c41', 'B00', 'a00', 'a01', 'a10', 'a11', 'a20', 'a21', 'd50', 'd41',
    'H00', 'U51', 'b00', 'b01', 'b10', 'b11', 'b20', 'b21', 'U50', 'a30', 'a31', 'a40',
    'c10', 'c00', 'c01', 'U41', 'c11', 'c20', 'c21', 'b30', 'b31', 'b40', 'd01', 'd00',
    'd10', 'd20', 'd11', 'd21', 'c40', 'c30', 'c31', 'e01', 'e10', 'e11', 'K00', 'd30',
    'd31', 'd40', 'e20', 'e21', 'f01', 'e30', 'f10', 'e31', 'e40', 'f11', 'f20', 'f21',
    'f40', 'h01', 'K01', 'h10', 'f30', 'f31', 'h11', 'K10', 'h20', 'K11', 'h21', 'h30',
    'K20', 'h31', 'K21', 'h40', 'K30', 'K31', 'K40', 'F41', 'F50', 'F51',
))


def layer_norm(residual):
    centered = residual - jnp.mean(residual, axis=-1, keepdims=True)
    inv_std = lax.rsqrt(jnp.mean(centered * centered, axis=-1, keepdims=True) + LN_EPS)
    return centered * inv_std, inv_std


def norm_back(normed, inv_std, grad_out):
    return inv_std * (grad_out - jnp.mean(grad_out, axis=-1, keepdims=True)
                      - normed * jnp.mean(grad_out * normed, axis=-1, keepdims=True))


def gelu(pre_act):
    return pre_act * (0.5 * (1.0 + lax.erf(pre_act * 0.7071067811865476)))


def gelu_parts(pre_act):
    gauss_cdf = 0.5 * (1.0 + lax.erf(pre_act * 0.7071067811865476))
    density = jnp.exp(-0.5 * pre_act * pre_act) * 0.3989422804014327
    return pre_act * gauss_cdf, gauss_cdf + pre_act * density


def pool_logits(residual, images, head_bf):
    pooled = jnp.mean(residual.reshape(images, -1, residual.shape[-1]), axis=1).astype(jnp.bfloat16)
    return pooled, jnp.dot(pooled, head_bf, preferred_element_type=jnp.float32)


def order_of(m):
    i = ADMIT.index(m) % 3
    return tuple(LINKS[(i + s) % 3] for s in range(3))


def unmask(block, order):
    return ((block // order[0]) % 2) * 4 + ((block // order[1]) % 2) * 2 + (block // order[2]) % 2


def flip(a, b):
    out = 0
    for v in (1, 2, 4):
        x, y = (a // v) % 2, (b // v) % 2
        out = out + (x + y - 2 * x * y) * v
    return out


def place():
    rep, data = lax.axis_index('rep'), lax.axis_index('data')
    return rep, data, rep * 2 + data // 2, data % 2


def dot(a, b, ca=1, cb=0):
    return lax.dot_general(a, b, (((ca,), (cb,)), ((), ())), preferred_element_type=jnp.float32)


def add_bf(a, b):
    return (a.astype(jnp.float32) + b.astype(jnp.float32)).astype(jnp.bfloat16)


ANY = pl.BlockSpec(memory_space=pl.ANY)
WHOLE = pl.BlockSpec(memory_space=pltpu.VMEM)
DMA = pltpu.SemaphoreType.DMA
F32, BF16 = jnp.float32, jnp.bfloat16


def back_body(l, last, order_up, order_down, v_ref, d_ref, r_ref, w1_ref, w2_ref, slope_ref, z_ref, *refs):
    up_s, up_k, down_s, down_k = refs[:4]
    refs = refs[4:]
    if not last:
        dn_ref, vn_ref = refs[:2]
        refs = refs[2:]
    (w1, w2, sl, zb, at_own, at_far, v_own, v_far, mine, far, got, acc,
     in_sem, out_sem, send_sem, recv_sem) = refs
    rep, data, chip, core = place()
    peer = (rep, data + 1 - 2 * core)
    barrier = pltpu.get_barrier_semaphore()

    def load(i, slot):
        cols = pl.ds(pl.multiple_of(i * HB, HB), HB)
        return (pltpu.make_async_copy(w2_ref.at[l, cols, :], w2.at[slot], in_sem.at[0, slot]),
                pltpu.make_async_copy(slope_ref.at[:, cols], sl.at[slot], in_sem.at[1, slot]),
                pltpu.make_async_copy(z_ref.at[:, cols], zb.at[slot], in_sem.at[2, slot]),
                pltpu.make_async_copy(w1_ref.at[l, :, cols], w1.at[slot], in_sem.at[3, slot]))

    def start(i, slot):
        for copy in load(i, slot):
            copy.start()

    def remote(i, k):
        return pltpu.make_async_remote_copy(
            src_ref=far.at[i % NS, k], dst_ref=got.at[i % NS, k],
            send_sem=send_sem.at[i % NS, k], recv_sem=recv_sem.at[i % NS, k],
            device_id=peer, device_id_type=pl.DeviceIdType.MESH)

    def stores(i):
        block = flip(i, chip)
        out = []
        for k, (os, ok, order) in enumerate(((up_s, up_k, order_up), (down_s, down_k, order_down))):
            pos = unmask(block, order)
            out.append((pos // 4, pltpu.make_async_copy(mine.at[i % NS, k], os.at[pos % 4], out_sem.at[i % NS, k]),
                        pltpu.make_async_copy(mine.at[i % NS, k], ok.at[pos % 4], out_sem.at[i % NS, k])))
        return out

    def finish(i):
        for k in (0, 1):
            remote(i, k).wait_recv()
            mine[i % NS, k] = add_bf(mine[i % NS, k], got[i % NS, k])
        for high, to_send, to_keep in stores(i):
            @pl.when(high == 1)
            def _():
                to_send.start()

            @pl.when(high == 0)
            def _():
                to_keep.start()

    def settle(i):
        for k in (0, 1):
            remote(i, k).wait_send()
        for high, to_send, to_keep in stores(i):
            @pl.when(high == 1)
            def _():
                to_send.wait()

            @pl.when(high == 0)
            def _():
                to_keep.wait()

    start(0, 0)
    start(1, 1)
    pl.semaphore_signal(barrier, inc=1, device_id=peer, device_id_type=pl.DeviceIdType.MESH)
    residual = r_ref[...]
    normed, inv_std = layer_norm(residual)
    a_t = normed.astype(BF16).T
    own, other = pl.ds(pl.multiple_of(core * HB, HB), HB), pl.ds(pl.multiple_of((1 - core) * HB, HB), HB)
    acc[...] = jnp.zeros_like(acc)
    at_own[...] = a_t[:HB]
    at_far[...] = a_t[HB:]
    v_own[...] = v_ref[:, own]
    v_far[...] = v_ref[:, other]

    @pl.when(core == 1)
    def _():
        tmp = at_own[...]
        at_own[...] = at_far[...]
        at_far[...] = tmp

    pl.semaphore_wait(barrier, 1)

    def step(i, _):
        slot = i % 3

        @pl.when(i + 2 < NB)
        def _():
            start(i + 2, (i + 2) % 3)

        @pl.when(i >= NS)
        def _():
            settle(i - NS)

        copies = load(i, slot)
        copies[0].wait()
        copies[1].wait()
        s = (dot(v_ref[...], w2[slot].astype(BF16), 1, 1) * sl[slot]).astype(BF16)
        far[i % NS, 0] = dot(at_far[...], s).astype(BF16)
        remote(i, 0).start()
        copies[2].wait()
        z_t = zb[slot].T
        far[i % NS, 1] = dot(z_t, v_far[...]).astype(BF16)
        remote(i, 1).start()
        mine[i % NS, 0] = dot(at_own[...], s).astype(BF16)
        mine[i % NS, 1] = dot(z_t, v_own[...]).astype(BF16)
        copies[3].wait()
        if not last:
            acc[...] += dot(s, w1[slot].astype(BF16), 1, 1)

        @pl.when(i > 0)
        def _():
            finish(i - 1)

        return 0

    lax.fori_loop(0, NB, step, 0)
    finish(NB - 1)
    if not last:
        residual = r_ref[...]
        normed, inv_std = layer_norm(residual)
        grad = d_ref[...] + norm_back(normed, inv_std, acc[...])
        dn_ref[...] = grad
        vn_ref[...] = grad.astype(BF16)

    for i in range(NB - NS, NB):
        settle(i)


def back(l, v, d, r, w_up, w_down, slope, z):
    rows, dim, hid = 512, 1024, 4096
    last = l == 0
    tile = jax.ShapeDtypeStruct((4, HB, HB), BF16)
    outs, specs = [tile] * 4, [ANY] * 4
    if not last:
        outs += [jax.ShapeDtypeStruct((rows, dim), F32), jax.ShapeDtypeStruct((rows, dim), BF16)]
        specs += [WHOLE, WHOLE]
    return pl.pallas_call(
        functools.partial(back_body, l, last, order_of((l, 0)), order_of((l, 1))),
        out_shape=outs, in_specs=[WHOLE, WHOLE, WHOLE, ANY, ANY, ANY, ANY], out_specs=specs,
        scratch_shapes=[pltpu.VMEM((3, dim, HB), F32), pltpu.VMEM((3, HB, dim), F32), pltpu.VMEM((3, rows, HB), F32),
                        pltpu.VMEM((3, rows, HB), BF16), pltpu.VMEM((HB, rows), BF16), pltpu.VMEM((HB, rows), BF16),
                        pltpu.VMEM((rows, HB), BF16), pltpu.VMEM((rows, HB), BF16),
                        pltpu.VMEM((NS, 2, HB, HB), BF16), pltpu.VMEM((NS, 2, HB, HB), BF16),
                        pltpu.VMEM((NS, 2, HB, HB), BF16), pltpu.VMEM((rows, dim), F32),
                        DMA((4, 3)), DMA((NS, 2)), DMA((NS, 2)), DMA((NS, 2))],
        compiler_params=pltpu.CompilerParams(collective_id=l, has_side_effects=True, vmem_limit_bytes=60 << 20),
        cost_estimate=pl.CostEstimate(flops=8 * rows * dim * hid, bytes_accessed=60 << 20, transcendentals=0),
        name='back')(v, d, r, w_up, w_down, slope, z)


def add_body(n, a_ref, b_ref, *refs):
    outs, (a, b, in_sem, out_sem) = refs[:-4], refs[-4:]
    order = list(range(n // 2, n)) + list(range(n // 2)) if n > 1 else [0]

    def copies(i):
        return (pltpu.make_async_copy(a_ref.at[i], a.at[i], in_sem.at[0, i]),
                pltpu.make_async_copy(b_ref.at[i], b.at[i], in_sem.at[1, i]))

    done = []
    for i in order:
        for c in copies(i):
            c.start()
    for i in order:
        for c in copies(i):
            c.wait()
        a[i] = add_bf(a[i], b[i])
        if n == 1:
            dst = outs[0].at[0]
        elif i >= n // 2:
            dst = outs[0].at[i - n // 2]
        else:
            dst = outs[1].at[i]
        c = pltpu.make_async_copy(a.at[i], dst, out_sem.at[i])
        c.start()
        done.append(c)
    for c in done:
        c.wait()


def add_halves(a, b):
    n = a.shape[0]
    out = jax.ShapeDtypeStruct((max(n // 2, 1), HB, HB), BF16)
    count = 2 if n > 1 else 1
    return pl.pallas_call(
        functools.partial(add_body, n), out_shape=[out] * count, in_specs=[ANY, ANY], out_specs=[ANY] * count,
        scratch_shapes=[pltpu.VMEM((n, HB, HB), BF16), pltpu.VMEM((n, HB, HB), BF16), DMA((2, n)), DMA((n,))],
        cost_estimate=pl.CostEstimate(flops=n << 29, bytes_accessed=3 * n << 19, transcendentals=0),
        name='add')(a, b)


def cat_body(a_ref, b_ref, o_ref, buf, in_sem, out_sem):
    n = a_ref.shape[0]
    loads = [pltpu.make_async_copy((a_ref if i < n else b_ref).at[i % n], buf.at[i], in_sem.at[i]) for i in range(2 * n)]
    stores = [pltpu.make_async_copy(buf.at[i], o_ref.at[i], out_sem.at[i]) for i in range(2 * n)]
    for c in loads:
        c.start()
    for c, d in zip(loads, stores):
        c.wait()
        d.start()
    for d in stores:
        d.wait()


def cat_halves(a, b):
    n = 2 * a.shape[0]
    return pl.pallas_call(
        cat_body, out_shape=jax.ShapeDtypeStruct((n, HB, HB), BF16), in_specs=[ANY, ANY], out_specs=ANY,
        scratch_shapes=[pltpu.VMEM((n, HB, HB), BF16), DMA((n,)), DMA((n,))],
        cost_estimate=pl.CostEstimate(flops=n << 29, bytes_accessed=2 * n << 19, transcendentals=0),
        name='cat')(a, b)


def fwd_body(l, r_ref, w1_ref, w2_ref, rn_ref, z_ref, slope_ref, w1, w2, act, zs, ss, in_sem, out_sem):
    def load(i):
        cols = pl.ds(pl.multiple_of(i * HB, HB), HB)
        return (pltpu.make_async_copy(w1_ref.at[l, :, cols], w1.at[i % 4], in_sem.at[0, i % 4]),
                pltpu.make_async_copy(w2_ref.at[l, cols, :], w2.at[i % 4], in_sem.at[1, i % 4]))

    def store(i):
        cols = pl.ds(pl.multiple_of(i * HB, HB), HB)
        return (pltpu.make_async_copy(zs.at[i % 3], z_ref.at[:, cols], out_sem.at[0, i % 3]),
                pltpu.make_async_copy(ss.at[i % 3], slope_ref.at[:, cols], out_sem.at[1, i % 3]))

    def first(i):
        hidden, slope = gelu_parts(dot(act[...], w1[i % 4].astype(BF16)))
        zs[i % 3] = hidden.astype(BF16)
        ss[i % 3] = slope

    def second(i):
        rn_ref[...] += dot(zs[i % 3], w2[i % 4].astype(BF16))

    for i in (0, 1, 2):
        for c in load(i):
            c.start()
    residual = r_ref[...]
    rn_ref[...] = residual
    act[...] = layer_norm(residual)[0].astype(BF16)
    load(0)[0].wait()
    first(0)
    for c in store(0):
        c.start()

    def step(i, _):
        load(i)[0].wait()
        load(i - 1)[1].wait()

        @pl.when(i >= 3)
        def _():
            for c in store(i - 3):
                c.wait()

        second(i - 1)
        first(i)
        for c in store(i):
            c.start()

        @pl.when(i + 2 < NB)
        def _():
            for c in load(i + 2):
                c.start()

        return 0

    lax.fori_loop(1, NB, step, 0)
    load(NB - 1)[1].wait()
    second(NB - 1)
    for i in range(NB - 3, NB):
        for c in store(i):
            c.wait()


def forward(l, r, w_up, w_down):
    rows, dim, hid = 512, 1024, 4096
    return pl.pallas_call(
        functools.partial(fwd_body, l),
        out_shape=[jax.ShapeDtypeStruct((rows, dim), F32), jax.ShapeDtypeStruct((rows, hid), BF16),
                   jax.ShapeDtypeStruct((rows, hid), F32)],
        in_specs=[WHOLE, ANY, ANY], out_specs=[WHOLE, ANY, ANY],
        scratch_shapes=[pltpu.VMEM((4, dim, HB), F32), pltpu.VMEM((4, HB, dim), F32), pltpu.VMEM((rows, dim), BF16),
                        pltpu.VMEM((3, rows, HB), BF16), pltpu.VMEM((3, rows, HB), F32), DMA((2, 4)), DMA((2, 3))],
        compiler_params=pltpu.CompilerParams(vmem_limit_bytes=48 << 20),
        cost_estimate=pl.CostEstimate(flops=4 * rows * dim * hid, bytes_accessed=46 << 20, transcendentals=0),
        name='forward')(r, w_up, w_down)


def update_body(l, k, kind, order, sc, into, rates_ref, *refs):
    acts = ()
    if kind == 'up':
        acts, refs = refs[:1], refs[1:]
    elif kind == 'down':
        acts, refs = refs[:2], refs[2:]
    pieces = 1 if sc else 4
    grads, refs = refs[:pieces], refs[pieces:]
    w_ref, m_ref = refs[:2]
    refs = refs[4:] if into else refs[2:]
    nw_ref, nm_ref, out_ref = refs[:3]
    w, m, g, ob, act, in_sem, g_sem, out_sem, ob_sem = refs[3:]
    _, _, chip, core = place()
    lr, mu = rates_ref[0], rates_ref[1]
    offs = (core * HB, (1 - core) * HB)

    def natural(i):
        cube = 0
        for s, v in enumerate(order):
            cube = cube + ((i // (4 >> s)) % 2) * v
        return flip(cube, chip)

    def at(i):
        span = pl.ds(pl.multiple_of(natural(i) * HB, HB), HB)
        return (l, slice(None), span) if k == 0 else (l, span, slice(None))

    def load(i, slot):
        out = [pltpu.make_async_copy(w_ref.at[at(i)], w.at[slot], in_sem.at[0, slot]),
               pltpu.make_async_copy(m_ref.at[at(i)], m.at[slot], in_sem.at[1, slot])]
        if kind == 'down':
            span = pl.ds(pl.multiple_of(natural(i) * HB, HB), HB)
            out.append(pltpu.make_async_copy(acts[1].at[:, span], act.at[slot], in_sem.at[2, slot]))
        return out

    def load_grad(i, slot, h, high):
        if sc:
            src = grads[0].at[natural(i) * 2 + (core if h == 0 else 1 - core)]
        else:
            src = grads[2 * h + high].at[i % 4]
        return pltpu.make_async_copy(src, g.at[slot, h], g_sem.at[slot, h])

    def start(i, slot):
        for c in load(i, slot):
            c.start()
        for h in (0, 1):
            if sc:
                load_grad(i, slot, h, 0).start()
                continue
            for high in (0, 1):
                @pl.when(i // 4 == high)
                def _():
                    load_grad(i, slot, h, high).start()

    def store(i, slot):
        return (pltpu.make_async_copy(w.at[slot], nw_ref.at[at(i)], out_sem.at[0, slot]),
                pltpu.make_async_copy(m.at[slot], nm_ref.at[at(i)], out_sem.at[1, slot]))

    def store_last(i):
        span = pl.ds(pl.multiple_of(natural(i) * HB, HB), HB)
        if kind == 'up':
            return pltpu.make_async_copy(ob.at[i % 2], out_ref.at[:, span], ob_sem.at[i % 2])
        dst = out_ref.at[:, span] if k == 0 else out_ref.at[span, :]
        return pltpu.make_async_copy(ob.at[i % 2], dst, ob_sem.at[i % 2])

    start(0, 0)
    start(1, 1)
    if kind == 'up':
        act[...] = layer_norm(acts[0][...])[0].astype(BF16)
    elif kind == 'down':
        out_ref[...] = acts[0][...]

    def step(i, _):
        slot = i % 4

        @pl.when(i + 2 < NB)
        def _():
            @pl.when(i >= 2)
            def _():
                for c in store(i - 2, (i + 2) % 4):
                    c.wait()

            start(i + 2, (i + 2) % 4)

        for c in load(i, slot):
            c.wait()
        for h in (0, 1):
            load_grad(i, slot, h, 0).wait()
            part = pl.ds(pl.multiple_of(offs[h], HB), HB)
            idx = (slot, part, slice(None)) if k == 0 else (slot, slice(None), part)
            new_m = mu * m[idx] + g[slot, h].astype(F32)
            m[idx] = new_m
            w[idx] = w[idx] - lr * new_m
        for c in store(i, slot):
            c.start()
        new_bf = w[slot].astype(BF16)
        if kind == 'down':
            out_ref[...] += dot(act[slot], new_bf)
        else:
            @pl.when(i >= 2)
            def _():
                store_last(i - 2).wait()

            if kind == 'up':
                ob[i % 2] = gelu(dot(act[...], new_bf)).astype(BF16)
            else:
                ob[i % 2] = new_bf
            store_last(i).start()
        return 0

    lax.fori_loop(0, NB, step, 0)
    for i in range(NB - 4, NB):
        for c in store(i, i % 4):
            c.wait()
    if kind != 'down':
        for i in range(NB - 2, NB):
            store_last(i).wait()


def update(m, kind, rates, acts, grads, w, mom, into):
    l, k = m
    dim, hid, rows = 1024, 4096, 512
    sc = len(grads) == 1
    wide = (dim, HB) if k == 0 else (HB, dim)
    if kind == 'up':
        act_specs, last, last_spec = [WHOLE], jax.ShapeDtypeStruct((rows, hid), BF16), ANY
        ob, act = (2, rows, HB), (rows, dim)
    elif kind == 'down':
        act_specs, last, last_spec = [WHOLE, ANY], jax.ShapeDtypeStruct((rows, dim), F32), WHOLE
        ob, act = (2, 16, 128), (4, rows, HB)
    else:
        act_specs, last_spec = [], ANY
        last = jax.ShapeDtypeStruct((dim, hid) if k == 0 else (hid, dim), BF16)
        ob, act = (2,) + wide, (16, 128)
    in_specs = [pl.BlockSpec(memory_space=pltpu.SMEM)] + act_specs + [ANY] * (len(grads) + 2)
    args = [rates, *acts, *grads, w, mom]
    aliases = {}
    if into is not None:
        aliases = {len(args): 0, len(args) + 1: 1}
        in_specs += [ANY, ANY]
        args += list(into)
    full = jax.ShapeDtypeStruct(w.shape, F32)
    return pl.pallas_call(
        functools.partial(update_body, l, k, kind, order_of(m), sc, into is not None),
        out_shape=[full, full, last], in_specs=in_specs, out_specs=[ANY, ANY, last_spec],
        scratch_shapes=[pltpu.VMEM((4,) + wide, F32), pltpu.VMEM((4,) + wide, F32), pltpu.VMEM((4, 2, HB, HB), BF16),
                        pltpu.VMEM(ob, BF16), pltpu.VMEM(act, BF16),
                        DMA((3, 4)), DMA((4, 2)), DMA((2, 4)), DMA((2,))],
        input_output_aliases=aliases,
        compiler_params=pltpu.CompilerParams(vmem_limit_bytes=48 << 20),
        cost_estimate=pl.CostEstimate(flops=10_000_000_000, bytes_accessed=80 << 20, transcendentals=0))(*args)


def solution(mesh):
    num_dev = mesh.shape['rep'] * mesh.shape['data']
    pairs = {v: [(i, i ^ max(2 * v, 1)) for i in range(num_dev)] for v in (0, 1, 2, 4)}

    def local_step(x_now, x_next, labels, w_up, w_down, w_head, mom_up, mom_down, mom_head, learn_rate, momentum):
        images, seq_len, model_dim = x_now.shape
        layers = w_up.shape[0]
        classes = w_head.shape[1]
        rows = images * seq_len
        global_batch = images * num_dev
        weights = (w_up, w_down)
        moms = (mom_up, mom_down)
        rates = jnp.stack([learn_rate, momentum])
        token = [None]

        def hold(*args):
            if token[0] is None:
                return args
            return lax.optimization_barrier((*args, token[0]))[:-1]

        def cp(x, link):
            return lax.ppermute(x, BATCH_AXES, pairs[link])

        residual = x_now.reshape(rows, model_dim).astype(F32)
        saved = []
        for l in range(layers):
            after, hid_bf, slope = forward(l, residual, w_up, w_down)
            saved.append((residual, slope, hid_bf))
            residual = after
        head_bf = w_head.astype(BF16)
        pooled, logits = pool_logits(residual, images, head_bf)
        soft_probs = jax.nn.softmax(logits, axis=-1)
        onehot = (labels[:, None] == jnp.arange(classes, dtype=jnp.int32)[None, :]).astype(F32)
        d_logits = ((soft_probs - onehot) / global_batch).astype(BF16)
        grad_head = jnp.einsum('bd,bc->dc', pooled, d_logits, preferred_element_type=F32)
        red_head = lax.psum(grad_head.astype(BF16), BATCH_AXES)
        d_pooled = jnp.einsum('bc,dc->bd', d_logits, head_bf, preferred_element_type=F32)
        d_resid = jnp.broadcast_to((d_pooled / seq_len)[:, None, :], (images, seq_len, model_dim)).reshape(rows, model_dim)

        d_res, v_bf = d_resid, d_resid.astype(BF16)
        box = {}
        new = [None, None]
        res_next = {0: x_next.reshape(rows, model_dim).astype(F32)}
        z_next = {}
        w_bf = {}

        def step(op, l, k):
            nonlocal d_res, v_bf
            m = (l, k)
            order = order_of(m)
            if op == 'B':
                v, d, r = hold(v_bf, d_res, saved[l][0])
                out = back(l, v, d, r, w_up, w_down, saved[l][1], saved[l][2])
                for j in (1, 0):
                    box['s1', (l, j)], box['k1', (l, j)] = out[2 * j], out[2 * j + 1]
                if l > 0:
                    d_res, v_bf = out[4:]
                out = out[3]
            elif op == 'a':
                send, = hold(box.pop(('s1', m)))
                box['r1', m] = cp(send, order[0])
                return
            elif op in 'bc':
                src, dst = {'b': ('1', '2'), 'c': ('2', '3')}[op]
                keep, got = hold(box.pop(('k' + src, m)), box.pop(('r' + src, m)))
                out, box['k' + dst, m] = add_halves(keep, got)
                box['r' + dst, m] = cp(out, order[1] if op == 'b' else order[2])
                out = box['k' + dst, m]
            elif op == 'd':
                keep, got = hold(box.pop(('k3', m)), box.pop(('r3', m)))
                out, = add_halves(keep, got)
                if m in GATHER_SC:
                    box['g', m] = (lax.all_gather(out, BATCH_AXES).reshape(num_dev, HB, HB),)
                else:
                    box['p0', m] = out
                    box['q0', m] = cp(out, order[2])
            elif op in 'ef':
                src, dst = {'e': ('0', '1'), 'f': ('1', '2')}[op]
                own, got = hold(box.pop(('p' + src, m)), box.pop(('q' + src, m)))
                out = cat_halves(own, got)
                if op == 'e':
                    box['p1', m] = out
                    box['q1', m] = cp(out, order[1])
                else:
                    far = cp(out, order[0])
                    box['g', m] = (out, far, cp(out, 0))
            elif op == 'h':
                own, far, other = box['g', m]
                send, = hold(far)
                box['g', m] = (own, far, other, cp(send, 0))
                return
            elif op in 'KU':
                kind = 'plain' if op == 'U' else ('up' if k == 0 else 'down')
                acts = ()
                if kind == 'up':
                    acts = (res_next[l],)
                elif kind == 'down':
                    acts = (res_next[l], z_next[l])
                held = hold(*acts, *box.pop(('g', m)))
                acts, grads = held[:len(acts)], held[len(acts):]
                nw, nm, out = update(m, kind, rates, acts, grads, weights[k], moms[k], new[k])
                new[k] = (nw, nm)
                if kind == 'up':
                    z_next[l] = out
                elif kind == 'down':
                    res_next[l + 1] = out
                else:
                    w_bf[m] = out
            elif op == 'F':
                if k == 0:
                    r, w = hold(res_next[l], w_bf[m])
                    out = gelu(jnp.dot(layer_norm(r)[0].astype(BF16), w, preferred_element_type=F32)).astype(BF16)
                    z_next[l] = out
                else:
                    r, z, w = hold(res_next[l], z_next[l], w_bf[m])
                    out = r + jnp.dot(z, w, preferred_element_type=F32)
                    res_next[l + 1] = out
            elif op == 'H':
                red, mh, wh = hold(red_head, mom_head, w_head)
                nm = momentum * mh + red.astype(F32)
                nw = wh - learn_rate * nm
                box['head'] = (nw, nm)
                out = nm
            token[0] = out

        for op, l, k in ORDER:
            step(op, l, k)
        new_head, new_mom_head = box['head']
        _, logits_next = pool_logits(res_next[layers], images, new_head.astype(jnp.bfloat16))
        return logits_next, new[0][0], new[1][0], new_head, new[0][1], new[1][1], new_mom_head

    batch_spec = P(BATCH_AXES)
    whole_spec = P()
    return jax.shard_map(local_step, mesh=mesh,
                         in_specs=(batch_spec, batch_spec, batch_spec) + (whole_spec,) * 8,
                         out_specs=(batch_spec,) + (whole_spec,) * 6,
                         check_vma=False)
```

time: 2530 us -> 1250 us (0.49)
  waiting for transfers between devices: 1580 us -> 333 us
  Pallas kernels: 0 us -> 767 us
  other arithmetic: 433 us -> 11.9 us
  matrix products: 397 us -> 23.6 us
  local copies, waits for them, and re-layouts: 94.4 us -> 14.9 us
  starting transfers between devices: 0.04 us -> 71.6 us
    psum x1, waiting for transfers between devices: 1580 us -> 0.01 us  [local_step(): red_head = lax.psum(grad_head.astype(BF16), BATCH_AXES)]
    pallas_call x0 -> x76, Pallas kernels: none -> 767 us  [the longest x12 328 us: update(): pl.pallas_call(functools.partial(update_body, l, k, kind, order_of(m), sc...]
    another operation x4 -> x1, other arithmetic: 412 us -> 0.07 us  [local_step(): rates = jnp.stack([learn_rate, momentum])]
    dot_general x42 -> x5, matrix products: 394 us -> 21.6 us  [the longest x2 11.1 us: step(): out = r + jnp.dot(z, w, preferred_element_type=F32)]
    ppermute x0 -> x76, waiting for transfers between devices: none -> 333 us  [cp(): return lax.ppermute(x, BATCH_AXES, pairs[link])]
    ppermute x0 -> x76, starting transfers between devices: none -> 71 us  [cp(): return lax.ppermute(x, BATCH_AXES, pairs[link])]
    unnamed x98 -> x90, local copies, waits for them, and re-layouts: 78.7 us -> 12.2 us
  transfers between devices with their start and end apart: 1 -> 81, of which waited for: 1 -> 19; matrix products, arithmetic and copies ran while one was open for 0% -> 1% of each run, Pallas kernels for 0% -> 48%
where the time goes in v2:
time: 1250 us; the launch traced here: 1240 us
  Pallas kernels  767 us (61%)
  waiting for transfers between devices  333 us (27%)
  starting transfers between devices  71.6 us (6%)
  matrix products  23.6 us (2%)
  between operations  17 us (1%)
  local copies, waits for them, and re-layouts  14.9 us (1%)
    ppermute x76, waiting for transfers between devices, cp(): return lax.ppermute(x, BATCH_AXES, pairs[link])  333 us
    pallas_call x12, Pallas kernels, update(): pl.pallas_call(functools.partial(update_body, l, k, kind, order_of(m), sc...  328 us
    pallas_call x6, Pallas kernels, back(): pl.pallas_call(functools.partial(back_body, l, last, order_of((l, 0)), or...  204 us
    pallas_call x6, Pallas kernels, forward(): pl.pallas_call(functools.partial(fwd_body, l), out_shape=[jax.ShapeDtypeS...  104 us
    pallas_call x36, Pallas kernels, add_halves(): pl.pallas_call(functools.partial(add_body, n), out_shape=[out] * count, i...  95.4 us
    ppermute x76, starting transfers between devices, cp(): return lax.ppermute(x, BATCH_AXES, pairs[link])  71 us
    pallas_call x16, Pallas kernels, cat_halves(): pl.pallas_call(cat_body, out_shape=jax.ShapeDtypeStruct((n, HB, HB), BF16...  36.3 us
  transfers between devices with their start and end apart: 81, of which 19 were waited for; matrix products, arithmetic and copies ran while one was open for 1% of the time, Pallas kernels for 48%

profile of v2, /device:TPU:0, one launch (start us, length us, event | category | flops | bytes accessed | tf_op | source)
XLA Modules:
  0.0 1239.6 jit_solution(11041220723296803018)
XLA Ops:
  8.7 17.3 %forward.6 = (f32[512,1024]{1,0:T(8,128)S(1)}, bf16[512,4096]{1,0:T(8,128)(2,1)}, f32[512,4096]{1,0:T(8,128)}) custom-call(f32[512,1024]{1,0:T(8,128)S(1)} %bitcast_convert_fusion.r_ref, f32[6,1024,4096]{2,1,0:T(8,128)} %refs_5_.7, f32[6,4096,1024]{2,1,0:T(8,128)} %refs_6_.14), custom_call_target="tpu_custom_call" | custom-call | flops 8589934592 | bytes 48234496 | tf_op jit(solution)/shard_map/forward/pallas_call | solution.py:368
  26.0 17.3 %forward.7 = (f32[512,1024]{1,0:T(8,128)S(1)}, bf16[512,4096]{1,0:T(8,128)(2,1)}, f32[512,4096]{1,0:T(8,128)}) custom-call(f32[512,1024]{1,0:T(8,128)S(1)} %get-tuple-element.399.r_ref, f32[6,1024,4096]{2,1,0:T(8,128)} %refs_5_.7, f32[6,4096,1024]{2,1,0:T(8,128)} %refs_6_.14), custom_call_target="tpu_custom_call" | custom-call | flops 8589934592 | bytes 48234496 | tf_op jit(solution)/shard_map/forward/pallas_call | solution.py:368
  43.4 17.3 %forward.8 = (f32[512,1024]{1,0:T(8,128)S(1)}, bf16[512,4096]{1,0:T(8,128)(2,1)}, f32[512,4096]{1,0:T(8,128)}) custom-call(f32[512,1024]{1,0:T(8,128)S(1)} %get-tuple-element.382.r_ref, f32[6,1024,4096]{2,1,0:T(8,128)} %refs_5_.7, f32[6,4096,1024]{2,1,0:T(8,128)} %refs_6_.14), custom_call_target="tpu_custom_call" | custom-call | flops 8589934592 | bytes 48234496 | tf_op jit(solution)/shard_map/forward/pallas_call | solution.py:368
  60.7 17.3 %forward.9 = (f32[512,1024]{1,0:T(8,128)S(1)}, bf16[512,4096]{1,0:T(8,128)(2,1)}, f32[512,4096]{1,0:T(8,128)}) custom-call(f32[512,1024]{1,0:T(8,128)S(1)} %get-tuple-element.363.r_ref, f32[6,1024,4096]{2,1,0:T(8,128)} %refs_5_.7, f32[6,4096,1024]{2,1,0:T(8,128)} %refs_6_.14), custom_call_target="tpu_custom_call" | custom-call | flops 8589934592 | bytes 48234496 | tf_op jit(solution)/shard_map/forward/pallas_call | solution.py:368
  78.1 17.4 %forward.10 = (f32[512,1024]{1,0:T(8,128)S(1)}, bf16[512,4096]{1,0:T(8,128)(2,1)}, f32[512,4096]{1,0:T(8,128)}) custom-call(f32[512,1024]{1,0:T(8,128)S(1)} %get-tuple-element.355.r_ref, f32[6,1024,4096]{2,1,0:T(8,128)} %refs_5_.7, f32[6,4096,1024]{2,1,0:T(8,128)} %refs_6_.14), custom_call_target="tpu_custom_call" | custom-call | flops 8589934592 | bytes 48234496 | tf_op jit(solution)/shard_map/forward/pallas_call | solution.py:368
  95.4 17.6 %forward.11 = (f32[512,1024]{1,0:T(8,128)S(1)}, bf16[512,4096]{1,0:T(8,128)(2,1)}, f32[512,4096]{1,0:T(8,128)}) custom-call(f32[512,1024]{1,0:T(8,128)S(1)} %get-tuple-element.346.r_ref, f32[6,1024,4096]{2,1,0:T(8,128)} %refs_5_.7, f32[6,4096,1024]{2,1,0:T(8,128)} %refs_6_.14), custom_call_target="tpu_custom_call" | custom-call | flops 8589934592 | bytes 48234496 | tf_op jit(solution)/shard_map/forward/pallas_call | solution.py:368
  117.5 35.8 %back.6 = (bf16[4,512,512]{2,1,0:T(8,128)(2,1)}, bf16[4,512,512]{2,1,0:T(8,128)(2,1)}, bf16[4,512,512]{2,1,0:T(8,128)(2,1)}, bf16[4,512,512]{2,1,0:T(8,128)(2,1)...) custom-call(bf16[512,1024]{1,0:T(8,128)(2,1)} %bitcast_convert_fusion.1.v_ref, f32[512,1024]{1,0:T(8,128)} %bitcast.21, ...), custom_call_target="tpu_custom_call" | custom-call | flops 17179869184 | bytes 62914560 | tf_op jit(solution)/shard_map/back/pallas_call | solution.py:231
  157.4 35.2 %back.7 = (bf16[4,512,512]{2,1,0:T(8,128)(2,1)}, bf16[4,512,512]{2,1,0:T(8,128)(2,1)}, bf16[4,512,512]{2,1,0:T(8,128)(2,1)}, bf16[4,512,512]{2,1,0:T(8,128)(2,1)...) custom-call(bf16[512,1024]{1,0:T(8,128)(2,1)} %get-tuple-element.353.v_ref, f32[512,1024]{1,0:T(8,128)} %get-tuple-element.354.d_ref, ...), custom_call_target="tpu_custom_call" | custom-call | flops 17179869184 | bytes 62914560 | tf_op jit(solution)/shard_map/back/pallas_call | solution.py:231
  196.5 35.7 %back.8 = (bf16[4,512,512]{2,1,0:T(8,128)(2,1)}, bf16[4,512,512]{2,1,0:T(8,128)(2,1)}, bf16[4,512,512]{2,1,0:T(8,128)(2,1)}, bf16[4,512,512]{2,1,0:T(8,128)(2,1)...) custom-call(bf16[512,1024]{1,0:T(8,128)(2,1)} %get-tuple-element.361.v_ref, f32[512,1024]{1,0:T(8,128)} %get-tuple-element.362.d_ref, ...), custom_call_target="tpu_custom_call" | custom-call | flops 17179869184 | bytes 62914560 | tf_op jit(solution)/shard_map/back/pallas_call | solution.py:231
  239.0 35.3 %back.9 = (bf16[4,512,512]{2,1,0:T(8,128)(2,1)}, bf16[4,512,512]{2,1,0:T(8,128)(2,1)}, bf16[4,512,512]{2,1,0:T(8,128)(2,1)}, bf16[4,512,512]{2,1,0:T(8,128)(2,1)...) custom-call(bf16[512,1024]{1,0:T(8,128)(2,1)} %get-tuple-element.380.v_ref, f32[512,1024]{1,0:T(8,128)} %get-tuple-element.381.d_ref, ...), custom_call_target="tpu_custom_call" | custom-call | flops 17179869184 | bytes 62914560 | tf_op jit(solution)/shard_map/back/pallas_call | solution.py:231
  282.0 35.4 %back.10 = (bf16[4,512,512]{2,1,0:T(8,128)(2,1)}, bf16[4,512,512]{2,1,0:T(8,128)(2,1)}, bf16[4,512,512]{2,1,0:T(8,128)(2,1)}, bf16[4,512,512]{2,1,0:T(8,128)(2,1...) custom-call(bf16[512,1024]{1,0:T(8,128)(2,1)} %get-tuple-element.397.v_ref, f32[512,1024]{1,0:T(8,128)} %get-tuple-element.398.d_ref, ...), custom_call_target="tpu_custom_call" | custom-call | flops 17179869184 | bytes 62914560 | tf_op jit(solution)/shard_map/back/pallas_call | solution.py:231
  323.0 34.5 %collective-permute-done.5.b_ref = bf16[2,512,512]{2,1,0:T(8,128)(2,1)} collective-permute-done((bf16[2,512,512]{2,1,0:T(8,128)(2,1)S(1)}, bf16[2,512,512]{2,1,0:T(8,128)(2,1)}, u32[]{:S(2)}, u32[]{:S(2)}) %collective-permute-start.5) | collective-permute-done | bytes 1048608 | tf_op jit(solution)/shard_map/ppermute | solution.py:553
  364.1 26.2 %back.11 = (bf16[4,512,512]{2,1,0:T(8,128)(2,1)}, bf16[4,512,512]{2,1,0:T(8,128)(2,1)}, bf16[4,512,512]{2,1,0:T(8,128)(2,1)}, bf16[4,512,512]{2,1,0:T(8,128)(2,1)}) custom-call(bf16[512,1024]{1,0:T(8,128)(2,1)} %get-tuple-element.416.v_ref, f32[512,1024]{1,0:T(8,128)} %get-tuple-element.417.d_ref, f32[512,1024]{1,0:T(8,128)} %copy-done, ...), custom_call_target="tpu_custom_call" | custom-call | flops 17179869184 | bytes 62914560 | tf_op jit(solution)/shard_map/back/pallas_call | solution.py:231
  422.5 67.5 %collective-permute-done.7.b_ref = bf16[4,512,512]{2,1,0:T(8,128)(2,1)} collective-permute-done((bf16[4,512,512]{2,1,0:T(8,128)(2,1)}, bf16[4,512,512]{2,1,0:T(8,128)(2,1)}, u32[]{:S(2)}, u32[]{:S(2)}) %collective-permute-start.7) | collective-permute-done | bytes 2097184 | tf_op jit(solution)/shard_map/ppermute | solution.py:553
  500.7 28.1 %shard_map.162 = (f32[6,4096,1024]{2,1,0:T(8,128)}, f32[6,4096,1024]{2,1,0:T(8,128)}, bf16[4096,1024]{1,0:T(8,128)(2,1)}) custom-call(f32[2]{0:T(128)S(1)} %pad_maximum_fusion.rates_ref, bf16[16,512,512]{2,1,0:T(8,128)(2,1)} %all-gather.9.cloned.1.call-done.refs_0_, f32[6,4096,1024]{2,1,0:T(8,128)} %refs_6_.14, f32[6,4096,1024]{2,1,0:T(8,128)} %refs_7_.7), custom_call_target="tpu_custom_call" | custom-call | flops 10000000000 | bytes 83886080 | tf_op jit(solution)/shard_map/pallas_call | solution.py:521
  538.7 18.3 %collective-permute-done.16.b_ref = bf16[4,512,512]{2,1,0:T(8,128)(2,1)} collective-permute-done((bf16[4,512,512]{2,1,0:T(8,128)(2,1)}, bf16[4,512,512]{2,1,0:T(8,128)(2,1)}, u32[]{:S(2)}, u32[]{:S(2)}) %collective-permute-start.16) | collective-permute-done | bytes 2097184 | tf_op jit(solution)/shard_map/ppermute | solution.py:553
  571.2 28.0 %shard_map.163 = (f32[6,1024,4096]{2,1,0:T(8,128)}, f32[6,1024,4096]{2,1,0:T(8,128)}, bf16[1024,4096]{1,0:T(8,128)(2,1)}) custom-call(f32[2]{0:T(128)S(1)} %pad_maximum_fusion.rates_ref, bf16[16,512,512]{2,1,0:T(8,128)(2,1)} %all-gather.11.cloned.1.call-done.refs_0_, f32[6,1024,4096]{2,1,0:T(8,128)} %refs_5_.7, f32[6,1024,4096]{2,1,0:T(8,128)} %refs_6_.15), custom_call_target="tpu_custom_call" | custom-call | flops 10000000000 | bytes 83886080 | tf_op jit(solution)/shard_map/pallas_call | solution.py:521
  614.2 28.6 %shard_map.164 = (f32[6,4096,1024]{2,1,0:T(8,128)}, f32[6,4096,1024]{2,1,0:T(8,128)}, bf16[4096,1024]{1,0:T(8,128)(2,1)}) custom-call(f32[2]{0:T(128)S(1)} %pad_maximum_fusion.rates_ref, bf16[16,512,512]{2,1,0:T(8,128)(2,1)} %all-gather.13.cloned.1.call-done.refs_0_, f32[6,4096,1024]{2,1,0:T(8,128)} %refs_6_.14, ...), custom_call_target="tpu_custom_call", output_to_operand_aliasing={{0}: (4, {}), {1}: (5, {})} | custom-call | flops 10000000000 | bytes 83886080 | tf_op jit(solution)/shard_map/pallas_call | solution.py:521
  645.2 25.0 %collective-permute-done.24.b_ref = bf16[2,512,512]{2,1,0:T(8,128)(2,1)} collective-permute-done((bf16[2,512,512]{2,1,0:T(8,128)(2,1)S(1)}, bf16[2,512,512]{2,1,0:T(8,128)(2,1)}, u32[]{:S(2)}, u32[]{:S(2)}) %collective-permute-start.24) | collective-permute-done | bytes 1048608 | tf_op jit(solution)/shard_map/ppermute | solution.py:553
  716.7 29.3 %collective-permute-done.26.b_ref = bf16[1,512,512]{2,1,0:T(8,128)(2,1)} collective-permute-done((bf16[1,512,512]{2,1,0:T(8,128)(2,1)}, bf16[1,512,512]{2,1,0:T(8,128)(2,1)}, u32[]{:S(2)}, u32[]{:S(2)}) %collective-permute-start.26) | collective-permute-done | bytes 524320 | tf_op jit(solution)/shard_map/ppermute | solution.py:553
  795.5 26.7 %shard_map.165 = (f32[6,1024,4096]{2,1,0:T(8,128)}, f32[6,1024,4096]{2,1,0:T(8,128)}, bf16[512,4096]{1,0:T(8,128)(2,1)}) custom-call(f32[2]{0:T(128)S(1)} %pad_maximum_fusion.rates_ref, f32[512,1024]{1,0:T(8,128)S(1)} %bitcast_convert_fusion.2.refs_0_, ...), custom_call_target="tpu_custom_call", output_to_operand_aliasing={{0}: (5, {}), {1}: (6, {})} | custom-call | flops 10000000000 | bytes 83886080 | tf_op jit(solution)/shard_map/pallas_call | solution.py:521
  851.0 35.2 %collective-permute-done.44.b_ref = bf16[1,512,512]{2,1,0:T(8,128)(2,1)} collective-permute-done((bf16[1,512,512]{2,1,0:T(8,128)(2,1)}, bf16[1,512,512]{2,1,0:T(8,128)(2,1)}, u32[]{:S(2)}, u32[]{:S(2)}) %collective-permute-start.44) | collective-permute-done | bytes 524320 | tf_op jit(solution)/shard_map/ppermute | solution.py:553
  913.3 26.8 %shard_map.166 = (f32[6,4096,1024]{2,1,0:T(8,128)}, f32[6,4096,1024]{2,1,0:T(8,128)}, f32[512,1024]{1,0:T(8,128)S(1)}) custom-call(f32[2]{0:T(128)S(1)} %pad_maximum_fusion.rates_ref, f32[512,1024]{1,0:T(8,128)S(1)} %bitcast_convert_fusion.2.refs_0_, bf16[512,4096]{1,0:T(8,128)(2,1)} %get-tuple-element.586.refs_1_, ...), custom_call_target="tpu_custom_call", output_to_operand_aliasing={{0}: (9, {}), {1}: (10, {})} | custom-call | flops 10000000000 | bytes 83886080 | tf_op jit(solution)/shard_map/pallas_call | solution.py:521
  958.3 20.1 %collective-permute-done.56.b_ref = bf16[2,512,512]{2,1,0:T(8,128)(2,1)} collective-permute-done((bf16[2,512,512]{2,1,0:T(8,128)(2,1)}, bf16[2,512,512]{2,1,0:T(8,128)(2,1)}, u32[]{:S(2)}, u32[]{:S(2)}) %collective-permute-start.56) | collective-permute-done | bytes 1048608 | tf_op jit(solution)/shard_map/ppermute | solution.py:553
  988.0 27.5 %shard_map.167 = (f32[6,1024,4096]{2,1,0:T(8,128)}, f32[6,1024,4096]{2,1,0:T(8,128)}, bf16[512,4096]{1,0:T(8,128)(2,1)}) custom-call(f32[2]{0:T(128)S(1)} %pad_maximum_fusion.rates_ref, f32[512,1024]{1,0:T(8,128)S(1)} %copy-done.2, bf16[4,512,512]{2,1,0:T(8,128)(2,1)S(1)} %copy-done.8, ...), custom_call_target="tpu_custom_call", output_to_operand_aliasing={{0}: (8, {}), {1}: (9, {})} | custom-call | flops 10000000000 | bytes 83886080 | tf_op jit(solution)/shard_map/pallas_call | solution.py:521
  1027.4 26.8 %shard_map.168 = (f32[6,4096,1024]{2,1,0:T(8,128)}, f32[6,4096,1024]{2,1,0:T(8,128)}, f32[512,1024]{1,0:T(8,128)S(1)}) custom-call(f32[2]{0:T(128)S(1)} %pad_maximum_fusion.rates_ref, f32[512,1024]{1,0:T(8,128)S(1)} %copy-done.2, bf16[512,4096]{1,0:T(8,128)(2,1)} %get-tuple-element.609.refs_1_, ...), custom_call_target="tpu_custom_call", output_to_operand_aliasing={{0}: (9, {}), {1}: (10, {})} | custom-call | flops 10000000000 | bytes 83886080 | tf_op jit(solution)/shard_map/pallas_call | solution.py:521
  1055.5 16.1 %collective-permute-done.67.refs_2_ = bf16[4,512,512]{2,1,0:T(8,128)(2,1)} collective-permute-done((bf16[4,512,512]{2,1,0:T(8,128)(2,1)}, bf16[4,512,512]{2,1,0:T(8,128)(2,1)}, u32[]{:S(2)}, u32[]{:S(2)}) %collective-permute-start.67) | collective-permute-done | bytes 2097184 | tf_op jit(solution)/shard_map/ppermute | solution.py:553
  1074.5 27.0 %shard_map.169 = (f32[6,1024,4096]{2,1,0:T(8,128)}, f32[6,1024,4096]{2,1,0:T(8,128)}, bf16[512,4096]{1,0:T(8,128)(2,1)}) custom-call(f32[2]{0:T(128)S(1)} %pad_maximum_fusion.rates_ref, f32[512,1024]{1,0:T(8,128)S(1)} %get-tuple-element.627.refs_0_, bf16[4,512,512]{2,1,0:T(8,128)(2,1)} %cat.27.refs_1_, ...), custom_call_target="tpu_custom_call", output_to_operand_aliasing={{0}: (8, {}), {1}: (9, {})} | custom-call | flops 10000000000 | bytes 83886080 | tf_op jit(solution)/shard_map/pallas_call | solution.py:521
  1102.9 26.8 %shard_map.170 = (f32[6,4096,1024]{2,1,0:T(8,128)}, f32[6,4096,1024]{2,1,0:T(8,128)}, f32[512,1024]{1,0:T(8,128)S(1)}) custom-call(f32[2]{0:T(128)S(1)} %pad_maximum_fusion.rates_ref, f32[512,1024]{1,0:T(8,128)S(1)} %get-tuple-element.627.refs_0_, bf16[512,4096]{1,0:T(8,128)(2,1)} %get-tuple-element.628.refs_1_, ...), custom_call_target="tpu_custom_call", output_to_operand_aliasing={{0}: (9, {}), {1}: (10, {})} | custom-call | flops 10000000000 | bytes 83886080 | tf_op jit(solution)/shard_map/pallas_call | solution.py:521
  1130.2 27.0 %shard_map.171 = (f32[6,1024,4096]{2,1,0:T(8,128)}, f32[6,1024,4096]{2,1,0:T(8,128)}, bf16[512,4096]{1,0:T(8,128)(2,1)}) custom-call(f32[2]{0:T(128)S(1)} %pad_maximum_fusion.rates_ref, f32[512,1024]{1,0:T(8,128)S(1)} %get-tuple-element.646.refs_0_, bf16[4,512,512]{2,1,0:T(8,128)(2,1)} %cat.30.refs_1_, ...), custom_call_target="tpu_custom_call", output_to_operand_aliasing={{0}: (8, {}), {1}: (9, {})} | custom-call | flops 10000000000 | bytes 83886080 | tf_op jit(solution)/shard_map/pallas_call | solution.py:521
  1157.3 26.8 %shard_map.172 = (f32[6,4096,1024]{2,1,0:T(8,128)}, f32[6,4096,1024]{2,1,0:T(8,128)}, f32[512,1024]{1,0:T(8,128)S(1)}) custom-call(f32[2]{0:T(128)S(1)} %pad_maximum_fusion.rates_ref, f32[512,1024]{1,0:T(8,128)S(1)} %get-tuple-element.646.refs_0_, bf16[512,4096]{1,0:T(8,128)(2,1)} %get-tuple-element.647.refs_1_, ...), custom_call_target="tpu_custom_call", output_to_operand_aliasing={{0}: (9, {}), {1}: (10, {})} | custom-call | flops 10000000000 | bytes 83886080 | tf_op jit(solution)/shard_map/pallas_call | solution.py:521
  1184.1 27.7 %shard_map.173 = (f32[6,1024,4096]{2,1,0:T(8,128)}, f32[6,1024,4096]{2,1,0:T(8,128)}, bf16[512,4096]{1,0:T(8,128)(2,1)}) custom-call(f32[2]{0:T(128)S(1)} %pad_maximum_fusion.rates_ref, f32[512,1024]{1,0:T(8,128)S(1)} %get-tuple-element.664.refs_0_, bf16[4,512,512]{2,1,0:T(8,128)(2,1)} %cat.29.refs_1_, ...), custom_call_target="tpu_custom_call", output_to_operand_aliasing={{0}: (8, {}), {1}: (9, {})} | custom-call | flops 10000000000 | bytes 83886080 | tf_op jit(solution)/shard_map/pallas_call | solution.py:521
  (320 shorter events, 340.6 us)
Async XLA Ops:
  7.2 415.3 %all-reduce.2.cloned.1.call-start = ((), (), s32[]{:S(2)}) async-start(), calls=%async_computation | async-start | bytes 4096000 | tf_op jit(solution)/shard_map/psum | solution.py:567
  153.3 78.9 %collective-permute-start.1 = (bf16[4,512,512]{2,1,0:T(8,128)(2,1)}, bf16[4,512,512]{2,1,0:T(8,128)(2,1)}, u32[]{:S(2)}, u32[]{:S(2)}) collective-permute-start(bf16[4,512,512]{2,1,0:T(8,128)(2,1)} %get-tuple-element.372), channel_id=1, source_target_pairs={{0,2},{1,3},{2,0},{3,1},{4,6},{5,7},{6,4},{7,5},{8,10},{9,11},{10,... | collective-permute-start | bytes 6291464 | tf_op jit(solution)/shard_map/ppermute | solution.py:553
  156.0 79.5 %collective-permute-start = (bf16[4,512,512]{2,1,0:T(8,128)(2,1)}, bf16[4,512,512]{2,1,0:T(8,128)(2,1)}, u32[]{:S(2)}, u32[]{:S(2)}) collective-permute-start(bf16[4,512,512]{2,1,0:T(8,128)(2,1)} %get-tuple-element.370), channel_id=1, source_target_pairs={{0,4},{1,5},{2,6},{3,7},{4,0},{5,1},{6,2},{7,3},{8,12},{9,13},{10,... | collective-permute-start | bytes 6291464 | tf_op jit(solution)/shard_map/ppermute | solution.py:553
  192.7 84.1 %collective-permute-start.2 = (bf16[4,512,512]{2,1,0:T(8,128)(2,1)}, bf16[4,512,512]{2,1,0:T(8,128)(2,1)S(1)}, u32[]{:S(2)}, u32[]{:S(2)}) collective-permute-start(bf16[4,512,512]{2,1,0:T(8,128)(2,1)} %get-tuple-element.388), channel_id=1, source_target_pairs={{0,8},{1,9},{2,10},{3,11},{4,12},{5,13},{6,14},{7,15},{8,0},{9,1},... | collective-permute-start | bytes 6291464 | tf_op jit(solution)/shard_map/ppermute | solution.py:553
  196.4 304.3 %all-gather.9.cloned.1.call-start = ((), (), s32[]{:S(2)}) async-start(), calls=%async_computation.1 | async-start | bytes 8912896 | tf_op jit(solution)/shard_map/all_gather | solution.py:604
  320.4 250.8 %all-gather.11.cloned.1.call-start = ((), (), s32[]{:S(2)}) async-start(), calls=%async_computation.2 | async-start | bytes 8912896 | tf_op jit(solution)/shard_map/all_gather | solution.py:604
  393.5 218.3 %all-gather.13.cloned.1.call-start = ((), (), s32[]{:S(2)}) async-start(), calls=%async_computation.3 | async-start | bytes 8912896 | tf_op jit(solution)/shard_map/all_gather | solution.py:604
  413.7 375.7 %all-gather.15.cloned.1.call-start = ((), (), s32[]{:S(2)}) async-start(), calls=%async_computation.4 | async-start | bytes 8912896 | tf_op jit(solution)/shard_map/all_gather | solution.py:604
  413.7 76.3 %collective-permute-start.7 = (bf16[4,512,512]{2,1,0:T(8,128)(2,1)}, bf16[4,512,512]{2,1,0:T(8,128)(2,1)}, u32[]{:S(2)}, u32[]{:S(2)}) collective-permute-start(bf16[4,512,512]{2,1,0:T(8,128)(2,1)} %get-tuple-element.424), channel_id=1, source_target_pairs={{0,2},{1,3},{2,0},{3,1},{4,6},{5,7},{6,4},{7,5},{8,10},{9,11},{10,... | collective-permute-start | bytes 6291464 | tf_op jit(solution)/shard_map/ppermute | solution.py:553
  417.4 114.6 %collective-permute-start.12 = (bf16[4,512,512]{2,1,0:T(8,128)(2,1)}, bf16[4,512,512]{2,1,0:T(8,128)(2,1)}, u32[]{:S(2)}, u32[]{:S(2)}) collective-permute-start(bf16[4,512,512]{2,1,0:T(8,128)(2,1)} %get-tuple-element.443), channel_id=1, source_target_pairs={{0,4},{1,5},{2,6},{3,7},{4,0},{5,1},{6,2},{7,3},{8,12},{9,13},{10,... | collective-permute-start | bytes 6291464 | tf_op jit(solution)/shard_map/ppermute | solution.py:553
  420.1 115.4 %collective-permute-start.11 = (bf16[4,512,512]{2,1,0:T(8,128)(2,1)}, bf16[4,512,512]{2,1,0:T(8,128)(2,1)}, u32[]{:S(2)}, u32[]{:S(2)}) collective-permute-start(bf16[4,512,512]{2,1,0:T(8,128)(2,1)} %get-tuple-element.441), channel_id=1, source_target_pairs={{0,8},{1,9},{2,10},{3,11},{4,12},{5,13},{6,14},{7,15},{8,0},{9,1},... | collective-permute-start | bytes 6291464 | tf_op jit(solution)/shard_map/ppermute | solution.py:553
  422.2 134.9 %collective-permute-start.16 = (bf16[4,512,512]{2,1,0:T(8,128)(2,1)}, bf16[4,512,512]{2,1,0:T(8,128)(2,1)}, u32[]{:S(2)}, u32[]{:S(2)}) collective-permute-start(bf16[4,512,512]{2,1,0:T(8,128)(2,1)} %get-tuple-element.457), channel_id=1, source_target_pairs={{0,2},{1,3},{2,0},{3,1},{4,6},{5,7},{6,4},{7,5},{8,10},{9,11},{10,... | collective-permute-start | bytes 6291464 | tf_op jit(solution)/shard_map/ppermute | solution.py:553
  422.2 138.0 %collective-permute-start.15 = (bf16[4,512,512]{2,1,0:T(8,128)(2,1)}, bf16[4,512,512]{2,1,0:T(8,128)(2,1)}, u32[]{:S(2)}, u32[]{:S(2)}) collective-permute-start(bf16[4,512,512]{2,1,0:T(8,128)(2,1)} %get-tuple-element.455), channel_id=1, source_target_pairs={{0,4},{1,5},{2,6},{3,7},{4,0},{5,1},{6,2},{7,3},{8,12},{9,13},{10,... | collective-permute-start | bytes 6291464 | tf_op jit(solution)/shard_map/ppermute | solution.py:553
  490.0 73.4 %collective-permute-start.14 = (bf16[4,512,512]{2,1,0:T(8,128)(2,1)S(1)}, bf16[4,512,512]{2,1,0:T(8,128)(2,1)}, u32[]{:S(2)}, u32[]{:S(2)}) collective-permute-start(bf16[4,512,512]{2,1,0:T(8,128)(2,1)S(1)} %copy-done.22), channel_id=1, source_target_pairs={{0,8},{1,9},{2,10},{3,11},{4,12},{5,13},{6,14},{7,15},{8,0},{9,1},... | collective-permute-start | bytes 6291464 | tf_op jit(solution)/shard_map/ppermute | solution.py:553
  599.2 77.4 %collective-permute-start.22 = (bf16[4,512,512]{2,1,0:T(8,128)(2,1)}, bf16[4,512,512]{2,1,0:T(8,128)(2,1)}, u32[]{:S(2)}, u32[]{:S(2)}) collective-permute-start(bf16[4,512,512]{2,1,0:T(8,128)(2,1)} %get-tuple-element.488), channel_id=1, source_target_pairs={{0,2},{1,3},{2,0},{3,1},{4,6},{5,7},{6,4},{7,5},{8,10},{9,11},{10,... | collective-permute-start | bytes 6291464 | tf_op jit(solution)/shard_map/ppermute | solution.py:553
  600.7 79.1 %collective-permute-start.21 = (bf16[4,512,512]{2,1,0:T(8,128)(2,1)}, bf16[4,512,512]{2,1,0:T(8,128)(2,1)}, u32[]{:S(2)}, u32[]{:S(2)}) collective-permute-start(bf16[4,512,512]{2,1,0:T(8,128)(2,1)} %get-tuple-element.485), channel_id=1, source_target_pairs={{0,4},{1,5},{2,6},{3,7},{4,0},{5,1},{6,2},{7,3},{8,12},{9,13},{10,... | collective-permute-start | bytes 6291464 | tf_op jit(solution)/shard_map/ppermute | solution.py:553
  602.1 80.9 %collective-permute-start.20 = (bf16[4,512,512]{2,1,0:T(8,128)(2,1)S(1)}, bf16[4,512,512]{2,1,0:T(8,128)(2,1)}, u32[]{:S(2)}, u32[]{:S(2)}) collective-permute-start(bf16[4,512,512]{2,1,0:T(8,128)(2,1)S(1)} %copy-done.21), channel_id=1, source_target_pairs={{0,8},{1,9},{2,10},{3,11},{4,12},{5,13},{6,14},{7,15},{8,0},{9,1},... | collective-permute-start | bytes 6291464 | tf_op jit(solution)/shard_map/ppermute | solution.py:553
  607.5 62.8 %collective-permute-start.24 = (bf16[2,512,512]{2,1,0:T(8,128)(2,1)S(1)}, bf16[2,512,512]{2,1,0:T(8,128)(2,1)}, u32[]{:S(2)}, u32[]{:S(2)}) collective-permute-start(bf16[2,512,512]{2,1,0:T(8,128)(2,1)S(1)} %copy-done.28), channel_id=1, source_target_pairs={{0,8},{1,9},{2,10},{3,11},{4,12},{5,13},{6,14},{7,15},{8,0},{9,1},... | collective-permute-start | bytes 3145736 | tf_op jit(solution)/shard_map/ppermute | solution.py:553
  612.8 60.0 %collective-permute-start.23 = (bf16[2,512,512]{2,1,0:T(8,128)(2,1)}, bf16[2,512,512]{2,1,0:T(8,128)(2,1)}, u32[]{:S(2)}, u32[]{:S(2)}) collective-permute-start(bf16[2,512,512]{2,1,0:T(8,128)(2,1)} %get-tuple-element.489), channel_id=1, source_target_pairs={{0,2},{1,3},{2,0},{3,1},{4,6},{5,7},{6,4},{7,5},{8,10},{9,11},{10,... | collective-permute-start | bytes 3145736 | tf_op jit(solution)/shard_map/ppermute | solution.py:553
  693.5 74.5 %collective-permute-start.34 = (bf16[2,512,512]{2,1,0:T(8,128)(2,1)S(1)}, bf16[2,512,512]{2,1,0:T(8,128)(2,1)}, u32[]{:S(2)}, u32[]{:S(2)}) collective-permute-start(bf16[2,512,512]{2,1,0:T(8,128)(2,1)S(1)} %copy-done.29), channel_id=1, source_target_pairs={{0,2},{1,3},{2,0},{3,1},{4,6},{5,7},{6,4},{7,5},{8,10},{9,11},{10,... | collective-permute-start | bytes 3145736 | tf_op jit(solution)/shard_map/ppermute | solution.py:553
  693.9 78.4 %collective-permute-start.33 = (bf16[2,512,512]{2,1,0:T(8,128)(2,1)S(1)}, bf16[2,512,512]{2,1,0:T(8,128)(2,1)}, u32[]{:S(2)}, u32[]{:S(2)}) collective-permute-start(bf16[2,512,512]{2,1,0:T(8,128)(2,1)S(1)} %copy-done.24), channel_id=1, source_target_pairs={{0,4},{1,5},{2,6},{3,7},{4,0},{5,1},{6,2},{7,3},{8,12},{9,13},{10,... | collective-permute-start | bytes 3145736 | tf_op jit(solution)/shard_map/ppermute | solution.py:553
  695.6 79.2 %collective-permute-start.32 = (bf16[2,512,512]{2,1,0:T(8,128)(2,1)S(1)}, bf16[2,512,512]{2,1,0:T(8,128)(2,1)}, u32[]{:S(2)}, u32[]{:S(2)}) collective-permute-start(bf16[2,512,512]{2,1,0:T(8,128)(2,1)S(1)} %copy-done.25), channel_id=1, source_target_pairs={{0,8},{1,9},{2,10},{3,11},{4,12},{5,13},{6,14},{7,15},{8,0},{9,1},... | collective-permute-start | bytes 3145736 | tf_op jit(solution)/shard_map/ppermute | solution.py:553
  837.5 69.9 %collective-permute-start.42 = (bf16[4,512,512]{2,1,0:T(8,128)(2,1)}, bf16[4,512,512]{2,1,0:T(8,128)(2,1)}, u32[]{:S(2)}, u32[]{:S(2)}) collective-permute-start(bf16[4,512,512]{2,1,0:T(8,128)(2,1)} %cat.21.refs_2_), channel_id=1, source_target_pairs={{0,4},{1,5},{2,6},{3,7},{4,0},{5,1},{6,2},{7,3},{8,12},{9,13},{10,... | collective-permute-start | bytes 6291464 | tf_op jit(solution)/shard_map/ppermute | solution.py:553
  840.5 57.0 %collective-permute-start.51 = (bf16[2,512,512]{2,1,0:T(8,128)(2,1)S(1)}, bf16[2,512,512]{2,1,0:T(8,128)(2,1)}, u32[]{:S(2)}, u32[]{:S(2)}) collective-permute-start(bf16[2,512,512]{2,1,0:T(8,128)(2,1)S(1)} %copy-done.27), channel_id=1, source_target_pairs={{0,4},{1,5},{2,6},{3,7},{4,0},{5,1},{6,2},{7,3},{8,12},{9,13},{10,... | collective-permute-start | bytes 3145736 | tf_op jit(solution)/shard_map/ppermute | solution.py:553
  909.6 74.8 %collective-permute-start.58 = (bf16[4,512,512]{2,1,0:T(8,128)(2,1)}, bf16[4,512,512]{2,1,0:T(8,128)(2,1)}, u32[]{:S(2)}, u32[]{:S(2)}) collective-permute-start(bf16[4,512,512]{2,1,0:T(8,128)(2,1)} %cat.26.refs_2_), channel_id=1, source_target_pairs={{0,2},{1,3},{2,0},{3,1},{4,6},{5,7},{6,4},{7,5},{8,10},{9,11},{10,... | collective-permute-start | bytes 6291464 | tf_op jit(solution)/shard_map/ppermute | solution.py:553
  911.0 67.3 %collective-permute-start.56 = (bf16[2,512,512]{2,1,0:T(8,128)(2,1)}, bf16[2,512,512]{2,1,0:T(8,128)(2,1)}, u32[]{:S(2)}, u32[]{:S(2)}) collective-permute-start(bf16[2,512,512]{2,1,0:T(8,128)(2,1)} %cat.24.a_ref), channel_id=1, source_target_pairs={{0,8},{1,9},{2,10},{3,11},{4,12},{5,13},{6,14},{7,15},{8,0},{9,1},... | collective-permute-start | bytes 3145736 | tf_op jit(solution)/shard_map/ppermute | solution.py:553
  912.0 72.5 %collective-permute-start.54 = (bf16[4,512,512]{2,1,0:T(8,128)(2,1)}, bf16[4,512,512]{2,1,0:T(8,128)(2,1)}, u32[]{:S(2)}, u32[]{:S(2)}) collective-permute-start(bf16[4,512,512]{2,1,0:T(8,128)(2,1)} %cat.23.refs_1_), channel_id=1, source_target_pairs={{0,1},{1,0},{2,3},{3,2},{4,5},{5,4},{6,7},{7,6},{8,9},{9,8},{10,11... | collective-permute-start | bytes 6291464 | tf_op jit(solution)/shard_map/ppermute | solution.py:553
  957.8 68.3 %collective-permute-start.59 = (bf16[4,512,512]{2,1,0:T(8,128)(2,1)}, bf16[4,512,512]{2,1,0:T(8,128)(2,1)}, u32[]{:S(2)}, u32[]{:S(2)}) collective-permute-start(bf16[4,512,512]{2,1,0:T(8,128)(2,1)} %cat.26.refs_2_), channel_id=1, source_target_pairs={{0,1},{1,0},{2,3},{3,2},{4,5},{5,4},{6,7},{7,6},{8,9},{9,8},{10,11... | collective-permute-start | bytes 6291464 | tf_op jit(solution)/shard_map/ppermute | solution.py:553
  984.5 69.7 %collective-permute-start.64 = (bf16[4,512,512]{2,1,0:T(8,128)(2,1)}, bf16[4,512,512]{2,1,0:T(8,128)(2,1)}, u32[]{:S(2)}, u32[]{:S(2)}) collective-permute-start(bf16[4,512,512]{2,1,0:T(8,128)(2,1)} %cat.28.refs_2_), channel_id=1, source_target_pairs={{0,8},{1,9},{2,10},{3,11},{4,12},{5,13},{6,14},{7,15},{8,0},{9,1},... | collective-permute-start | bytes 6291464 | tf_op jit(solution)/shard_map/ppermute | solution.py:553
  986.2 68.5 %collective-permute-start.62 = (bf16[4,512,512]{2,1,0:T(8,128)(2,1)}, bf16[4,512,512]{2,1,0:T(8,128)(2,1)}, u32[]{:S(2)}, u32[]{:S(2)}) collective-permute-start(bf16[4,512,512]{2,1,0:T(8,128)(2,1)} %cat.27.refs_1_), channel_id=1, source_target_pairs={{0,1},{1,0},{2,3},{3,2},{4,5},{5,4},{6,7},{7,6},{8,9},{9,8},{10,11... | collective-permute-start | bytes 6291464 | tf_op jit(solution)/shard_map/ppermute | solution.py:553
  1071.6 58.1 %collective-permute-start.73 = (bf16[4,512,512]{2,1,0:T(8,128)(2,1)}, bf16[4,512,512]{2,1,0:T(8,128)(2,1)}, u32[]{:S(2)}, u32[]{:S(2)}) collective-permute-start(bf16[4,512,512]{2,1,0:T(8,128)(2,1)} %cat.29.refs_1_), channel_id=1, source_target_pairs={{0,8},{1,9},{2,10},{3,11},{4,12},{5,13},{6,14},{7,15},{8,0},{9,1},... | collective-permute-start | bytes 6291464 | tf_op jit(solution)/shard_map/ppermute | solution.py:553
  1073.2 57.0 %collective-permute-start.69 = (bf16[4,512,512]{2,1,0:T(8,128)(2,1)}, bf16[4,512,512]{2,1,0:T(8,128)(2,1)}, u32[]{:S(2)}, u32[]{:S(2)}) collective-permute-start(bf16[4,512,512]{2,1,0:T(8,128)(2,1)} %collective-permute-done.67.refs_2_), channel_id=1, source_target_pairs={{0,1},{1,0},{2,3},{3,2},{4,5},{5,4},{6,7},{7,6},{8,9},{9,8},{10,11... | collective-permute-start | bytes 6291464 | tf_op jit(solution)/shard_map/ppermute | solution.py:553
  (94 other events, 2245.3 us)
Sparse Core Ops, SparseCore 0:
  196.6 75.8 all-reduce.1
  320.5 68.9 all-gather.8
  393.6 77.8 all-gather.10
  473.6 75.4 all-gather.12
  691.6 74.1 all-gather.14

commit v3 on v2

--- a/solution.py
+++ b/solution.py
@@ -14,17 +14,18 @@
 HB = 512
 NS = 4
 LINKS = (1, 2, 4)
-ADMIT = ((5, 1), (5, 0), (4, 1), (0, 0), (0, 1), (1, 0), (1, 1), (2, 0), (2, 1), (3, 0), (3, 1), (4, 0),)
-GATHER_SC = ((0, 0), (4, 1), (5, 0), (5, 1),)
+ADMIT = ((5, 1), (5, 0), (4, 1), (3, 1), (4, 0), (1, 0), (2, 0), (1, 1), (0, 0), (0, 1), (2, 1), (3, 0),)
+GATHER_SC = ((0, 0), (0, 1), (2, 1), (3, 0),)
 ORDER = tuple((t[0], int(t[1]), int(t[2])) for t in (
-    'B50', 'a51', 'a50', 'B40', 'a41', 'B30', 'b51', 'b50', 'B20', 'c51', 'b41', 'B10',
-    'd51', 'c50', 'c41', 'B00', 'a00', 'a01', 'a10', 'a11', 'a20', 'a21', 'd50', 'd41',
-    'H00', 'U51', 'b00', 'b01', 'b10', 'b11', 'b20', 'b21', 'U50', 'a30', 'a31', 'a40',
-    'c10', 'c00', 'c01', 'U41', 'c11', 'c20', 'c21', 'b30', 'b31', 'b40', 'd01', 'd00',
-    'd10', 'd20', 'd11', 'd21', 'c40', 'c30', 'c31', 'e01', 'e10', 'e11', 'K00', 'd30',
-    'd31', 'd40', 'e20', 'e21', 'f01', 'e30', 'f10', 'e31', 'e40', 'f11', 'f20', 'f21',
-    'f40', 'h01', 'K01', 'h10', 'f30', 'f31', 'h11', 'K10', 'h20', 'K11', 'h21', 'h30',
-    'K20', 'h31', 'K21', 'h40', 'K30', 'K31', 'K40', 'F41', 'F50', 'F51',
+    'B50', 'a51', 'a50', 'B40', 'a41', 'B30', 'a31', 'a40', 'b50', 'b51', 'B20', 'b41',
+    'c50', 'b31', 'b40', 'B10', 'c51', 'd50', 'a10', 'c41', 'c31', 'c40', 'd51', 'a20',
+    'e50', 'd41', 'a11', 'B00', 'd40', 'a00', 'e41', 'b10', 'H00', 'b20', 'd31', 'a01',
+    'e51', 'e40', 'b11', 'f50', 'f41', 'c20', 'c10', 'f51', 'b00', 'e31', 'b01', 'h50',
+    'f40', 'd10', 'a21', 'U50', 'c11', 'h51', 'f31', 'U51', 'c01', 'd11', 'a30', 'd20',
+    'c00', 'h41', 'd01', 'h40', 'U41', 'h31', 'e10', 'U40', 'b30', 'e20', 'b21', 'e11',
+    'd00', 'U31', 'f10', 'c30', 'c21', 'U01', 'f20', 'f11', 'd21', 'K00', 'd30', 'F01',
+    'h20', 'h10', 'h11', 'K10', 'K11', 'K20', 'K21', 'K30', 'F31', 'F40', 'F41', 'F50',
+    'F51',
 ))
 
 
@@ -90,14 +91,14 @@
 F32, BF16 = jnp.float32, jnp.bfloat16
 
 
-def back_body(l, last, order_up, order_down, v_ref, d_ref, r_ref, w1_ref, w2_ref, slope_ref, z_ref, *refs):
+def back_body(l, last, order_up, order_down, v_hbm, d_hbm, r_hbm, w1_ref, w2_ref, slope_ref, z_ref, *refs):
     up_s, up_k, down_s, down_k = refs[:4]
     refs = refs[4:]
     if not last:
-        dn_ref, vn_ref = refs[:2]
+        dn_hbm, vn_hbm = refs[:2]
         refs = refs[2:]
-    (w1, w2, sl, zb, at_own, at_far, v_own, v_far, mine, far, got, acc,
-     in_sem, out_sem, send_sem, recv_sem) = refs
+    (w1, w2, sl, zb, v_ref, d_ref, r_ref, at_own, at_far, v_own, v_far, mine, far, got, acc,
+     in_sem, one_sem, out_sem, send_sem, recv_sem) = refs
     rep, data, chip, core = place()
     peer = (rep, data + 1 - 2 * core)
     barrier = pltpu.get_barrier_semaphore()
@@ -105,8 +106,8 @@
     def load(i, slot):
         cols = pl.ds(pl.multiple_of(i * HB, HB), HB)
         return (pltpu.make_async_copy(w2_ref.at[l, cols, :], w2.at[slot], in_sem.at[0, slot]),
-                pltpu.make_async_copy(slope_ref.at[:, cols], sl.at[slot], in_sem.at[1, slot]),
-                pltpu.make_async_copy(z_ref.at[:, cols], zb.at[slot], in_sem.at[2, slot]),
+                pltpu.make_async_copy(slope_ref.at[l, :, cols], sl.at[slot], in_sem.at[1, slot]),
+                pltpu.make_async_copy(z_ref.at[l, :, cols], zb.at[slot], in_sem.at[2, slot]),
                 pltpu.make_async_copy(w1_ref.at[l, :, cols], w1.at[slot], in_sem.at[3, slot]))
 
     def start(i, slot):
@@ -153,9 +154,17 @@
             def _():
                 to_keep.wait()
 
+    pl.semaphore_signal(barrier, inc=1, device_id=peer, device_id_type=pl.DeviceIdType.MESH)
+    get_v = pltpu.make_async_copy(v_hbm, v_ref, one_sem.at[0])
+    get_r = pltpu.make_async_copy(r_hbm.at[l], r_ref, one_sem.at[1])
+    get_r.start()
+    get_v.start()
     start(0, 0)
     start(1, 1)
-    pl.semaphore_signal(barrier, inc=1, device_id=peer, device_id_type=pl.DeviceIdType.MESH)
+    if not last:
+        get_d = pltpu.make_async_copy(d_hbm, d_ref, one_sem.at[2])
+        get_d.start()
+    get_r.wait()
     residual = r_ref[...]
     normed, inv_std = layer_norm(residual)
     a_t = normed.astype(BF16).T
@@ -163,6 +172,7 @@
     acc[...] = jnp.zeros_like(acc)
     at_own[...] = a_t[:HB]
     at_far[...] = a_t[HB:]
+    get_v.wait()
     v_own[...] = v_ref[:, own]
     v_far[...] = v_ref[:, other]
 
@@ -208,16 +218,23 @@
         return 0
 
     lax.fori_loop(0, NB, step, 0)
-    finish(NB - 1)
     if not last:
+        get_d.wait()
         residual = r_ref[...]
         normed, inv_std = layer_norm(residual)
         grad = d_ref[...] + norm_back(normed, inv_std, acc[...])
-        dn_ref[...] = grad
-        vn_ref[...] = grad.astype(BF16)
-
+        d_ref[...] = grad
+        v_ref[...] = grad.astype(BF16)
+        put_d = pltpu.make_async_copy(d_ref, dn_hbm, one_sem.at[2])
+        put_v = pltpu.make_async_copy(v_ref, vn_hbm, one_sem.at[0])
+        put_d.start()
+        put_v.start()
+    finish(NB - 1)
     for i in range(NB - NS, NB):
         settle(i)
+    if not last:
+        put_d.wait()
+        put_v.wait()
 
 
 def back(l, v, d, r, w_up, w_down, slope, z):
@@ -227,16 +244,17 @@
     outs, specs = [tile] * 4, [ANY] * 4
     if not last:
         outs += [jax.ShapeDtypeStruct((rows, dim), F32), jax.ShapeDtypeStruct((rows, dim), BF16)]
-        specs += [WHOLE, WHOLE]
+        specs += [ANY, ANY]
     return pl.pallas_call(
         functools.partial(back_body, l, last, order_of((l, 0)), order_of((l, 1))),
-        out_shape=outs, in_specs=[WHOLE, WHOLE, WHOLE, ANY, ANY, ANY, ANY], out_specs=specs,
+        out_shape=outs, in_specs=[ANY] * 7, out_specs=specs,
         scratch_shapes=[pltpu.VMEM((3, dim, HB), F32), pltpu.VMEM((3, HB, dim), F32), pltpu.VMEM((3, rows, HB), F32),
-                        pltpu.VMEM((3, rows, HB), BF16), pltpu.VMEM((HB, rows), BF16), pltpu.VMEM((HB, rows), BF16),
+                        pltpu.VMEM((3, rows, HB), BF16), pltpu.VMEM((rows, dim), BF16), pltpu.VMEM((rows, dim), F32),
+                        pltpu.VMEM((rows, dim), F32), pltpu.VMEM((HB, rows), BF16), pltpu.VMEM((HB, rows), BF16),
                         pltpu.VMEM((rows, HB), BF16), pltpu.VMEM((rows, HB), BF16),
                         pltpu.VMEM((NS, 2, HB, HB), BF16), pltpu.VMEM((NS, 2, HB, HB), BF16),
                         pltpu.VMEM((NS, 2, HB, HB), BF16), pltpu.VMEM((rows, dim), F32),
-                        DMA((4, 3)), DMA((NS, 2)), DMA((NS, 2)), DMA((NS, 2))],
+                        DMA((4, 3)), DMA((3,)), DMA((NS, 2)), DMA((NS, 2)), DMA((NS, 2))],
         compiler_params=pltpu.CompilerParams(collective_id=l, has_side_effects=True, vmem_limit_bytes=60 << 20),
         cost_estimate=pl.CostEstimate(flops=8 * rows * dim * hid, bytes_accessed=60 << 20, transcendentals=0),
         name='back')(v, d, r, w_up, w_down, slope, z)
@@ -304,77 +322,112 @@
         name='cat')(a, b)
 
 
-def fwd_body(l, r_ref, w1_ref, w2_ref, rn_ref, z_ref, slope_ref, w1, w2, act, zs, ss, in_sem, out_sem):
-    def load(i):
-        cols = pl.ds(pl.multiple_of(i * HB, HB), HB)
-        return (pltpu.make_async_copy(w1_ref.at[l, :, cols], w1.at[i % 4], in_sem.at[0, i % 4]),
-                pltpu.make_async_copy(w2_ref.at[l, cols, :], w2.at[i % 4], in_sem.at[1, i % 4]))
-
-    def store(i):
-        cols = pl.ds(pl.multiple_of(i * HB, HB), HB)
-        return (pltpu.make_async_copy(zs.at[i % 3], z_ref.at[:, cols], out_sem.at[0, i % 3]),
-                pltpu.make_async_copy(ss.at[i % 3], slope_ref.at[:, cols], out_sem.at[1, i % 3]))
-
-    def first(i):
-        hidden, slope = gelu_parts(dot(act[...], w1[i % 4].astype(BF16)))
-        zs[i % 3] = hidden.astype(BF16)
-        ss[i % 3] = slope
-
-    def second(i):
-        rn_ref[...] += dot(zs[i % 3], w2[i % 4].astype(BF16))
-
-    for i in (0, 1, 2):
-        for c in load(i):
+def fwd_body(layers, x_ref, w1_ref, w2_ref, rs_ref, z_ref, slope_ref, w1, w2, res, keep, act, zs, ss, in_sem, out_sem, res_sem):
+    total = layers * NB
+
+    def load(t):
+        l, cols = t // NB, pl.ds(pl.multiple_of((t % NB) * HB, HB), HB)
+        return (pltpu.make_async_copy(w1_ref.at[l, :, cols], w1.at[t % 4], in_sem.at[0, t % 4]),
+                pltpu.make_async_copy(w2_ref.at[l, cols, :], w2.at[t % 4], in_sem.at[1, t % 4]))
+
+    def store(t):
+        l, cols = t // NB, pl.ds(pl.multiple_of((t % NB) * HB, HB), HB)
+        return (pltpu.make_async_copy(zs.at[t % 3], z_ref.at[l, :, cols], out_sem.at[0, t % 3]),
+                pltpu.make_async_copy(ss.at[t % 3], slope_ref.at[l, :, cols], out_sem.at[1, t % 3]))
+
+    def store_res(l):
+        return pltpu.make_async_copy(keep.at[l % 2], rs_ref.at[l], res_sem.at[l % 2])
+
+    def prefetch(t):
+        @pl.when(t < total)
+        def _():
+            for c in load(t):
+                c.start()
+
+    def first(t):
+        @pl.when(t >= 3)
+        def _():
+            for c in store(t - 3):
+                c.wait()
+
+        hidden, slope = gelu_parts(dot(act[...], w1[t % 4].astype(BF16)))
+        zs[t % 3] = hidden.astype(BF16)
+        ss[t % 3] = slope
+        for c in store(t):
             c.start()
-    residual = r_ref[...]
-    rn_ref[...] = residual
-    act[...] = layer_norm(residual)[0].astype(BF16)
-    load(0)[0].wait()
-    first(0)
-    for c in store(0):
-        c.start()
-
-    def step(i, _):
-        load(i)[0].wait()
-        load(i - 1)[1].wait()
-
-        @pl.when(i >= 3)
+
+    def second(t):
+        res[...] += dot(zs[t % 3], w2[t % 4].astype(BF16))
+
+    for t in (0, 1, 2):
+        for c in load(t):
+            c.start()
+    res[...] = x_ref[...].astype(F32)
+
+    def block(l, _):
+        t0 = l * NB
+
+        @pl.when(l >= 2)
         def _():
-            for c in store(i - 3):
-                c.wait()
-
-        second(i - 1)
-        first(i)
-        for c in store(i):
-            c.start()
-
-        @pl.when(i + 2 < NB)
-        def _():
-            for c in load(i + 2):
+            store_res(l - 2).wait()
+
+        residual = res[...]
+        keep[l % 2] = residual
+        store_res(l).start()
+        act[...] = layer_norm(residual)[0].astype(BF16)
+        load(t0)[0].wait()
+        first(t0)
+
+        def step(i, _):
+            t = t0 + i
+            prefetch(t + 2)
+            load(t)[0].wait()
+            load(t - 1)[1].wait()
+
+            @pl.when(t >= 3)
+            def _():
+                for c in store(t - 3):
+                    c.wait()
+
+            res[...] += dot(zs[(t - 1) % 3], w2[(t - 1) % 4].astype(BF16))
+            hidden, slope = gelu_parts(dot(act[...], w1[t % 4].astype(BF16)))
+            zs[t % 3] = hidden.astype(BF16)
+            ss[t % 3] = slope
+            for c in store(t):
                 c.start()
-
+            return 0
+
+        lax.fori_loop(1, NB, step, 0)
+        load(t0 + NB - 1)[1].wait()
+        second(t0 + NB - 1)
+        prefetch(t0 + NB + 2)
         return 0
 
-    lax.fori_loop(1, NB, step, 0)
-    load(NB - 1)[1].wait()
-    second(NB - 1)
-    for i in range(NB - 3, NB):
-        for c in store(i):
+    lax.fori_loop(0, layers, block, 0)
+
+    store_res(layers - 2).wait()
+    keep[layers % 2] = res[...]
+    store_res(layers).start()
+    for t in range(total - 3, total):
+        for c in store(t):
             c.wait()
-
-
-def forward(l, r, w_up, w_down):
-    rows, dim, hid = 512, 1024, 4096
+    for l in (layers - 1, layers):
+        store_res(l).wait()
+
+
+def forward(x, w_up, w_down):
+    rows, dim, hid, layers = 512, 1024, 4096, 6
     return pl.pallas_call(
-        functools.partial(fwd_body, l),
-        out_shape=[jax.ShapeDtypeStruct((rows, dim), F32), jax.ShapeDtypeStruct((rows, hid), BF16),
-                   jax.ShapeDtypeStruct((rows, hid), F32)],
-        in_specs=[WHOLE, ANY, ANY], out_specs=[WHOLE, ANY, ANY],
-        scratch_shapes=[pltpu.VMEM((4, dim, HB), F32), pltpu.VMEM((4, HB, dim), F32), pltpu.VMEM((rows, dim), BF16),
-                        pltpu.VMEM((3, rows, HB), BF16), pltpu.VMEM((3, rows, HB), F32), DMA((2, 4)), DMA((2, 3))],
-        compiler_params=pltpu.CompilerParams(vmem_limit_bytes=48 << 20),
-        cost_estimate=pl.CostEstimate(flops=4 * rows * dim * hid, bytes_accessed=46 << 20, transcendentals=0),
-        name='forward')(r, w_up, w_down)
+        functools.partial(fwd_body, layers),
+        out_shape=[jax.ShapeDtypeStruct((layers + 1, rows, dim), F32), jax.ShapeDtypeStruct((layers, rows, hid), BF16),
+                   jax.ShapeDtypeStruct((layers, rows, hid), F32)],
+        in_specs=[WHOLE, ANY, ANY], out_specs=[ANY, ANY, ANY],
+        scratch_shapes=[pltpu.VMEM((4, dim, HB), F32), pltpu.VMEM((4, HB, dim), F32), pltpu.VMEM((rows, dim), F32),
+                        pltpu.VMEM((2, rows, dim), F32), pltpu.VMEM((rows, dim), BF16), pltpu.VMEM((3, rows, HB), BF16),
+                        pltpu.VMEM((3, rows, HB), F32), DMA((2, 4)), DMA((2, 3)), DMA((2,))],
+        compiler_params=pltpu.CompilerParams(vmem_limit_bytes=50 << 20),
+        cost_estimate=pl.CostEstimate(flops=24 * rows * dim * hid, bytes_accessed=280 << 20, transcendentals=0),
+        name='forward')(x, w_up, w_down)
 
 
 def update_body(l, k, kind, order, sc, into, rates_ref, *refs):
@@ -388,10 +441,11 @@
     w_ref, m_ref = refs[:2]
     refs = refs[4:] if into else refs[2:]
     nw_ref, nm_ref, out_ref = refs[:3]
-    w, m, g, ob, act, in_sem, g_sem, out_sem, ob_sem = refs[3:]
+    w, m, g, ob, act, in_sem, act_sem, out_sem, ob_sem = refs[3:]
     _, _, chip, core = place()
     lr, mu = rates_ref[0], rates_ref[1]
-    offs = (core * HB, (1 - core) * HB)
+    sides = [pl.ds(pl.multiple_of(core * HB, HB), HB), pl.ds(pl.multiple_of((1 - core) * HB, HB), HB)]
+    slots = 6
 
     def natural(i):
         cube = 0
@@ -399,117 +453,134 @@
             cube = cube + ((i // (4 >> s)) % 2) * v
         return flip(cube, chip)
 
-    def at(i):
-        span = pl.ds(pl.multiple_of(natural(i) * HB, HB), HB)
-        return (l, slice(None), span) if k == 0 else (l, span, slice(None))
-
-    def load(i, slot):
-        out = [pltpu.make_async_copy(w_ref.at[at(i)], w.at[slot], in_sem.at[0, slot]),
-               pltpu.make_async_copy(m_ref.at[at(i)], m.at[slot], in_sem.at[1, slot])]
-        if kind == 'down':
-            span = pl.ds(pl.multiple_of(natural(i) * HB, HB), HB)
-            out.append(pltpu.make_async_copy(acts[1].at[:, span], act.at[slot], in_sem.at[2, slot]))
-        return out
-
-    def load_grad(i, slot, h, high):
+    def span(i):
+        return pl.ds(pl.multiple_of(natural(i) * HB, HB), HB)
+
+    def at(i, h):
+        return (l, sides[h], span(i)) if k == 0 else (l, span(i), sides[h])
+
+    def load(i, h):
+        slot = (2 * i + h) % slots
+        return (pltpu.make_async_copy(w_ref.at[at(i, h)], w.at[slot], in_sem.at[0, slot]),
+                pltpu.make_async_copy(m_ref.at[at(i, h)], m.at[slot], in_sem.at[1, slot]))
+
+    def load_act(i):
+        return pltpu.make_async_copy(acts[1].at[:, span(i)], act.at[i % 3], act_sem.at[i % 3])
+
+    def load_grad(i, h, high):
+        slot = (2 * i + h) % slots
+        src = grads[0].at[natural(i) * 2 + (core if h == 0 else 1 - core)] if sc else grads[2 * h + high].at[i % 4]
+        return pltpu.make_async_copy(src, g.at[slot], in_sem.at[2, slot])
+
+    def start(i, h):
+        for c in load(i, h):
+            c.start()
+        if kind == 'down' and h == 0:
+            load_act(i).start()
         if sc:
-            src = grads[0].at[natural(i) * 2 + (core if h == 0 else 1 - core)]
-        else:
-            src = grads[2 * h + high].at[i % 4]
-        return pltpu.make_async_copy(src, g.at[slot, h], g_sem.at[slot, h])
-
-    def start(i, slot):
-        for c in load(i, slot):
-            c.start()
-        for h in (0, 1):
-            if sc:
-                load_grad(i, slot, h, 0).start()
-                continue
-            for high in (0, 1):
-                @pl.when(i // 4 == high)
-                def _():
-                    load_grad(i, slot, h, high).start()
-
-    def store(i, slot):
-        return (pltpu.make_async_copy(w.at[slot], nw_ref.at[at(i)], out_sem.at[0, slot]),
-                pltpu.make_async_copy(m.at[slot], nm_ref.at[at(i)], out_sem.at[1, slot]))
-
-    def store_last(i):
-        span = pl.ds(pl.multiple_of(natural(i) * HB, HB), HB)
+            load_grad(i, h, 0).start()
+            return
+        for high in (0, 1):
+            @pl.when(i // 4 == high)
+            def _():
+                load_grad(i, h, high).start()
+
+    def store(i, h):
+        slot = (2 * i + h) % slots
+        return (pltpu.make_async_copy(w.at[slot], nw_ref.at[at(i, h)], out_sem.at[0, slot]),
+                pltpu.make_async_copy(m.at[slot], nm_ref.at[at(i, h)], out_sem.at[1, slot]))
+
+    def store_last(i, h):
         if kind == 'up':
-            return pltpu.make_async_copy(ob.at[i % 2], out_ref.at[:, span], ob_sem.at[i % 2])
-        dst = out_ref.at[:, span] if k == 0 else out_ref.at[span, :]
-        return pltpu.make_async_copy(ob.at[i % 2], dst, ob_sem.at[i % 2])
+            return pltpu.make_async_copy(ob.at[i % 2], out_ref.at[:, span(i)], ob_sem.at[i % 2])
+        return pltpu.make_async_copy(ob.at[i % 2, h], out_ref.at[at(i, h)[1:]], ob_sem.at[i % 2, h])
+
+    def whole_last(i):
+        return (store_last(i, 0),) if kind == 'up' else (store_last(i, 0), store_last(i, 1))
 
     start(0, 0)
-    start(1, 1)
+    start(0, 1)
+    start(1, 0)
     if kind == 'up':
-        act[...] = layer_norm(acts[0][...])[0].astype(BF16)
+        residual = acts[0][...]
+        normed = layer_norm(residual)[0].astype(BF16)
+        act[...] = normed
     elif kind == 'down':
         out_ref[...] = acts[0][...]
 
     def step(i, _):
-        slot = i % 4
-
-        @pl.when(i + 2 < NB)
-        def _():
+        pre = None
+        if kind != 'down':
             @pl.when(i >= 2)
             def _():
-                for c in store(i - 2, (i + 2) % 4):
+                for c in whole_last(i - 2):
                     c.wait()
-
-            start(i + 2, (i + 2) % 4)
-
-        for c in load(i, slot):
-            c.wait()
         for h in (0, 1):
-            load_grad(i, slot, h, 0).wait()
-            part = pl.ds(pl.multiple_of(offs[h], HB), HB)
-            idx = (slot, part, slice(None)) if k == 0 else (slot, slice(None), part)
-            new_m = mu * m[idx] + g[slot, h].astype(F32)
-            m[idx] = new_m
-            w[idx] = w[idx] - lr * new_m
-        for c in store(i, slot):
-            c.start()
-        new_bf = w[slot].astype(BF16)
-        if kind == 'down':
-            out_ref[...] += dot(act[slot], new_bf)
-        else:
-            @pl.when(i >= 2)
+            slot = (2 * i + h) % slots
+            ahead, side = (i + 1, 1) if h == 0 else (i + 2, 0)
+            back_i, back_h = (i - 2, 1) if h == 0 else (i - 1, 0)
+
+            @pl.when(ahead < NB)
             def _():
-                store_last(i - 2).wait()
-
+                @pl.when(back_i >= 0)
+                def _():
+                    for c in store(back_i, back_h):
+                        c.wait()
+
+                start(ahead, side)
+
+            for c in load(i, h):
+                c.wait()
+            load_grad(i, h, 0).wait()
+            new_m = mu * m[slot] + g[slot].astype(F32)
+            new_w = w[slot] - lr * new_m
+            m[slot] = new_m
+            w[slot] = new_w
+            for c in store(i, h):
+                c.start()
+            new_bf = new_w.astype(BF16)
             if kind == 'up':
-                ob[i % 2] = gelu(dot(act[...], new_bf)).astype(BF16)
+                part = dot(act[:, sides[h]], new_bf)
+                pre = part if h == 0 else pre + part
+            elif kind == 'down':
+                if h == 0:
+                    load_act(i).wait()
+                out_ref[:, sides[h]] += dot(act[i % 3], new_bf)
             else:
-                ob[i % 2] = new_bf
-            store_last(i).start()
+                ob[i % 2, h] = new_bf
+        if kind == 'up':
+            ob[i % 2] = gelu(pre).astype(BF16)
+        if kind != 'down':
+            for c in whole_last(i):
+                c.start()
         return 0
 
     lax.fori_loop(0, NB, step, 0)
-    for i in range(NB - 4, NB):
-        for c in store(i, i % 4):
+    for s in range(2 * NB - 6, 2 * NB):
+        for c in store(s // 2, s % 2):
             c.wait()
     if kind != 'down':
         for i in range(NB - 2, NB):
-            store_last(i).wait()
+            for c in whole_last(i):
+                c.wait()
 
 
 def update(m, kind, rates, acts, grads, w, mom, into):
     l, k = m
     dim, hid, rows = 1024, 4096, 512
     sc = len(grads) == 1
-    wide = (dim, HB) if k == 0 else (HB, dim)
+    ob_sem = DMA((2,))
     if kind == 'up':
         act_specs, last, last_spec = [WHOLE], jax.ShapeDtypeStruct((rows, hid), BF16), ANY
         ob, act = (2, rows, HB), (rows, dim)
     elif kind == 'down':
         act_specs, last, last_spec = [WHOLE, ANY], jax.ShapeDtypeStruct((rows, dim), F32), WHOLE
-        ob, act = (2, 16, 128), (4, rows, HB)
+        ob, act = (2, 16, 128), (3, rows, HB)
     else:
         act_specs, last_spec = [], ANY
         last = jax.ShapeDtypeStruct((dim, hid) if k == 0 else (hid, dim), BF16)
-        ob, act = (2,) + wide, (16, 128)
+        ob, act = (2, 2, HB, HB), (16, 128)
+        ob_sem = DMA((2, 2))
     in_specs = [pl.BlockSpec(memory_space=pltpu.SMEM)] + act_specs + [ANY] * (len(grads) + 2)
     args = [rates, *acts, *grads, w, mom]
     aliases = {}
@@ -521,9 +592,9 @@
     return pl.pallas_call(
         functools.partial(update_body, l, k, kind, order_of(m), sc, into is not None),
         out_shape=[full, full, last], in_specs=in_specs, out_specs=[ANY, ANY, last_spec],
-        scratch_shapes=[pltpu.VMEM((4,) + wide, F32), pltpu.VMEM((4,) + wide, F32), pltpu.VMEM((4, 2, HB, HB), BF16),
+        scratch_shapes=[pltpu.VMEM((6, HB, HB), F32), pltpu.VMEM((6, HB, HB), F32), pltpu.VMEM((6, HB, HB), BF16),
                         pltpu.VMEM(ob, BF16), pltpu.VMEM(act, BF16),
-                        DMA((3, 4)), DMA((4, 2)), DMA((2, 4)), DMA((2,))],
+                        DMA((3, 6)), DMA((3,)), DMA((2, 6)), ob_sem],
         input_output_aliases=aliases,
         compiler_params=pltpu.CompilerParams(vmem_limit_bytes=48 << 20),
         cost_estimate=pl.CostEstimate(flops=10_000_000_000, bytes_accessed=80 << 20, transcendentals=0))(*args)
@@ -552,12 +623,8 @@
         def cp(x, link):
             return lax.ppermute(x, BATCH_AXES, pairs[link])
 
-        residual = x_now.reshape(rows, model_dim).astype(F32)
-        saved = []
-        for l in range(layers):
-            after, hid_bf, slope = forward(l, residual, w_up, w_down)
-            saved.append((residual, slope, hid_bf))
-            residual = after
+        stream, hidden, slopes = forward(x_now.reshape(rows, model_dim), w_up, w_down)
+        residual = stream[layers]
         head_bf = w_head.astype(BF16)
         pooled, logits = pool_logits(residual, images, head_bf)
         soft_probs = jax.nn.softmax(logits, axis=-1)
@@ -580,8 +647,8 @@
             m = (l, k)
             order = order_of(m)
             if op == 'B':
-                v, d, r = hold(v_bf, d_res, saved[l][0])
-                out = back(l, v, d, r, w_up, w_down, saved[l][1], saved[l][2])
+                v, d = hold(v_bf, d_res)
+                out = back(l, v, d, stream, w_up, w_down, slopes, hidden)
                 for j in (1, 0):
                     box['s1', (l, j)], box['k1', (l, j)] = out[2 * j], out[2 * j + 1]
                 if l > 0:

time: 1250 us -> 1300 us (1.040)
  waiting for transfers between devices: 333 us -> 365 us
  matrix products: 23.6 us -> 48.2 us
    psum x1, waiting for transfers between devices: 0.01 us -> 17.7 us  [local_step(): red_head = lax.psum(grad_head.astype(BF16), BATCH_AXES)]
    dot_general x2 -> x4, matrix products: 11.1 us -> 25.3 us  [step(): out = r + jnp.dot(z, w, preferred_element_type=F32)]
    ppermute x76, waiting for transfers between devices: 333 us -> 347 us  [cp(): return lax.ppermute(x, BATCH_AXES, pairs[link])]
    pallas_call x6 -> x1, Pallas kernels: 104 us -> 92.8 us  [forward(): pl.pallas_call(functools.partial(fwd_body, layers), out_shape=[jax.ShapeD...]
  transfers between devices with their start and end apart: 81 -> 81, of which waited for: 19 -> 19; matrix products, arithmetic and copies ran while one was open for 1% -> 2% of each run, Pallas kernels for 48% -> 47%
where the time goes in v3:
time: 1300 us
  Pallas kernels  763 us (59%)
  waiting for transfers between devices  365 us (28%)
  starting transfers between devices  71.1 us (5%)
  matrix products  48.2 us (4%)
  local copies, waits for them, and re-layouts  20.7 us (2%)
  between operations  17.2 us (1%)
    ppermute x76, waiting for transfers between devices, cp(): return lax.ppermute(x, BATCH_AXES, pairs[link])  347 us
    pallas_call x12, Pallas kernels, update(): pl.pallas_call(functools.partial(update_body, l, k, kind, order_of(m), sc...  339 us
    pallas_call x6, Pallas kernels, back(): pl.pallas_call(functools.partial(back_body, l, last, order_of((l, 0)), or...  201 us
    pallas_call x36, Pallas kernels, add_halves(): pl.pallas_call(functools.partial(add_body, n), out_shape=[out] * count, i...  94.4 us
    pallas_call x1, Pallas kernels, forward(): pl.pallas_call(functools.partial(fwd_body, layers), out_shape=[jax.ShapeD...  92.8 us
    ppermute x76, starting transfers between devices, cp(): return lax.ppermute(x, BATCH_AXES, pairs[link])  70.9 us
    pallas_call x16, Pallas kernels, cat_halves(): pl.pallas_call(cat_body, out_shape=jax.ShapeDtypeStruct((n, HB, HB), BF16...  36.3 us
  transfers between devices with their start and end apart: 81, of which 19 were waited for; matrix products, arithmetic and copies ran while one was open for 2% of the time, Pallas kernels for 47%

profile of v3, /device:TPU:0, one launch (start us, length us, event | category | flops | bytes accessed | tf_op | source)
XLA Modules:
  0.0 1295.3 jit_solution(10171994093791553827)
XLA Ops:
  8.4 92.8 %forward.1 = (f32[7,512,1024]{2,1,0:T(8,128)}, bf16[6,512,4096]{2,1,0:T(8,128)(2,1)}, f32[6,512,4096]{2,1,0:T(8,128)}) custom-call(bf16[512,1024]{1,0:T(8,128)(2,1)S(1)} %bitcast.23, f32[6,1024,4096]{2,1,0:T(8,128)} %refs_2_.5, f32[6,4096,1024]{2,1,0:T(8,128)} %refs_3_.4), custom_call_target="tpu_custom_call" | custom-call | flops 51539607552 | bytes 293601280 | tf_op jit(solution)/shard_map/forward/pallas_call | solution.py:420
  109.7 34.5 %back.6 = (bf16[4,512,512]{2,1,0:T(8,128)(2,1)}, bf16[4,512,512]{2,1,0:T(8,128)(2,1)}, bf16[4,512,512]{2,1,0:T(8,128)(2,1)}, bf16[4,512,512]{2,1,0:T(8,128)(2,1)...) custom-call(bf16[512,1024]{1,0:T(8,128)(2,1)} %bitcast_convert_fusion.v_hbm, f32[512,1024]{1,0:T(8,128)} %bitcast.24, ...), custom_call_target="tpu_custom_call" | custom-call | flops 17179869184 | bytes 62914560 | tf_op jit(solution)/shard_map/back/pallas_call | solution.py:248
  148.9 34.8 %back.7 = (bf16[4,512,512]{2,1,0:T(8,128)(2,1)}, bf16[4,512,512]{2,1,0:T(8,128)(2,1)}, bf16[4,512,512]{2,1,0:T(8,128)(2,1)}, bf16[4,512,512]{2,1,0:T(8,128)(2,1)...) custom-call(bf16[512,1024]{1,0:T(8,128)(2,1)} %get-tuple-element.331.v_hbm, f32[512,1024]{1,0:T(8,128)} %get-tuple-element.332.d_hbm, ...), custom_call_target="tpu_custom_call" | custom-call | flops 17179869184 | bytes 62914560 | tf_op jit(solution)/shard_map/back/pallas_call | solution.py:248
  185.4 34.6 %back.8 = (bf16[4,512,512]{2,1,0:T(8,128)(2,1)}, bf16[4,512,512]{2,1,0:T(8,128)(2,1)}, bf16[4,512,512]{2,1,0:T(8,128)(2,1)}, bf16[4,512,512]{2,1,0:T(8,128)(2,1)...) custom-call(bf16[512,1024]{1,0:T(8,128)(2,1)} %get-tuple-element.336.v_hbm, f32[512,1024]{1,0:T(8,128)} %get-tuple-element.337.d_hbm, ...), custom_call_target="tpu_custom_call" | custom-call | flops 17179869184 | bytes 62914560 | tf_op jit(solution)/shard_map/back/pallas_call | solution.py:248
  227.4 35.0 %back.9 = (bf16[4,512,512]{2,1,0:T(8,128)(2,1)}, bf16[4,512,512]{2,1,0:T(8,128)(2,1)}, bf16[4,512,512]{2,1,0:T(8,128)(2,1)}, bf16[4,512,512]{2,1,0:T(8,128)(2,1)...) custom-call(bf16[512,1024]{1,0:T(8,128)(2,1)} %get-tuple-element.352.v_hbm, f32[512,1024]{1,0:T(8,128)} %get-tuple-element.353.d_hbm, ...), custom_call_target="tpu_custom_call" | custom-call | flops 17179869184 | bytes 62914560 | tf_op jit(solution)/shard_map/back/pallas_call | solution.py:248
  280.6 34.7 %back.10 = (bf16[4,512,512]{2,1,0:T(8,128)(2,1)}, bf16[4,512,512]{2,1,0:T(8,128)(2,1)}, bf16[4,512,512]{2,1,0:T(8,128)(2,1)}, bf16[4,512,512]{2,1,0:T(8,128)(2,1...) custom-call(bf16[512,1024]{1,0:T(8,128)(2,1)} %get-tuple-element.377.v_hbm, f32[512,1024]{1,0:T(8,128)} %get-tuple-element.378.d_hbm, ...), custom_call_target="tpu_custom_call" | custom-call | flops 17179869184 | bytes 62914560 | tf_op jit(solution)/shard_map/back/pallas_call | solution.py:248
  352.4 27.3 %back.11 = (bf16[4,512,512]{2,1,0:T(8,128)(2,1)}, bf16[4,512,512]{2,1,0:T(8,128)(2,1)}, bf16[4,512,512]{2,1,0:T(8,128)(2,1)}, bf16[4,512,512]{2,1,0:T(8,128)(2,1)}) custom-call(bf16[512,1024]{1,0:T(8,128)(2,1)} %get-tuple-element.409.v_hbm, f32[512,1024]{1,0:T(8,128)} %get-tuple-element.410.d_hbm, f32[7,512,1024]{2,1,0:T(8,128)} %get-tuple-element.325.r_hbm, ...), custom_call_target="tpu_custom_call" | custom-call | flops 17179869184 | bytes 62914560 | tf_op jit(solution)/shard_map/back/pallas_call | solution.py:248
  396.6 17.7 %all-reduce.2.cloned.1.call-done = bf16[1024,1000]{0,1:T(8,128)(2,1)} async-done(((bf16[1024,1000]{0,1:T(8,128)(2,1)}), bf16[1024,1000]{0,1:T(8,128)(2,1)}) %all-reduce.2.cloned.1.call-update) | async-done | bytes 2048016 | tf_op jit(solution)/shard_map/psum | solution.py:634
  416.3 8.9 multiply_subtract_fusion
  458.3 59.4 %collective-permute-done.22.b_ref = bf16[2,512,512]{2,1,0:T(8,128)(2,1)} collective-permute-done((bf16[2,512,512]{2,1,0:T(8,128)(2,1)S(1)}, bf16[2,512,512]{2,1,0:T(8,128)(2,1)}, u32[]{:S(2)}, u32[]{:S(2)}) %collective-permute-start.22) | collective-permute-done | bytes 1048608 | tf_op jit(solution)/shard_map/ppermute | solution.py:624
  540.6 21.7 %collective-permute-done.37.b_ref = bf16[2,512,512]{2,1,0:T(8,128)(2,1)S(1)} collective-permute-done((bf16[2,512,512]{2,1,0:T(8,128)(2,1)S(1)}, bf16[2,512,512]{2,1,0:T(8,128)(2,1)S(1)}, u32[]{:S(2)}, u32[]{:S(2)}) %collective-permute-start.37) | collective-permute-done | bytes 1048608 | tf_op jit(solution)/shard_map/ppermute | solution.py:624
  569.7 29.6 %shard_map.162 = (f32[6,1024,4096]{2,1,0:T(8,128)}, f32[6,1024,4096]{2,1,0:T(8,128)}, bf16[1024,4096]{1,0:T(8,128)(2,1)}) custom-call(f32[2]{0:T(128)S(1)} %pad_maximum_fusion.rates_ref, bf16[4,512,512]{2,1,0:T(8,128)(2,1)} %cat.20.refs_0_, bf16[4,512,512]{2,1,0:T(8,128)(2,1)} %collective-permute-done.31.refs_1_, ...), custom_call_target="tpu_custom_call" | custom-call | flops 10000000000 | bytes 83886080 | tf_op jit(solution)/shard_map/pallas_call | solution.py:592
  605.9 22.0 %collective-permute-done.43.b_ref = bf16[2,512,512]{2,1,0:T(8,128)(2,1)} collective-permute-done((bf16[2,512,512]{2,1,0:T(8,128)(2,1)}, bf16[2,512,512]{2,1,0:T(8,128)(2,1)}, u32[]{:S(2)}, u32[]{:S(2)}) %collective-permute-start.43) | collective-permute-done | bytes 1048608 | tf_op jit(solution)/shard_map/ppermute | solution.py:624
  632.4 28.8 %shard_map.163 = (f32[6,4096,1024]{2,1,0:T(8,128)}, f32[6,4096,1024]{2,1,0:T(8,128)}, bf16[4096,1024]{1,0:T(8,128)(2,1)}) custom-call(f32[2]{0:T(128)S(1)} %pad_maximum_fusion.rates_ref, bf16[4,512,512]{2,1,0:T(8,128)(2,1)S(1)} %copy-done.4, bf16[4,512,512]{2,1,0:T(8,128)(2,1)} %collective-permute-done.40.refs_1_, ...), custom_call_target="tpu_custom_call" | custom-call | flops 10000000000 | bytes 83886080 | tf_op jit(solution)/shard_map/pallas_call | solution.py:592
  680.6 69.7 %collective-permute-done.54.refs_1_ = bf16[4,512,512]{2,1,0:T(8,128)(2,1)S(1)} collective-permute-done((bf16[4,512,512]{2,1,0:T(8,128)(2,1)S(1)}, bf16[4,512,512]{2,1,0:T(8,128)(2,1)S(1)}, u32[]{:S(2)}, u32[]{:S(2)}) %collective-permute-start.54) | collective-permute-done | bytes 2097184 | tf_op jit(solution)/shard_map/ppermute | solution.py:624
  756.0 28.0 %shard_map.164 = (f32[6,4096,1024]{2,1,0:T(8,128)}, f32[6,4096,1024]{2,1,0:T(8,128)}, bf16[4096,1024]{1,0:T(8,128)(2,1)}) custom-call(f32[2]{0:T(128)S(1)} %pad_maximum_fusion.rates_ref, bf16[4,512,512]{2,1,0:T(8,128)(2,1)S(1)} %copy-done, bf16[4,512,512]{2,1,0:T(8,128)(2,1)S(1)} %collective-permute-done.54.refs_1_, ...), custom_call_target="tpu_custom_call", output_to_operand_aliasing={{0}: (7, {}), {1}: (8, {})} | custom-call | flops 10000000000 | bytes 83886080 | tf_op jit(solution)/shard_map/pallas_call | solution.py:592
  789.4 29.0 %shard_map.165 = (f32[6,1024,4096]{2,1,0:T(8,128)}, f32[6,1024,4096]{2,1,0:T(8,128)}, bf16[1024,4096]{1,0:T(8,128)(2,1)}) custom-call(f32[2]{0:T(128)S(1)} %pad_maximum_fusion.rates_ref, bf16[4,512,512]{2,1,0:T(8,128)(2,1)S(1)} %copy-done.2, bf16[4,512,512]{2,1,0:T(8,128)(2,1)} %collective-permute-done.49.refs_1_, ...), custom_call_target="tpu_custom_call", output_to_operand_aliasing={{0}: (7, {}), {1}: (8, {})} | custom-call | flops 10000000000 | bytes 83886080 | tf_op jit(solution)/shard_map/pallas_call | solution.py:592
  833.8 71.8 %collective-permute-done.60.refs_1_ = bf16[4,512,512]{2,1,0:T(8,128)(2,1)S(1)} collective-permute-done((bf16[4,512,512]{2,1,0:T(8,128)(2,1)S(1)}, bf16[4,512,512]{2,1,0:T(8,128)(2,1)S(1)}, u32[]{:S(2)}, u32[]{:S(2)}) %collective-permute-start.60) | collective-permute-done | bytes 2097184 | tf_op jit(solution)/shard_map/ppermute | solution.py:624
  911.1 27.4 %shard_map.166 = (f32[6,4096,1024]{2,1,0:T(8,128)}, f32[6,4096,1024]{2,1,0:T(8,128)}, bf16[4096,1024]{1,0:T(8,128)(2,1)}) custom-call(f32[2]{0:T(128)S(1)} %pad_maximum_fusion.rates_ref, bf16[4,512,512]{2,1,0:T(8,128)(2,1)S(1)} %copy-done.1, bf16[4,512,512]{2,1,0:T(8,128)(2,1)S(1)} %collective-permute-done.60.refs_1_, ...), custom_call_target="tpu_custom_call", output_to_operand_aliasing={{0}: (7, {}), {1}: (8, {})} | custom-call | flops 10000000000 | bytes 83886080 | tf_op jit(solution)/shard_map/pallas_call | solution.py:592
  942.0 11.7 collective-permute-done.58.b_ref
  959.9 29.4 %shard_map.167 = (f32[6,4096,1024]{2,1,0:T(8,128)}, f32[6,4096,1024]{2,1,0:T(8,128)}, bf16[4096,1024]{1,0:T(8,128)(2,1)}) custom-call(f32[2]{0:T(128)S(1)} %pad_maximum_fusion.rates_ref, bf16[16,512,512]{2,1,0:T(8,128)(2,1)} %all-gather.11.cloned.1.call-done.refs_0_, f32[6,4096,1024]{2,1,0:T(8,128)} %refs_3_.4, ...), custom_call_target="tpu_custom_call", output_to_operand_aliasing={{0}: (4, {}), {1}: (5, {})} | custom-call | flops 10000000000 | bytes 83886080 | tf_op jit(solution)/shard_map/pallas_call | solution.py:592
  999.1 28.5 %shard_map.168 = (f32[6,1024,4096]{2,1,0:T(8,128)}, f32[6,1024,4096]{2,1,0:T(8,128)}, bf16[512,4096]{1,0:T(8,128)(2,1)}) custom-call(f32[2]{0:T(128)S(1)} %pad_maximum_fusion.rates_ref, f32[512,1024]{1,0:T(8,128)S(1)} %bitcast_convert_fusion.1.refs_0_, ...), custom_call_target="tpu_custom_call", output_to_operand_aliasing={{0}: (5, {}), {1}: (6, {})} | custom-call | flops 10000000000 | bytes 83886080 | tf_op jit(solution)/shard_map/pallas_call | solution.py:592
  1033.3 8.2 convolution_add_fusion.3.refs_0_
  1041.5 61.7 %collective-permute-done.67.refs_2_ = bf16[4,512,512]{2,1,0:T(8,128)(2,1)S(1)} collective-permute-done((bf16[4,512,512]{2,1,0:T(8,128)(2,1)}, bf16[4,512,512]{2,1,0:T(8,128)(2,1)S(1)}, u32[]{:S(2)}, u32[]{:S(2)}) %collective-permute-start.67) | collective-permute-done | bytes 2097184 | tf_op jit(solution)/shard_map/ppermute | solution.py:624
  1109.0 26.8 %shard_map.169 = (f32[6,1024,4096]{2,1,0:T(8,128)}, f32[6,1024,4096]{2,1,0:T(8,128)}, bf16[512,4096]{1,0:T(8,128)(2,1)}) custom-call(f32[2]{0:T(128)S(1)} %pad_maximum_fusion.rates_ref, f32[512,1024]{1,0:T(8,128)S(1)} %convolution_add_fusion.3.refs_0_, bf16[4,512,512]{2,1,0:T(8,128)(2,1)S(1)} %copy-done.3, ...), custom_call_target="tpu_custom_call", output_to_operand_aliasing={{0}: (8, {}), {1}: (9, {})} | custom-call | flops 10000000000 | bytes 83886080 | tf_op jit(solution)/shard_map/pallas_call | solution.py:592
  1137.2 27.2 %shard_map.170 = (f32[6,4096,1024]{2,1,0:T(8,128)}, f32[6,4096,1024]{2,1,0:T(8,128)}, f32[512,1024]{1,0:T(8,128)S(1)}) custom-call(f32[2]{0:T(128)S(1)} %pad_maximum_fusion.rates_ref, f32[512,1024]{1,0:T(8,128)S(1)} %convolution_add_fusion.3.refs_0_, bf16[512,4096]{1,0:T(8,128)(2,1)} %get-tuple-element.597.refs_1_, ...), custom_call_target="tpu_custom_call", output_to_operand_aliasing={{0}: (9, {}), {1}: (10, {})} | custom-call | flops 10000000000 | bytes 83886080 | tf_op jit(solution)/shard_map/pallas_call | solution.py:592
  1164.5 28.0 %shard_map.171 = (f32[6,1024,4096]{2,1,0:T(8,128)}, f32[6,1024,4096]{2,1,0:T(8,128)}, bf16[512,4096]{1,0:T(8,128)(2,1)}) custom-call(f32[2]{0:T(128)S(1)} %pad_maximum_fusion.rates_ref, f32[512,1024]{1,0:T(8,128)S(1)} %get-tuple-element.614.refs_0_, bf16[4,512,512]{2,1,0:T(8,128)(2,1)} %cat.30.refs_1_, ...), custom_call_target="tpu_custom_call", output_to_operand_aliasing={{0}: (8, {}), {1}: (9, {})} | custom-call | flops 10000000000 | bytes 83886080 | tf_op jit(solution)/shard_map/pallas_call | solution.py:592
  1192.6 27.5 %shard_map.172 = (f32[6,4096,1024]{2,1,0:T(8,128)}, f32[6,4096,1024]{2,1,0:T(8,128)}, f32[512,1024]{1,0:T(8,128)S(1)}) custom-call(f32[2]{0:T(128)S(1)} %pad_maximum_fusion.rates_ref, f32[512,1024]{1,0:T(8,128)S(1)} %get-tuple-element.614.refs_0_, bf16[512,4096]{1,0:T(8,128)(2,1)} %get-tuple-element.615.refs_1_, ...), custom_call_target="tpu_custom_call", output_to_operand_aliasing={{0}: (6, {}), {1}: (7, {})} | custom-call | flops 10000000000 | bytes 83886080 | tf_op jit(solution)/shard_map/pallas_call | solution.py:592
  1223.0 28.4 %shard_map.173 = (f32[6,1024,4096]{2,1,0:T(8,128)}, f32[6,1024,4096]{2,1,0:T(8,128)}, bf16[512,4096]{1,0:T(8,128)(2,1)}) custom-call(f32[2]{0:T(128)S(1)} %pad_maximum_fusion.rates_ref, f32[512,1024]{1,0:T(8,128)S(1)} %copy-done.6, bf16[16,512,512]{2,1,0:T(8,128)(2,1)} %all-gather.15.cloned.1.call-done.refs_1_, ...), custom_call_target="tpu_custom_call", output_to_operand_aliasing={{0}: (5, {}), {1}: (6, {})} | custom-call | flops 10000000000 | bytes 83886080 | tf_op jit(solution)/shard_map/pallas_call | solution.py:592
  1252.0 6.5 convolution_add_fusion.2
  1259.9 7.8 multiply_convert_fusion.1
  1274.4 8.1 multiply_convert_fusion
  (349 shorter events, 270.9 us)
Async XLA Ops:
  7.2 407.1 %all-reduce.2.cloned.1.call-start = ((), (), s32[]{:S(2)}) async-start(), calls=%async_computation | async-start | bytes 4096000 | tf_op jit(solution)/shard_map/psum | solution.py:634
  144.2 76.7 %collective-permute-start.1 = (bf16[4,512,512]{2,1,0:T(8,128)(2,1)}, bf16[4,512,512]{2,1,0:T(8,128)(2,1)}, u32[]{:S(2)}, u32[]{:S(2)}) collective-permute-start(bf16[4,512,512]{2,1,0:T(8,128)(2,1)} %get-tuple-element.344), channel_id=1, source_target_pairs={{0,4},{1,5},{2,6},{3,7},{4,0},{5,1},{6,2},{7,3},{8,12},{9,13},{10,... | collective-permute-start | bytes 6291464 | tf_op jit(solution)/shard_map/ppermute | solution.py:624
  147.4 76.7 %collective-permute-start = (bf16[4,512,512]{2,1,0:T(8,128)(2,1)}, bf16[4,512,512]{2,1,0:T(8,128)(2,1)}, u32[]{:S(2)}, u32[]{:S(2)}) collective-permute-start(bf16[4,512,512]{2,1,0:T(8,128)(2,1)} %get-tuple-element.341), channel_id=1, source_target_pairs={{0,2},{1,3},{2,0},{3,1},{4,6},{5,7},{6,4},{7,5},{8,10},{9,11},{10,... | collective-permute-start | bytes 6291464 | tf_op jit(solution)/shard_map/ppermute | solution.py:624
  183.7 78.7 %collective-permute-start.5 = (bf16[4,512,512]{2,1,0:T(8,128)(2,1)}, bf16[4,512,512]{2,1,0:T(8,128)(2,1)}, u32[]{:S(2)}, u32[]{:S(2)}) collective-permute-start(bf16[4,512,512]{2,1,0:T(8,128)(2,1)} %get-tuple-element.363), channel_id=1, source_target_pairs={{0,8},{1,9},{2,10},{3,11},{4,12},{5,13},{6,14},{7,15},{8,0},{9,1},... | collective-permute-start | bytes 6291464 | tf_op jit(solution)/shard_map/ppermute | solution.py:624
  336.5 623.4 %all-gather.11.cloned.1.call-start = ((), (), s32[]{:S(2)}) async-start(), calls=%async_computation.2 | async-start | bytes 8912896 | tf_op jit(solution)/shard_map/all_gather | solution.py:671
  341.1 74.6 %collective-permute-start.18 = (bf16[4,512,512]{2,1,0:T(8,128)(2,1)S(1)}, bf16[4,512,512]{2,1,0:T(8,128)(2,1)}, u32[]{:S(2)}, u32[]{:S(2)}) collective-permute-start(bf16[4,512,512]{2,1,0:T(8,128)(2,1)S(1)} %copy-done.34), channel_id=1, source_target_pairs={{0,2},{1,3},{2,0},{3,1},{4,6},{5,7},{6,4},{7,5},{8,10},{9,11},{10,... | collective-permute-start | bytes 6291464 | tf_op jit(solution)/shard_map/ppermute | solution.py:624
  347.3 66.9 %collective-permute-start.17 = (bf16[1,512,512]{2,1,0:T(8,128)(2,1)}, bf16[1,512,512]{2,1,0:T(8,128)(2,1)}, u32[]{:S(2)}, u32[]{:S(2)}) collective-permute-start(bf16[1,512,512]{2,1,0:T(8,128)(2,1)} %get-tuple-element.418), channel_id=1, source_target_pairs={{0,8},{1,9},{2,10},{3,11},{4,12},{5,13},{6,14},{7,15},{8,0},{9,1},... | collective-permute-start | bytes 1572872 | tf_op jit(solution)/shard_map/ppermute | solution.py:624
  352.3 84.3 %collective-permute-start.26 = (bf16[4,512,512]{2,1,0:T(8,128)(2,1)}, bf16[4,512,512]{2,1,0:T(8,128)(2,1)}, u32[]{:S(2)}, u32[]{:S(2)}) collective-permute-start(bf16[4,512,512]{2,1,0:T(8,128)(2,1)} %get-tuple-element.442), channel_id=1, source_target_pairs={{0,4},{1,5},{2,6},{3,7},{4,0},{5,1},{6,2},{7,3},{8,12},{9,13},{10,... | collective-permute-start | bytes 6291464 | tf_op jit(solution)/shard_map/ppermute | solution.py:624
  433.9 92.7 %collective-permute-start.15 = (bf16[4,512,512]{2,1,0:T(8,128)(2,1)S(1)}, bf16[4,512,512]{2,1,0:T(8,128)(2,1)}, u32[]{:S(2)}, u32[]{:S(2)}) collective-permute-start(bf16[4,512,512]{2,1,0:T(8,128)(2,1)S(1)} %copy-done.35), channel_id=1, source_target_pairs={{0,8},{1,9},{2,10},{3,11},{4,12},{5,13},{6,14},{7,15},{8,0},{9,1},... | collective-permute-start | bytes 6291464 | tf_op jit(solution)/shard_map/ppermute | solution.py:624
  436.5 96.7 %collective-permute-start.33 = (bf16[4,512,512]{2,1,0:T(8,128)(2,1)}, bf16[4,512,512]{2,1,0:T(8,128)(2,1)}, u32[]{:S(2)}, u32[]{:S(2)}) collective-permute-start(bf16[4,512,512]{2,1,0:T(8,128)(2,1)} %get-tuple-element.467), channel_id=1, source_target_pairs={{0,2},{1,3},{2,0},{3,1},{4,6},{5,7},{6,4},{7,5},{8,10},{9,11},{10,... | collective-permute-start | bytes 6291464 | tf_op jit(solution)/shard_map/ppermute | solution.py:624
  445.6 91.0 %collective-permute-start.31 = (bf16[4,512,512]{2,1,0:T(8,128)(2,1)}, bf16[4,512,512]{2,1,0:T(8,128)(2,1)}, u32[]{:S(2)}, u32[]{:S(2)}) collective-permute-start(bf16[4,512,512]{2,1,0:T(8,128)(2,1)} %cat.20.refs_0_), channel_id=1, source_target_pairs={{0,4},{1,5},{2,6},{3,7},{4,0},{5,1},{6,2},{7,3},{8,12},{9,13},{10,... | collective-permute-start | bytes 6291464 | tf_op jit(solution)/shard_map/ppermute | solution.py:624
  451.8 65.8 %collective-permute-start.22 = (bf16[2,512,512]{2,1,0:T(8,128)(2,1)S(1)}, bf16[2,512,512]{2,1,0:T(8,128)(2,1)}, u32[]{:S(2)}, u32[]{:S(2)}) collective-permute-start(bf16[2,512,512]{2,1,0:T(8,128)(2,1)S(1)} %copy-done.41), channel_id=1, source_target_pairs={{0,2},{1,3},{2,0},{3,1},{4,6},{5,7},{6,4},{7,5},{8,10},{9,11},{10,... | collective-permute-start | bytes 3145736 | tf_op jit(solution)/shard_map/ppermute | solution.py:624
  454.8 69.4 %collective-permute-start.21 = (bf16[2,512,512]{2,1,0:T(8,128)(2,1)}, bf16[2,512,512]{2,1,0:T(8,128)(2,1)}, u32[]{:S(2)}, u32[]{:S(2)}) collective-permute-start(bf16[2,512,512]{2,1,0:T(8,128)(2,1)} %cat.18.a_ref), channel_id=1, source_target_pairs={{0,4},{1,5},{2,6},{3,7},{4,0},{5,1},{6,2},{7,3},{8,12},{9,13},{10,... | collective-permute-start | bytes 3145736 | tf_op jit(solution)/shard_map/ppermute | solution.py:624
  567.4 63.5 %collective-permute-start.41 = (bf16[4,512,512]{2,1,0:T(8,128)(2,1)S(1)}, bf16[4,512,512]{2,1,0:T(8,128)(2,1)}, u32[]{:S(2)}, u32[]{:S(2)}) collective-permute-start(bf16[4,512,512]{2,1,0:T(8,128)(2,1)S(1)} %copy-done.4), channel_id=1, source_target_pairs={{0,1},{1,0},{2,3},{3,2},{4,5},{5,4},{6,7},{7,6},{8,9},{9,8},{10,11... | collective-permute-start | bytes 6291464 | tf_op jit(solution)/shard_map/ppermute | solution.py:624
  603.0 64.3 %collective-permute-start.29 = (bf16[1,512,512]{2,1,0:T(8,128)(2,1)}, bf16[1,512,512]{2,1,0:T(8,128)(2,1)}, u32[]{:S(2)}, u32[]{:S(2)}) collective-permute-start(bf16[1,512,512]{2,1,0:T(8,128)(2,1)} %get-tuple-element.464), channel_id=1, source_target_pairs={{0,8},{1,9},{2,10},{3,11},{4,12},{5,13},{6,14},{7,15},{8,0},{9,1},... | collective-permute-start | bytes 1572872 | tf_op jit(solution)/shard_map/ppermute | solution.py:624
  604.4 65.0 %collective-permute-start.28 = (bf16[2,512,512]{2,1,0:T(8,128)(2,1)S(1)}, bf16[2,512,512]{2,1,0:T(8,128)(2,1)}, u32[]{:S(2)}, u32[]{:S(2)}) collective-permute-start(bf16[2,512,512]{2,1,0:T(8,128)(2,1)S(1)} %copy-done.37), channel_id=1, source_target_pairs={{0,2},{1,3},{2,0},{3,1},{4,6},{5,7},{6,4},{7,5},{8,10},{9,11},{10,... | collective-permute-start | bytes 3145736 | tf_op jit(solution)/shard_map/ppermute | solution.py:624
  678.6 320.5 %all-gather.9.cloned.1.call-start = ((), (), s32[]{:S(2)}) async-start(), calls=%async_computation.1 | async-start | bytes 8912896 | tf_op jit(solution)/shard_map/all_gather | solution.py:671
  678.7 71.6 %collective-permute-start.54 = (bf16[4,512,512]{2,1,0:T(8,128)(2,1)S(1)}, bf16[4,512,512]{2,1,0:T(8,128)(2,1)S(1)}, u32[]{:S(2)}, u32[]{:S(2)}) collective-permute-start(bf16[4,512,512]{2,1,0:T(8,128)(2,1)S(1)} %copy-done), channel_id=1, source_target_pairs={{0,8},{1,9},{2,10},{3,11},{4,12},{5,13},{6,14},{7,15},{8,0},{9,1},... | collective-permute-start | bytes 6291464 | tf_op jit(solution)/shard_map/ppermute | solution.py:624
  680.2 71.5 %collective-permute-start.49 = (bf16[4,512,512]{2,1,0:T(8,128)(2,1)}, bf16[4,512,512]{2,1,0:T(8,128)(2,1)}, u32[]{:S(2)}, u32[]{:S(2)}) collective-permute-start(bf16[4,512,512]{2,1,0:T(8,128)(2,1)} %cat.24.refs_0_), channel_id=1, source_target_pairs={{0,4},{1,5},{2,6},{3,7},{4,0},{5,1},{6,2},{7,3},{8,12},{9,13},{10,... | collective-permute-start | bytes 6291464 | tf_op jit(solution)/shard_map/ppermute | solution.py:624
  680.6 71.7 %collective-permute-start.55 = (bf16[4,512,512]{2,1,0:T(8,128)(2,1)S(1)}, bf16[4,512,512]{2,1,0:T(8,128)(2,1)S(1)}, u32[]{:S(2)}, u32[]{:S(2)}) collective-permute-start(bf16[4,512,512]{2,1,0:T(8,128)(2,1)S(1)} %copy-done), channel_id=1, source_target_pairs={{0,1},{1,0},{2,3},{3,2},{4,5},{5,4},{6,7},{7,6},{8,9},{9,8},{10,11... | collective-permute-start | bytes 6291464 | tf_op jit(solution)/shard_map/ppermute | solution.py:624
  751.7 66.8 %collective-permute-start.48 = (bf16[4,512,512]{2,1,0:T(8,128)(2,1)}, bf16[4,512,512]{2,1,0:T(8,128)(2,1)}, u32[]{:S(2)}, u32[]{:S(2)}) collective-permute-start(bf16[4,512,512]{2,1,0:T(8,128)(2,1)} %get-tuple-element.512), channel_id=1, source_target_pairs={{0,8},{1,9},{2,10},{3,11},{4,12},{5,13},{6,14},{7,15},{8,0},{9,1},... | collective-permute-start | bytes 6291464 | tf_op jit(solution)/shard_map/ppermute | solution.py:624
  754.4 69.3 %collective-permute-start.46 = (bf16[4,512,512]{2,1,0:T(8,128)(2,1)}, bf16[4,512,512]{2,1,0:T(8,128)(2,1)}, u32[]{:S(2)}, u32[]{:S(2)}) collective-permute-start(bf16[4,512,512]{2,1,0:T(8,128)(2,1)} %get-tuple-element.509), channel_id=1, source_target_pairs={{0,4},{1,5},{2,6},{3,7},{4,0},{5,1},{6,2},{7,3},{8,12},{9,13},{10,... | collective-permute-start | bytes 6291464 | tf_op jit(solution)/shard_map/ppermute | solution.py:624
  832.2 360.3 %all-gather.13.cloned.1.call-start = ((), (), s32[]{:S(2)}) async-start(), calls=%async_computation.3 | async-start | bytes 8912896 | tf_op jit(solution)/shard_map/all_gather | solution.py:671
  832.3 73.2 %collective-permute-start.60 = (bf16[4,512,512]{2,1,0:T(8,128)(2,1)S(1)}, bf16[4,512,512]{2,1,0:T(8,128)(2,1)S(1)}, u32[]{:S(2)}, u32[]{:S(2)}) collective-permute-start(bf16[4,512,512]{2,1,0:T(8,128)(2,1)S(1)} %copy-done.1), channel_id=1, source_target_pairs={{0,2},{1,3},{2,0},{3,1},{4,6},{5,7},{6,4},{7,5},{8,10},{9,11},{10,... | collective-permute-start | bytes 6291464 | tf_op jit(solution)/shard_map/ppermute | solution.py:624
  833.8 74.9 %collective-permute-start.61 = (bf16[4,512,512]{2,1,0:T(8,128)(2,1)S(1)}, bf16[4,512,512]{2,1,0:T(8,128)(2,1)S(1)}, u32[]{:S(2)}, u32[]{:S(2)}) collective-permute-start(bf16[4,512,512]{2,1,0:T(8,128)(2,1)S(1)} %copy-done.1), channel_id=1, source_target_pairs={{0,1},{1,0},{2,3},{3,2},{4,5},{5,4},{6,7},{7,6},{8,9},{9,8},{10,11... | collective-permute-start | bytes 6291464 | tf_op jit(solution)/shard_map/ppermute | solution.py:624
  906.7 82.6 %collective-permute-start.65 = (bf16[2,512,512]{2,1,0:T(8,128)(2,1)}, bf16[2,512,512]{2,1,0:T(8,128)(2,1)}, u32[]{:S(2)}, u32[]{:S(2)}) collective-permute-start(bf16[2,512,512]{2,1,0:T(8,128)(2,1)} %cat.27.a_ref), channel_id=1, source_target_pairs={{0,4},{1,5},{2,6},{3,7},{4,0},{5,1},{6,2},{7,3},{8,12},{9,13},{10,... | collective-permute-start | bytes 3145736 | tf_op jit(solution)/shard_map/ppermute | solution.py:624
  908.2 83.6 %collective-permute-start.64 = (bf16[2,512,512]{2,1,0:T(8,128)(2,1)}, bf16[2,512,512]{2,1,0:T(8,128)(2,1)}, u32[]{:S(2)}, u32[]{:S(2)}) collective-permute-start(bf16[2,512,512]{2,1,0:T(8,128)(2,1)} %cat.28.a_ref), channel_id=1, source_target_pairs={{0,8},{1,9},{2,10},{3,11},{4,12},{5,13},{6,14},{7,15},{8,0},{9,1},... | collective-permute-start | bytes 3145736 | tf_op jit(solution)/shard_map/ppermute | solution.py:624
  997.3 224.2 %all-gather.15.cloned.1.call-start = ((), (), s32[]{:S(2)}) async-start(), calls=%async_computation.4 | async-start | bytes 8912896 | tf_op jit(solution)/shard_map/all_gather | solution.py:671
  1030.7 72.5 %collective-permute-start.67 = (bf16[4,512,512]{2,1,0:T(8,128)(2,1)}, bf16[4,512,512]{2,1,0:T(8,128)(2,1)S(1)}, u32[]{:S(2)}, u32[]{:S(2)}) collective-permute-start(bf16[4,512,512]{2,1,0:T(8,128)(2,1)} %cat.29.refs_1_), channel_id=1, source_target_pairs={{0,8},{1,9},{2,10},{3,11},{4,12},{5,13},{6,14},{7,15},{8,0},{9,1},... | collective-permute-start | bytes 6291464 | tf_op jit(solution)/shard_map/ppermute | solution.py:624
  1031.4 72.9 %collective-permute-start.68 = (bf16[4,512,512]{2,1,0:T(8,128)(2,1)}, bf16[4,512,512]{2,1,0:T(8,128)(2,1)S(1)}, u32[]{:S(2)}, u32[]{:S(2)}) collective-permute-start(bf16[4,512,512]{2,1,0:T(8,128)(2,1)} %cat.29.refs_1_), channel_id=1, source_target_pairs={{0,1},{1,0},{2,3},{3,2},{4,5},{5,4},{6,7},{7,6},{8,9},{9,8},{10,11... | collective-permute-start | bytes 6291464 | tf_op jit(solution)/shard_map/ppermute | solution.py:624
  1031.4 72.4 %collective-permute-start.73 = (bf16[4,512,512]{2,1,0:T(8,128)(2,1)}, bf16[4,512,512]{2,1,0:T(8,128)(2,1)}, u32[]{:S(2)}, u32[]{:S(2)}) collective-permute-start(bf16[4,512,512]{2,1,0:T(8,128)(2,1)} %cat.30.refs_1_), channel_id=1, source_target_pairs={{0,2},{1,3},{2,0},{3,1},{4,6},{5,7},{6,4},{7,5},{8,10},{9,11},{10,... | collective-permute-start | bytes 6291464 | tf_op jit(solution)/shard_map/ppermute | solution.py:624
  1031.9 71.9 %collective-permute-start.70 = (bf16[4,512,512]{2,1,0:T(8,128)(2,1)}, bf16[4,512,512]{2,1,0:T(8,128)(2,1)S(1)}, u32[]{:S(2)}, u32[]{:S(2)}) collective-permute-start(bf16[4,512,512]{2,1,0:T(8,128)(2,1)} %cat.31.refs_2_), channel_id=1, source_target_pairs={{0,4},{1,5},{2,6},{3,7},{4,0},{5,1},{6,2},{7,3},{8,12},{9,13},{10,... | collective-permute-start | bytes 6291464 | tf_op jit(solution)/shard_map/ppermute | solution.py:624
  (107 other events, 2385.0 us)
Sparse Core Ops, SparseCore 0:
  336.6 77.5 all-reduce.1
  678.8 72.5 all-gather.10
  832.4 74.2 all-gather.8
  997.4 65.9 all-gather.12
  1065.4 60.5 all-gather.14

commit v4 on v3

--- a/solution.py
+++ b/solution.py
@@ -14,18 +14,17 @@
 HB = 512
 NS = 4
 LINKS = (1, 2, 4)
-ADMIT = ((5, 1), (5, 0), (4, 1), (3, 1), (4, 0), (1, 0), (2, 0), (1, 1), (0, 0), (0, 1), (2, 1), (3, 0),)
-GATHER_SC = ((0, 0), (0, 1), (2, 1), (3, 0),)
+ADMIT = ((5, 0), (5, 1), (4, 1), (3, 1), (3, 0), (4, 0), (1, 0), (1, 1), (0, 0), (2, 0), (2, 1), (0, 1),)
+GATHER_SC = ((0, 0), (0, 1), (3, 1), (4, 0), (5, 1),)
 ORDER = tuple((t[0], int(t[1]), int(t[2])) for t in (
-    'B50', 'a51', 'a50', 'B40', 'a41', 'B30', 'a31', 'a40', 'b50', 'b51', 'B20', 'b41',
-    'c50', 'b31', 'b40', 'B10', 'c51', 'd50', 'a10', 'c41', 'c31', 'c40', 'd51', 'a20',
-    'e50', 'd41', 'a11', 'B00', 'd40', 'a00', 'e41', 'b10', 'H00', 'b20', 'd31', 'a01',
-    'e51', 'e40', 'b11', 'f50', 'f41', 'c20', 'c10', 'f51', 'b00', 'e31', 'b01', 'h50',
-    'f40', 'd10', 'a21', 'U50', 'c11', 'h51', 'f31', 'U51', 'c01', 'd11', 'a30', 'd20',
-    'c00', 'h41', 'd01', 'h40', 'U41', 'h31', 'e10', 'U40', 'b30', 'e20', 'b21', 'e11',
-    'd00', 'U31', 'f10', 'c30', 'c21', 'U01', 'f20', 'f11', 'd21', 'K00', 'd30', 'F01',
-    'h20', 'h10', 'h11', 'K10', 'K11', 'K20', 'K21', 'K30', 'F31', 'F40', 'F41', 'F50',
-    'F51',
+    'B50', 'a50', 'a51', 'B40', 'a41', 'B30', 'a31', 'a30', 'a40', 'b50', 'b51', 'B20',
+    'b41', 'b31', 'b30', 'b40', 'B10', 'a10', 'c50', 'c31', 'c41', 'c30', 'c51', 'd50',
+    'a11', 'c40', 'd41', 'd31', 'B00', 'a00', 'a20', 'b10', 'e50', 'd30', 'a21', 'd51',
+    'a01', 'b11', 'H00', 'd40', 'e41', 'U31', 'b00', 'c10', 'b20', 'e30', 'f50', 'U51',
+    'c11', 'b21', 'b01', 'f41', 'd10', 'c00', 'U40', 'f30', 'c20', 'c21', 'd00', 'h50',
+    'U50', 'h41', 'd11', 'c01', 'h30', 'd21', 'e10', 'U30', 'd20', 'e11', 'd01', 'K00',
+    'f10', 'e20', 'e21', 'f11', 'U41', 'f20', 'K01', 'h10', 'f21', 'h11', 'K10', 'h20',
+    'K11', 'h21', 'K20', 'K21', 'F30', 'F31', 'F40', 'F41', 'F50', 'F51',
 ))
 
 

time: 1300 us -> 1320 us (1.015)
  waiting for transfers between devices: 365 us -> 396 us
    ppermute x76 -> x71, waiting for transfers between devices: 347 us -> 395 us  [cp(): return lax.ppermute(x, BATCH_AXES, pairs[link])]
    psum x1, waiting for transfers between devices: 17.7 us -> 0.02 us  [local_step(): red_head = lax.psum(grad_head.astype(BF16), BATCH_AXES)]
    ppermute x76 -> x71, starting transfers between devices: 70.9 us -> 58 us  [cp(): return lax.ppermute(x, BATCH_AXES, pairs[link])]
    pallas_call x16 -> x14, Pallas kernels: 36.3 us -> 31.7 us  [cat_halves(): pl.pallas_call(cat_body, out_shape=jax.ShapeDtypeStruct((n, HB, HB), BF16...]
  transfers between devices with their start and end apart: 81 -> 77, of which waited for: 19 -> 19; matrix products, arithmetic and copies ran while one was open for 2% -> 1% of each run, Pallas kernels for 47% -> 46%
where the time goes in v4:
time: 1320 us; the launch traced here: 1310 us
  Pallas kernels  760 us (58%)
  waiting for transfers between devices  396 us (30%)
  starting transfers between devices  58.6 us (4%)
  matrix products  48 us (4%)
  local copies, waits for them, and re-layouts  17.2 us (1%)
  between operations  17.1 us (1%)
    ppermute x71, waiting for transfers between devices, cp(): return lax.ppermute(x, BATCH_AXES, pairs[link])  395 us
    pallas_call x12, Pallas kernels, update(): pl.pallas_call(functools.partial(update_body, l, k, kind, order_of(m), sc...  340 us
    pallas_call x6, Pallas kernels, back(): pl.pallas_call(functools.partial(back_body, l, last, order_of((l, 0)), or...  200 us
    pallas_call x36, Pallas kernels, add_halves(): pl.pallas_call(functools.partial(add_body, n), out_shape=[out] * count, i...  95.3 us
    pallas_call x1, Pallas kernels, forward(): pl.pallas_call(functools.partial(fwd_body, layers), out_shape=[jax.ShapeD...  92.8 us
    ppermute x71, starting transfers between devices, cp(): return lax.ppermute(x, BATCH_AXES, pairs[link])  58 us
    pallas_call x14, Pallas kernels, cat_halves(): pl.pallas_call(cat_body, out_shape=jax.ShapeDtypeStruct((n, HB, HB), BF16...  31.7 us
  transfers between devices with their start and end apart: 77, of which 19 were waited for; matrix products, arithmetic and copies ran while one was open for 1% of the time, Pallas kernels for 46%

profile of v4, /device:TPU:0, one launch (start us, length us, event | category | flops | bytes accessed | tf_op | source)
XLA Modules:
  0.0 1309.8 jit_solution(17844426969278014033)
XLA Ops:
  8.4 92.8 %forward.1 = (f32[7,512,1024]{2,1,0:T(8,128)}, bf16[6,512,4096]{2,1,0:T(8,128)(2,1)}, f32[6,512,4096]{2,1,0:T(8,128)}) custom-call(bf16[512,1024]{1,0:T(8,128)(2,1)S(1)} %bitcast.22, f32[6,1024,4096]{2,1,0:T(8,128)} %refs_5_.9, f32[6,4096,1024]{2,1,0:T(8,128)} %refs_6_.7), custom_call_target="tpu_custom_call" | custom-call | flops 51539607552 | bytes 293601280 | tf_op jit(solution)/shard_map/forward/pallas_call | solution.py:419
  109.7 34.4 %back.6 = (bf16[4,512,512]{2,1,0:T(8,128)(2,1)}, bf16[4,512,512]{2,1,0:T(8,128)(2,1)}, bf16[4,512,512]{2,1,0:T(8,128)(2,1)}, bf16[4,512,512]{2,1,0:T(8,128)(2,1)...) custom-call(bf16[512,1024]{1,0:T(8,128)(2,1)} %bitcast_convert_fusion.v_hbm, f32[512,1024]{1,0:T(8,128)} %bitcast.23, ...), custom_call_target="tpu_custom_call" | custom-call | flops 17179869184 | bytes 62914560 | tf_op jit(solution)/shard_map/back/pallas_call | solution.py:247
  148.9 34.7 %back.7 = (bf16[4,512,512]{2,1,0:T(8,128)(2,1)}, bf16[4,512,512]{2,1,0:T(8,128)(2,1)}, bf16[4,512,512]{2,1,0:T(8,128)(2,1)}, bf16[4,512,512]{2,1,0:T(8,128)(2,1)...) custom-call(bf16[512,1024]{1,0:T(8,128)(2,1)} %get-tuple-element.323.v_hbm, f32[512,1024]{1,0:T(8,128)} %get-tuple-element.324.d_hbm, ...), custom_call_target="tpu_custom_call" | custom-call | flops 17179869184 | bytes 62914560 | tf_op jit(solution)/shard_map/back/pallas_call | solution.py:247
  185.4 34.4 %back.8 = (bf16[4,512,512]{2,1,0:T(8,128)(2,1)}, bf16[4,512,512]{2,1,0:T(8,128)(2,1)}, bf16[4,512,512]{2,1,0:T(8,128)(2,1)}, bf16[4,512,512]{2,1,0:T(8,128)(2,1)...) custom-call(bf16[512,1024]{1,0:T(8,128)(2,1)} %get-tuple-element.328.v_hbm, f32[512,1024]{1,0:T(8,128)} %get-tuple-element.329.d_hbm, ...), custom_call_target="tpu_custom_call" | custom-call | flops 17179869184 | bytes 62914560 | tf_op jit(solution)/shard_map/back/pallas_call | solution.py:247
  231.6 34.6 %back.9 = (bf16[4,512,512]{2,1,0:T(8,128)(2,1)}, bf16[4,512,512]{2,1,0:T(8,128)(2,1)}, bf16[4,512,512]{2,1,0:T(8,128)(2,1)}, bf16[4,512,512]{2,1,0:T(8,128)(2,1)...) custom-call(bf16[512,1024]{1,0:T(8,128)(2,1)} %get-tuple-element.344.v_hbm, f32[512,1024]{1,0:T(8,128)} %get-tuple-element.345.d_hbm, ...), custom_call_target="tpu_custom_call" | custom-call | flops 17179869184 | bytes 62914560 | tf_op jit(solution)/shard_map/back/pallas_call | solution.py:247
  293.3 14.7 %collective-permute-done.7.b_ref = bf16[2,512,512]{2,1,0:T(8,128)(2,1)S(1)} collective-permute-done((bf16[2,512,512]{2,1,0:T(8,128)(2,1)}, bf16[2,512,512]{2,1,0:T(8,128)(2,1)S(1)}, u32[]{:S(2)}, u32[]{:S(2)}) %collective-permute-start.7) | collective-permute-done | bytes 1048608 | tf_op jit(solution)/shard_map/ppermute | solution.py:623
  309.7 34.9 %back.10 = (bf16[4,512,512]{2,1,0:T(8,128)(2,1)}, bf16[4,512,512]{2,1,0:T(8,128)(2,1)}, bf16[4,512,512]{2,1,0:T(8,128)(2,1)}, bf16[4,512,512]{2,1,0:T(8,128)(2,1...) custom-call(bf16[512,1024]{1,0:T(8,128)(2,1)} %get-tuple-element.371.v_hbm, f32[512,1024]{1,0:T(8,128)} %get-tuple-element.372.d_hbm, ...), custom_call_target="tpu_custom_call" | custom-call | flops 17179869184 | bytes 62914560 | tf_op jit(solution)/shard_map/back/pallas_call | solution.py:247
  376.0 27.3 %back.11 = (bf16[4,512,512]{2,1,0:T(8,128)(2,1)}, bf16[4,512,512]{2,1,0:T(8,128)(2,1)}, bf16[4,512,512]{2,1,0:T(8,128)(2,1)}, bf16[4,512,512]{2,1,0:T(8,128)(2,1)}) custom-call(bf16[512,1024]{1,0:T(8,128)(2,1)} %get-tuple-element.409.v_hbm, f32[512,1024]{1,0:T(8,128)} %get-tuple-element.410.d_hbm, f32[7,512,1024]{2,1,0:T(8,128)} %get-tuple-element.317.r_hbm, ...), custom_call_target="tpu_custom_call" | custom-call | flops 17179869184 | bytes 62914560 | tf_op jit(solution)/shard_map/back/pallas_call | solution.py:247
  403.3 44.8 %collective-permute-done.22.b_ref = bf16[4,512,512]{2,1,0:T(8,128)(2,1)} collective-permute-done((bf16[4,512,512]{2,1,0:T(8,128)(2,1)S(1)}, bf16[4,512,512]{2,1,0:T(8,128)(2,1)}, u32[]{:S(2)}, u32[]{:S(2)}) %collective-permute-start.22) | collective-permute-done | bytes 2097184 | tf_op jit(solution)/shard_map/ppermute | solution.py:623
  473.1 71.4 %collective-permute-done.18.b_ref = bf16[4,512,512]{2,1,0:T(8,128)(2,1)} collective-permute-done((bf16[4,512,512]{2,1,0:T(8,128)(2,1)S(1)}, bf16[4,512,512]{2,1,0:T(8,128)(2,1)}, u32[]{:S(2)}, u32[]{:S(2)}) %collective-permute-start.18) | collective-permute-done | bytes 2097184 | tf_op jit(solution)/shard_map/ppermute | solution.py:623
  547.7 9.0 multiply_subtract_fusion
  563.5 50.0 %collective-permute-done.16.b_ref = bf16[1,512,512]{2,1,0:T(8,128)(2,1)} collective-permute-done((bf16[1,512,512]{2,1,0:T(8,128)(2,1)}, bf16[1,512,512]{2,1,0:T(8,128)(2,1)}, u32[]{:S(2)}, u32[]{:S(2)}) %collective-permute-start.16) | collective-permute-done | bytes 524320 | tf_op jit(solution)/shard_map/ppermute | solution.py:623
  617.8 14.0 %collective-permute-done.15.b_ref = bf16[4,512,512]{2,1,0:T(8,128)(2,1)} collective-permute-done((bf16[4,512,512]{2,1,0:T(8,128)(2,1)}, bf16[4,512,512]{2,1,0:T(8,128)(2,1)}, u32[]{:S(2)}, u32[]{:S(2)}) %collective-permute-start.15) | collective-permute-done | bytes 2097184 | tf_op jit(solution)/shard_map/ppermute | solution.py:623
  632.1 29.4 %shard_map.162 = (f32[6,4096,1024]{2,1,0:T(8,128)}, f32[6,4096,1024]{2,1,0:T(8,128)}, bf16[4096,1024]{1,0:T(8,128)(2,1)}) custom-call(f32[2]{0:T(128)S(1)} %pad_maximum_fusion.rates_ref, bf16[16,512,512]{2,1,0:T(8,128)(2,1)} %all-gather.11.cloned.1.call-done.refs_0_, f32[6,4096,1024]{2,1,0:T(8,128)} %refs_6_.7, f32[6,4096,1024]{2,1,0:T(8,128)} %refs_7_.3), custom_call_target="tpu_custom_call" | custom-call | flops 10000000000 | bytes 83886080 | tf_op jit(solution)/shard_map/pallas_call | solution.py:591
  679.0 29.4 %shard_map.163 = (f32[6,4096,1024]{2,1,0:T(8,128)}, f32[6,4096,1024]{2,1,0:T(8,128)}, bf16[4096,1024]{1,0:T(8,128)(2,1)}) custom-call(f32[2]{0:T(128)S(1)} %pad_maximum_fusion.rates_ref, bf16[16,512,512]{2,1,0:T(8,128)(2,1)} %all-gather.13.cloned.1.call-done.refs_0_, f32[6,4096,1024]{2,1,0:T(8,128)} %refs_6_.7, ...), custom_call_target="tpu_custom_call", output_to_operand_aliasing={{0}: (4, {}), {1}: (5, {})} | custom-call | flops 10000000000 | bytes 83886080 | tf_op jit(solution)/shard_map/pallas_call | solution.py:591
  721.9 17.0 %collective-permute-done.25.b_ref = bf16[1,512,512]{2,1,0:T(8,128)(2,1)} collective-permute-done((bf16[1,512,512]{2,1,0:T(8,128)(2,1)}, bf16[1,512,512]{2,1,0:T(8,128)(2,1)}, u32[]{:S(2)}, u32[]{:S(2)}) %collective-permute-start.25) | collective-permute-done | bytes 524320 | tf_op jit(solution)/shard_map/ppermute | solution.py:623
  744.3 29.5 %shard_map.164 = (f32[6,1024,4096]{2,1,0:T(8,128)}, f32[6,1024,4096]{2,1,0:T(8,128)}, bf16[1024,4096]{1,0:T(8,128)(2,1)}) custom-call(f32[2]{0:T(128)S(1)} %pad_maximum_fusion.rates_ref, bf16[16,512,512]{2,1,0:T(8,128)(2,1)} %all-gather.15.cloned.1.call-done.refs_0_, f32[6,1024,4096]{2,1,0:T(8,128)} %refs_5_.9, f32[6,1024,4096]{2,1,0:T(8,128)} %refs_6_.6), custom_call_target="tpu_custom_call" | custom-call | flops 10000000000 | bytes 83886080 | tf_op jit(solution)/shard_map/pallas_call | solution.py:591
  783.9 37.1 %collective-permute-done.39.refs_1_ = bf16[4,512,512]{2,1,0:T(8,128)(2,1)S(1)} collective-permute-done((bf16[4,512,512]{2,1,0:T(8,128)(2,1)S(1)}, bf16[4,512,512]{2,1,0:T(8,128)(2,1)S(1)}, u32[]{:S(2)}, u32[]{:S(2)}) %collective-permute-start.39) | collective-permute-done | bytes 2097184 | tf_op jit(solution)/shard_map/ppermute | solution.py:623
  827.4 28.5 %shard_map.165 = (f32[6,1024,4096]{2,1,0:T(8,128)}, f32[6,1024,4096]{2,1,0:T(8,128)}, bf16[1024,4096]{1,0:T(8,128)(2,1)}) custom-call(f32[2]{0:T(128)S(1)} %pad_maximum_fusion.rates_ref, bf16[4,512,512]{2,1,0:T(8,128)(2,1)S(1)} %copy-done.2, bf16[4,512,512]{2,1,0:T(8,128)(2,1)S(1)} %collective-permute-done.39.refs_1_, ...), custom_call_target="tpu_custom_call", output_to_operand_aliasing={{0}: (7, {}), {1}: (8, {})} | custom-call | flops 10000000000 | bytes 83886080 | tf_op jit(solution)/shard_map/pallas_call | solution.py:591
  855.9 14.8 %collective-permute-done.38.b_ref = bf16[1,512,512]{2,1,0:T(8,128)(2,1)} collective-permute-done((bf16[1,512,512]{2,1,0:T(8,128)(2,1)}, bf16[1,512,512]{2,1,0:T(8,128)(2,1)}, u32[]{:S(2)}, u32[]{:S(2)}) %collective-permute-start.38) | collective-permute-done | bytes 524320 | tf_op jit(solution)/shard_map/ppermute | solution.py:623
  885.4 10.8 collective-permute-done.49.b_ref
  902.5 29.0 %shard_map.166 = (f32[6,1024,4096]{2,1,0:T(8,128)}, f32[6,1024,4096]{2,1,0:T(8,128)}, bf16[1024,4096]{1,0:T(8,128)(2,1)}) custom-call(f32[2]{0:T(128)S(1)} %pad_maximum_fusion.rates_ref, bf16[4,512,512]{2,1,0:T(8,128)(2,1)S(1)} %copy-done.3, bf16[4,512,512]{2,1,0:T(8,128)(2,1)} %collective-permute-done.45.refs_1_, ...), custom_call_target="tpu_custom_call", output_to_operand_aliasing={{0}: (7, {}), {1}: (8, {})} | custom-call | flops 10000000000 | bytes 83886080 | tf_op jit(solution)/shard_map/pallas_call | solution.py:591
  942.7 70.5 %collective-permute-done.53.refs_1_ = bf16[4,512,512]{2,1,0:T(8,128)(2,1)} collective-permute-done((bf16[4,512,512]{2,1,0:T(8,128)(2,1)}, bf16[4,512,512]{2,1,0:T(8,128)(2,1)}, u32[]{:S(2)}, u32[]{:S(2)}) %collective-permute-start.53) | collective-permute-done | bytes 2097184 | tf_op jit(solution)/shard_map/ppermute | solution.py:623
  1016.7 28.0 %shard_map.167 = (f32[6,1024,4096]{2,1,0:T(8,128)}, f32[6,1024,4096]{2,1,0:T(8,128)}, bf16[512,4096]{1,0:T(8,128)(2,1)}) custom-call(f32[2]{0:T(128)S(1)} %pad_maximum_fusion.rates_ref, f32[512,1024]{1,0:T(8,128)S(1)} %bitcast_convert_fusion.1.refs_0_, ...), custom_call_target="tpu_custom_call", output_to_operand_aliasing={{0}: (5, {}), {1}: (6, {})} | custom-call | flops 10000000000 | bytes 83886080 | tf_op jit(solution)/shard_map/pallas_call | solution.py:591
  1058.4 29.3 %shard_map.168 = (f32[6,4096,1024]{2,1,0:T(8,128)}, f32[6,4096,1024]{2,1,0:T(8,128)}, bf16[4096,1024]{1,0:T(8,128)(2,1)}) custom-call(f32[2]{0:T(128)S(1)} %pad_maximum_fusion.rates_ref, bf16[4,512,512]{2,1,0:T(8,128)(2,1)} %cat.18.refs_0_, bf16[4,512,512]{2,1,0:T(8,128)(2,1)} %collective-permute-done.53.refs_1_, ...), custom_call_target="tpu_custom_call", output_to_operand_aliasing={{0}: (7, {}), {1}: (8, {})} | custom-call | flops 10000000000 | bytes 83886080 | tf_op jit(solution)/shard_map/pallas_call | solution.py:591
  1091.3 27.2 %shard_map.169 = (f32[6,4096,1024]{2,1,0:T(8,128)}, f32[6,4096,1024]{2,1,0:T(8,128)}, f32[512,1024]{1,0:T(8,128)S(1)}) custom-call(f32[2]{0:T(128)S(1)} %pad_maximum_fusion.rates_ref, f32[512,1024]{1,0:T(8,128)S(1)} %bitcast_convert_fusion.1.refs_0_, bf16[512,4096]{1,0:T(8,128)(2,1)} %get-tuple-element.562.refs_1_, ...), custom_call_target="tpu_custom_call", output_to_operand_aliasing={{0}: (6, {}), {1}: (7, {})} | custom-call | flops 10000000000 | bytes 83886080 | tf_op jit(solution)/shard_map/pallas_call | solution.py:591
  1127.1 27.3 %shard_map.170 = (f32[6,1024,4096]{2,1,0:T(8,128)}, f32[6,1024,4096]{2,1,0:T(8,128)}, bf16[512,4096]{1,0:T(8,128)(2,1)}) custom-call(f32[2]{0:T(128)S(1)} %pad_maximum_fusion.rates_ref, f32[512,1024]{1,0:T(8,128)S(1)} %copy-done.1, bf16[4,512,512]{2,1,0:T(8,128)(2,1)S(1)} %copy-done.4, ...), custom_call_target="tpu_custom_call", output_to_operand_aliasing={{0}: (8, {}), {1}: (9, {})} | custom-call | flops 10000000000 | bytes 83886080 | tf_op jit(solution)/shard_map/pallas_call | solution.py:591
  1154.5 16.7 %collective-permute-done.65.refs_2_ = bf16[4,512,512]{2,1,0:T(8,128)(2,1)S(1)} collective-permute-done((bf16[4,512,512]{2,1,0:T(8,128)(2,1)}, bf16[4,512,512]{2,1,0:T(8,128)(2,1)S(1)}, u32[]{:S(2)}, u32[]{:S(2)}) %collective-permute-start.65) | collective-permute-done | bytes 2097184 | tf_op jit(solution)/shard_map/ppermute | solution.py:623
  1171.3 28.7 %shard_map.171 = (f32[6,4096,1024]{2,1,0:T(8,128)}, f32[6,4096,1024]{2,1,0:T(8,128)}, f32[512,1024]{1,0:T(8,128)S(1)}) custom-call(f32[2]{0:T(128)S(1)} %pad_maximum_fusion.rates_ref, f32[512,1024]{1,0:T(8,128)S(1)} %copy-done.1, bf16[512,4096]{1,0:T(8,128)(2,1)} %get-tuple-element.580.refs_1_, ...), custom_call_target="tpu_custom_call", output_to_operand_aliasing={{0}: (9, {}), {1}: (10, {})} | custom-call | flops 10000000000 | bytes 83886080 | tf_op jit(solution)/shard_map/pallas_call | solution.py:591
  1201.4 26.7 %shard_map.172 = (f32[6,1024,4096]{2,1,0:T(8,128)}, f32[6,1024,4096]{2,1,0:T(8,128)}, bf16[512,4096]{1,0:T(8,128)(2,1)}) custom-call(f32[2]{0:T(128)S(1)} %pad_maximum_fusion.rates_ref, f32[512,1024]{1,0:T(8,128)S(1)} %get-tuple-element.598.refs_0_, bf16[4,512,512]{2,1,0:T(8,128)(2,1)S(1)} %copy-done.5, ...), custom_call_target="tpu_custom_call", output_to_operand_aliasing={{0}: (8, {}), {1}: (9, {})} | custom-call | flops 10000000000 | bytes 83886080 | tf_op jit(solution)/shard_map/pallas_call | solution.py:591
  1229.4 27.3 %shard_map.173 = (f32[6,4096,1024]{2,1,0:T(8,128)}, f32[6,4096,1024]{2,1,0:T(8,128)}, f32[512,1024]{1,0:T(8,128)S(1)}) custom-call(f32[2]{0:T(128)S(1)} %pad_maximum_fusion.rates_ref, f32[512,1024]{1,0:T(8,128)S(1)} %get-tuple-element.598.refs_0_, bf16[512,4096]{1,0:T(8,128)(2,1)} %get-tuple-element.599.refs_1_, ...), custom_call_target="tpu_custom_call", output_to_operand_aliasing={{0}: (9, {}), {1}: (10, {})} | custom-call | flops 10000000000 | bytes 83886080 | tf_op jit(solution)/shard_map/pallas_call | solution.py:591
  1257.2 7.8 multiply_convert_fusion.2
  (336 shorter events, 280.6 us)
Async XLA Ops:
  7.2 540.5 %all-reduce.2.cloned.1.call-start = ((), (), s32[]{:S(2)}) async-start(), calls=%async_computation | async-start | bytes 4096000 | tf_op jit(solution)/shard_map/psum | solution.py:633
  144.1 79.0 %collective-permute-start.1 = (bf16[4,512,512]{2,1,0:T(8,128)(2,1)}, bf16[4,512,512]{2,1,0:T(8,128)(2,1)}, u32[]{:S(2)}, u32[]{:S(2)}) collective-permute-start(bf16[4,512,512]{2,1,0:T(8,128)(2,1)} %get-tuple-element.336), channel_id=1, source_target_pairs={{0,2},{1,3},{2,0},{3,1},{4,6},{5,7},{6,4},{7,5},{8,10},{9,11},{10,... | collective-permute-start | bytes 6291464 | tf_op jit(solution)/shard_map/ppermute | solution.py:623
  147.4 79.0 %collective-permute-start = (bf16[4,512,512]{2,1,0:T(8,128)(2,1)}, bf16[4,512,512]{2,1,0:T(8,128)(2,1)}, u32[]{:S(2)}, u32[]{:S(2)}) collective-permute-start(bf16[4,512,512]{2,1,0:T(8,128)(2,1)} %get-tuple-element.333), channel_id=1, source_target_pairs={{0,4},{1,5},{2,6},{3,7},{4,0},{5,1},{6,2},{7,3},{8,12},{9,13},{10,... | collective-permute-start | bytes 6291464 | tf_op jit(solution)/shard_map/ppermute | solution.py:623
  183.6 82.7 %collective-permute-start.5 = (bf16[4,512,512]{2,1,0:T(8,128)(2,1)}, bf16[4,512,512]{2,1,0:T(8,128)(2,1)}, u32[]{:S(2)}, u32[]{:S(2)}) collective-permute-start(bf16[4,512,512]{2,1,0:T(8,128)(2,1)} %get-tuple-element.357), channel_id=1, source_target_pairs={{0,8},{1,9},{2,10},{3,11},{4,12},{5,13},{6,14},{7,15},{8,0},{9,1},... | collective-permute-start | bytes 6291464 | tf_op jit(solution)/shard_map/ppermute | solution.py:623
  222.9 393.4 %all-gather.11.cloned.1.call-start = ((), (), s32[]{:S(2)}) async-start(), calls=%async_computation.1 | async-start | bytes 8912896 | tf_op jit(solution)/shard_map/all_gather | solution.py:670
  229.7 78.4 %collective-permute-start.7 = (bf16[2,512,512]{2,1,0:T(8,128)(2,1)}, bf16[2,512,512]{2,1,0:T(8,128)(2,1)S(1)}, u32[]{:S(2)}, u32[]{:S(2)}) collective-permute-start(bf16[2,512,512]{2,1,0:T(8,128)(2,1)} %get-tuple-element.376), channel_id=1, source_target_pairs={{0,4},{1,5},{2,6},{3,7},{4,0},{5,1},{6,2},{7,3},{8,12},{9,13},{10,... | collective-permute-start | bytes 3145736 | tf_op jit(solution)/shard_map/ppermute | solution.py:623
  373.2 305.7 %all-gather.13.cloned.1.call-start = ((), (), s32[]{:S(2)}) async-start(), calls=%async_computation.2 | async-start | bytes 8912896 | tf_op jit(solution)/shard_map/all_gather | solution.py:670
  373.3 74.9 %collective-permute-start.22 = (bf16[4,512,512]{2,1,0:T(8,128)(2,1)S(1)}, bf16[4,512,512]{2,1,0:T(8,128)(2,1)}, u32[]{:S(2)}, u32[]{:S(2)}) collective-permute-start(bf16[4,512,512]{2,1,0:T(8,128)(2,1)S(1)} %copy-done.31), channel_id=1, source_target_pairs={{0,2},{1,3},{2,0},{3,1},{4,6},{5,7},{6,4},{7,5},{8,10},{9,11},{10,... | collective-permute-start | bytes 6291464 | tf_op jit(solution)/shard_map/ppermute | solution.py:623
  373.6 85.7 %collective-permute-start.20 = (bf16[1,512,512]{2,1,0:T(8,128)(2,1)S(1)}, bf16[1,512,512]{2,1,0:T(8,128)(2,1)}, u32[]{:S(2)}, u32[]{:S(2)}) collective-permute-start(bf16[1,512,512]{2,1,0:T(8,128)(2,1)S(1)} %copy-done.44), channel_id=1, source_target_pairs={{0,2},{1,3},{2,0},{3,1},{4,6},{5,7},{6,4},{7,5},{8,10},{9,11},{10,... | collective-permute-start | bytes 1572872 | tf_op jit(solution)/shard_map/ppermute | solution.py:623
  375.3 91.9 %collective-permute-start.19 = (bf16[1,512,512]{2,1,0:T(8,128)(2,1)S(1)}, bf16[1,512,512]{2,1,0:T(8,128)(2,1)}, u32[]{:S(2)}, u32[]{:S(2)}) collective-permute-start(bf16[1,512,512]{2,1,0:T(8,128)(2,1)S(1)} %copy-done.45), channel_id=1, source_target_pairs={{0,2},{1,3},{2,0},{3,1},{4,6},{5,7},{6,4},{7,5},{8,10},{9,11},{10,... | collective-permute-start | bytes 1572872 | tf_op jit(solution)/shard_map/ppermute | solution.py:623
  375.6 75.7 %collective-permute-start.21 = (bf16[1,512,512]{2,1,0:T(8,128)(2,1)}, bf16[1,512,512]{2,1,0:T(8,128)(2,1)}, u32[]{:S(2)}, u32[]{:S(2)}) collective-permute-start(bf16[1,512,512]{2,1,0:T(8,128)(2,1)} %add.118.a_ref), channel_id=1, source_target_pairs={{0,8},{1,9},{2,10},{3,11},{4,12},{5,13},{6,14},{7,15},{8,0},{9,1},... | collective-permute-start | bytes 1572872 | tf_op jit(solution)/shard_map/ppermute | solution.py:623
  469.4 274.8 %all-gather.15.cloned.1.call-start = ((), (), s32[]{:S(2)}) async-start(), calls=%async_computation.3 | async-start | bytes 8912896 | tf_op jit(solution)/shard_map/all_gather | solution.py:670
  469.7 74.8 %collective-permute-start.18 = (bf16[4,512,512]{2,1,0:T(8,128)(2,1)S(1)}, bf16[4,512,512]{2,1,0:T(8,128)(2,1)}, u32[]{:S(2)}, u32[]{:S(2)}) collective-permute-start(bf16[4,512,512]{2,1,0:T(8,128)(2,1)S(1)} %copy-done.30), channel_id=1, source_target_pairs={{0,4},{1,5},{2,6},{3,7},{4,0},{5,1},{6,2},{7,3},{8,12},{9,13},{10,... | collective-permute-start | bytes 6291464 | tf_op jit(solution)/shard_map/ppermute | solution.py:623
  471.4 85.3 %collective-permute-start.17 = (bf16[1,512,512]{2,1,0:T(8,128)(2,1)}, bf16[1,512,512]{2,1,0:T(8,128)(2,1)}, u32[]{:S(2)}, u32[]{:S(2)}) collective-permute-start(bf16[1,512,512]{2,1,0:T(8,128)(2,1)} %get-tuple-element.415), channel_id=1, source_target_pairs={{0,4},{1,5},{2,6},{3,7},{4,0},{5,1},{6,2},{7,3},{8,12},{9,13},{10,... | collective-permute-start | bytes 1572872 | tf_op jit(solution)/shard_map/ppermute | solution.py:623
  559.0 457.1 %all-gather.17.cloned.1.call-start = ((), (), s32[]{:S(2)}) async-start(), calls=%async_computation.4 | async-start | bytes 8912896 | tf_op jit(solution)/shard_map/all_gather | solution.py:670
  559.0 72.7 %collective-permute-start.15 = (bf16[4,512,512]{2,1,0:T(8,128)(2,1)}, bf16[4,512,512]{2,1,0:T(8,128)(2,1)}, u32[]{:S(2)}, u32[]{:S(2)}) collective-permute-start(bf16[4,512,512]{2,1,0:T(8,128)(2,1)} %get-tuple-element.414), channel_id=1, source_target_pairs={{0,8},{1,9},{2,10},{3,11},{4,12},{5,13},{6,14},{7,15},{8,0},{9,1},... | collective-permute-start | bytes 6291464 | tf_op jit(solution)/shard_map/ppermute | solution.py:623
  559.7 107.4 %collective-permute-start.32 = (bf16[4,512,512]{2,1,0:T(8,128)(2,1)S(1)}, bf16[4,512,512]{2,1,0:T(8,128)(2,1)}, u32[]{:S(2)}, u32[]{:S(2)}) collective-permute-start(bf16[4,512,512]{2,1,0:T(8,128)(2,1)S(1)} %copy-done.29), channel_id=1, source_target_pairs={{0,2},{1,3},{2,0},{3,1},{4,6},{5,7},{6,4},{7,5},{8,10},{9,11},{10,... | collective-permute-start | bytes 6291464 | tf_op jit(solution)/shard_map/ppermute | solution.py:623
  561.9 108.6 %collective-permute-start.31 = (bf16[1,512,512]{2,1,0:T(8,128)(2,1)}, bf16[1,512,512]{2,1,0:T(8,128)(2,1)}, u32[]{:S(2)}, u32[]{:S(2)}) collective-permute-start(bf16[1,512,512]{2,1,0:T(8,128)(2,1)} %add.123.a_ref), channel_id=1, source_target_pairs={{0,2},{1,3},{2,0},{3,1},{4,6},{5,7},{6,4},{7,5},{8,10},{9,11},{10,... | collective-permute-start | bytes 1572872 | tf_op jit(solution)/shard_map/ppermute | solution.py:623
  616.3 94.9 %collective-permute-start.28 = (bf16[4,512,512]{2,1,0:T(8,128)(2,1)}, bf16[4,512,512]{2,1,0:T(8,128)(2,1)}, u32[]{:S(2)}, u32[]{:S(2)}) collective-permute-start(bf16[4,512,512]{2,1,0:T(8,128)(2,1)} %get-tuple-element.455), channel_id=1, source_target_pairs={{0,4},{1,5},{2,6},{3,7},{4,0},{5,1},{6,2},{7,3},{8,12},{9,13},{10,... | collective-permute-start | bytes 6291464 | tf_op jit(solution)/shard_map/ppermute | solution.py:623
  631.8 84.5 %collective-permute-start.27 = (bf16[4,512,512]{2,1,0:T(8,128)(2,1)}, bf16[4,512,512]{2,1,0:T(8,128)(2,1)}, u32[]{:S(2)}, u32[]{:S(2)}) collective-permute-start(bf16[4,512,512]{2,1,0:T(8,128)(2,1)} %get-tuple-element.453), channel_id=1, source_target_pairs={{0,8},{1,9},{2,10},{3,11},{4,12},{5,13},{6,14},{7,15},{8,0},{9,1},... | collective-permute-start | bytes 6291464 | tf_op jit(solution)/shard_map/ppermute | solution.py:623
  674.4 67.0 %collective-permute-start.23 = (bf16[2,512,512]{2,1,0:T(8,128)(2,1)S(1)}, bf16[2,512,512]{2,1,0:T(8,128)(2,1)}, u32[]{:S(2)}, u32[]{:S(2)}) collective-permute-start(bf16[2,512,512]{2,1,0:T(8,128)(2,1)S(1)} %copy-done.38), channel_id=1, source_target_pairs={{0,2},{1,3},{2,0},{3,1},{4,6},{5,7},{6,4},{7,5},{8,10},{9,11},{10,... | collective-permute-start | bytes 3145736 | tf_op jit(solution)/shard_map/ppermute | solution.py:623
  783.7 307.5 %all-gather.19.cloned.1.call-start = ((), (), s32[]{:S(2)}) async-start(), calls=%async_computation.5 | async-start | bytes 8912896 | tf_op jit(solution)/shard_map/all_gather | solution.py:670
  824.9 77.7 %collective-permute-start.46 = (bf16[4,512,512]{2,1,0:T(8,128)(2,1)}, bf16[4,512,512]{2,1,0:T(8,128)(2,1)}, u32[]{:S(2)}, u32[]{:S(2)}) collective-permute-start(bf16[4,512,512]{2,1,0:T(8,128)(2,1)} %cat.19.refs_0_), channel_id=1, source_target_pairs={{0,1},{1,0},{2,3},{3,2},{4,5},{5,4},{6,7},{7,6},{8,9},{9,8},{10,11... | collective-permute-start | bytes 6291464 | tf_op jit(solution)/shard_map/ppermute | solution.py:623
  939.7 73.5 %collective-permute-start.53 = (bf16[4,512,512]{2,1,0:T(8,128)(2,1)}, bf16[4,512,512]{2,1,0:T(8,128)(2,1)}, u32[]{:S(2)}, u32[]{:S(2)}) collective-permute-start(bf16[4,512,512]{2,1,0:T(8,128)(2,1)} %cat.18.refs_0_), channel_id=1, source_target_pairs={{0,8},{1,9},{2,10},{3,11},{4,12},{5,13},{6,14},{7,15},{8,0},{9,1},... | collective-permute-start | bytes 6291464 | tf_op jit(solution)/shard_map/ppermute | solution.py:623
  941.3 74.9 %collective-permute-start.51 = (bf16[2,512,512]{2,1,0:T(8,128)(2,1)}, bf16[2,512,512]{2,1,0:T(8,128)(2,1)}, u32[]{:S(2)}, u32[]{:S(2)}) collective-permute-start(bf16[2,512,512]{2,1,0:T(8,128)(2,1)} %cat.20.a_ref), channel_id=1, source_target_pairs={{0,4},{1,5},{2,6},{3,7},{4,0},{5,1},{6,2},{7,3},{8,12},{9,13},{10,... | collective-permute-start | bytes 3145736 | tf_op jit(solution)/shard_map/ppermute | solution.py:623
  942.7 114.9 %collective-permute-start.54 = (bf16[4,512,512]{2,1,0:T(8,128)(2,1)}, bf16[4,512,512]{2,1,0:T(8,128)(2,1)}, u32[]{:S(2)}, u32[]{:S(2)}) collective-permute-start(bf16[4,512,512]{2,1,0:T(8,128)(2,1)} %cat.18.refs_0_), channel_id=1, source_target_pairs={{0,1},{1,0},{2,3},{3,2},{4,5},{5,4},{6,7},{7,6},{8,9},{9,8},{10,11... | collective-permute-start | bytes 6291464 | tf_op jit(solution)/shard_map/ppermute | solution.py:623
  1047.2 72.7 %collective-permute-start.58 = (bf16[4,512,512]{2,1,0:T(8,128)(2,1)}, bf16[4,512,512]{2,1,0:T(8,128)(2,1)}, u32[]{:S(2)}, u32[]{:S(2)}) collective-permute-start(bf16[4,512,512]{2,1,0:T(8,128)(2,1)} %cat.22.refs_1_), channel_id=1, source_target_pairs={{0,2},{1,3},{2,0},{3,1},{4,6},{5,7},{6,4},{7,5},{8,10},{9,11},{10,... | collective-permute-start | bytes 6291464 | tf_op jit(solution)/shard_map/ppermute | solution.py:623
  1053.7 66.7 %collective-permute-start.61 = (bf16[2,512,512]{2,1,0:T(8,128)(2,1)}, bf16[2,512,512]{2,1,0:T(8,128)(2,1)}, u32[]{:S(2)}, u32[]{:S(2)}) collective-permute-start(bf16[2,512,512]{2,1,0:T(8,128)(2,1)} %cat.24.a_ref), channel_id=1, source_target_pairs={{0,8},{1,9},{2,10},{3,11},{4,12},{5,13},{6,14},{7,15},{8,0},{9,1},... | collective-permute-start | bytes 3145736 | tf_op jit(solution)/shard_map/ppermute | solution.py:623
  1057.6 66.8 %collective-permute-start.59 = (bf16[4,512,512]{2,1,0:T(8,128)(2,1)}, bf16[4,512,512]{2,1,0:T(8,128)(2,1)}, u32[]{:S(2)}, u32[]{:S(2)}) collective-permute-start(bf16[4,512,512]{2,1,0:T(8,128)(2,1)} %cat.22.refs_1_), channel_id=1, source_target_pairs={{0,1},{1,0},{2,3},{3,2},{4,5},{5,4},{6,7},{7,6},{8,9},{9,8},{10,11... | collective-permute-start | bytes 6291464 | tf_op jit(solution)/shard_map/ppermute | solution.py:623
  1124.4 75.6 %collective-permute-start.68 = (bf16[4,512,512]{2,1,0:T(8,128)(2,1)}, bf16[4,512,512]{2,1,0:T(8,128)(2,1)}, u32[]{:S(2)}, u32[]{:S(2)}) collective-permute-start(bf16[4,512,512]{2,1,0:T(8,128)(2,1)} %cat.27.refs_2_), channel_id=1, source_target_pairs={{0,4},{1,5},{2,6},{3,7},{4,0},{5,1},{6,2},{7,3},{8,12},{9,13},{10,... | collective-permute-start | bytes 6291464 | tf_op jit(solution)/shard_map/ppermute | solution.py:623
  1125.5 74.5 %collective-permute-start.66 = (bf16[4,512,512]{2,1,0:T(8,128)(2,1)}, bf16[4,512,512]{2,1,0:T(8,128)(2,1)}, u32[]{:S(2)}, u32[]{:S(2)}) collective-permute-start(bf16[4,512,512]{2,1,0:T(8,128)(2,1)} %cat.26.refs_1_), channel_id=1, source_target_pairs={{0,1},{1,0},{2,3},{3,2},{4,5},{5,4},{6,7},{7,6},{8,9},{9,8},{10,11... | collective-permute-start | bytes 6291464 | tf_op jit(solution)/shard_map/ppermute | solution.py:623
  1154.4 73.6 %collective-permute-start.69 = (bf16[4,512,512]{2,1,0:T(8,128)(2,1)}, bf16[4,512,512]{2,1,0:T(8,128)(2,1)}, u32[]{:S(2)}, u32[]{:S(2)}) collective-permute-start(bf16[4,512,512]{2,1,0:T(8,128)(2,1)} %cat.27.refs_2_), channel_id=1, source_target_pairs={{0,1},{1,0},{2,3},{3,2},{4,5},{5,4},{6,7},{7,6},{8,9},{9,8},{10,11... | collective-permute-start | bytes 6291464 | tf_op jit(solution)/shard_map/ppermute | solution.py:623
  (99 other events, 2519.1 us)
Sparse Core Ops, SparseCore 0:
  223.0 78.5 all-reduce.1
  373.3 72.9 all-gather.10
  469.6 72.8 all-gather.12
  559.1 73.4 all-gather.14
  783.8 66.9 all-gather.16
  939.8 74.8 all-gather.18
